TPU v7x, 32 devices: a whole 2x2x4 slice. The times are simulated.
32 devices in a mesh: mesh: 8 (over z, y), member: 4 (over x, core).
Axes of the slice: x: 2, y: 2, z: 4, core: 2. Of those that a mesh axis runs over, the one named last changes fastest.
Arguments:
- node_states: bfloat16 [8, 4096, 512], P('member', 'mesh'), may hold values from -60 to 60
- projection: bfloat16 [512, 1536], P('member'), may hold values from -12 to 12
- output_weight: bfloat16 [512, 512], P('member'), may hold values from -0.25 to 0.25
- up_weight: bfloat16 [512, 2048], P('member'), may hold values from -0.25 to 0.25
- down_weight: bfloat16 [2048, 512], P('member'), may hold values from -0.125 to 0.125
- attention_gain: float32 [512], replicated, may hold values from 0.5 to 2
- feedforward_gain: float32 [512], replicated, may hold values from 0.5 to 2
- tile_lists: int32 [32, 8], P('mesh'), may hold values from 0 to 31, as said below
- tile_counts: int32 [32], P('mesh'), may hold values from 4 to 8, as said below
Outputs:
- updated_states: bfloat16 [8, 4096, 512], P('member', 'mesh')
Inputs may be any that keep to these rules, and one draw needn't show every extreme that they name: `tile_lists`: entry 0 of tile t's list is t. Every entry names a tile of the device that holds t, or one of the last 4 tiles of the device before it, or one of the first 4 tiles of the device after it along mesh (the first and last devices are neighbours). The first tile_counts[t] entries are distinct; later entries are ignored. `tile_counts`: every device holds a tile whose count is 8.
All inputs are finite; a program needn't handle non-finite values.
Results may differ from a plain program's by a relative error of at most 0.0056.
Values may be sent and summed in bfloat16 or wider, within the bound.
No kernel may reach another device: no remote copies, remote signals or barrier semaphores. Data moves between devices by JAX's collectives and lax.ppermute only.
A program may use at most 128 MiB of HBM per device.

v0:
```python
import functools
import math

import jax
import jax.numpy as jnp
from jax import lax
from jax.experimental import pallas as pl
from jax.experimental.pallas import tpu as pltpu
from jax.sharding import PartitionSpec as P

HEADS = 4
RIM_T = 4
SURE = 4
BF16 = jnp.bfloat16
F32 = jnp.float32
VMEM = pltpu.VMEM
SMEM = pltpu.SMEM
ANY = pl.ANY


def norm_rows(rows, gain):
    values = rows.astype(F32)
    center = values - jnp.mean(values, axis=-1, keepdims=True)
    spread = jnp.mean(center * center, axis=-1, keepdims=True)
    return (center * lax.rsqrt(spread + 1e-05) * gain).astype(BF16)


def dot(a, b):
    return lax.dot_general(a, b, (((1,), (0,)), ((), ())), preferred_element_type=F32)


def dot_t(a, b):
    return lax.dot_general(a, b, (((1,), (1,)), ((), ())), preferred_element_type=F32)


def gelu(x):
    return jax.nn.gelu(x, approximate=True)


def piece_copies(me, pieces, whole, sems, first, cols=None):
    rows = pieces[0].shape[0]
    return [
        pltpu.make_async_copy(
            piece if cols is None else piece.at[:, cols],
            whole.at[pl.ds(pl.multiple_of((me ^ k) * rows, rows), rows)],
            sems.at[first + k],
        )
        for k, piece in enumerate(pieces)
    ]


def start_all(copies):
    for copy in copies:
        copy.start()


def wait_all(copies):
    for copy in copies:
        copy.wait()


def project_pairs(normed, weight, key_cols, value_cols, keys, values, row, tile_rows):
    count = normed.shape[0]
    keys[pl.ds(row, count), :] = dot(normed, weight[:, key_cols]).astype(BF16)
    block = dot(normed, weight[:, value_cols]).astype(BF16)
    for t in range(count // tile_rows):
        values[row // tile_rows + t] = block[t * tile_rows : (t + 1) * tile_rows].T


def attend_tiles(lists, counts, slot, q_ref, k_ref, v_ref, out_ref, scores, tops, tile_rows):
    tiles, entries = lists.shape
    width = q_ref.shape[1]
    head = width // HEADS
    scale = math.log2(math.e) / math.sqrt(head)
    zero = jnp.zeros((tile_rows, head), BF16)

    def stage(t, p, at):
        row = pl.multiple_of(t * tile_rows, tile_rows)
        first = q_ref[pl.ds(row, tile_rows), 2 * p * head : (2 * p + 1) * head]
        second = q_ref[pl.ds(row, tile_rows), (2 * p + 1) * head : (2 * p + 2) * head]
        both = jnp.concatenate(
            [jnp.concatenate([first, zero], 1), jnp.concatenate([zero, second], 1)], 0
        )
        cols = slice(2 * p * head, (2 * p + 2) * head)
        keys = jnp.concatenate(
            [
                k_ref[pl.ds(pl.multiple_of(slot[t * entries + j] * tile_rows, tile_rows), tile_rows), cols]
                for j in range(entries)
            ],
            0,
        )
        product = dot_t(keys, both)
        scores[at] = product
        top = None
        for j in range(entries):
            part = product[j * tile_rows : (j + 1) * tile_rows]
            part = jnp.max(part.reshape(tile_rows // 8, 8, 2 * tile_rows), axis=0)
            if j >= SURE:
                part = jnp.where(j < counts[t], part, -jnp.inf)
            top = part if top is None else jnp.maximum(top, part)
        top = jnp.max(top, axis=0, keepdims=True) * scale
        tops[at] = jnp.broadcast_to(top, tops.shape[1:])

    def blend(t, p, at):
        row = pl.multiple_of(t * tile_rows, tile_rows)
        top = tops[at, 0:1]
        total, outs = None, [None, None]
        for pair in range(0, entries, 2):
            weights = []
            for j in (pair, pair + 1):
                highest = jnp.where(j < counts[t], top, jnp.inf) if j >= SURE else top
                weight = jnp.exp2(scores[at, j * tile_rows : (j + 1) * tile_rows] * scale - highest)
                part = jnp.sum(weight.reshape(tile_rows // 8, 8, 2 * tile_rows), axis=0)
                total = part if total is None else total + part
                weights.append(weight.astype(BF16))
            weights = jnp.concatenate(weights, 0)
            for a in range(2):
                h = 2 * p + a
                values = jnp.concatenate(
                    [
                        v_ref[slot[t * entries + j], h * head : (h + 1) * head, :]
                        for j in (pair, pair + 1)
                    ],
                    1,
                )
                out = dot(values, weights[:, a * tile_rows : (a + 1) * tile_rows])
                outs[a] = out if outs[a] is None else outs[a] + out
        total = jnp.sum(total, axis=0, keepdims=True)
        for a in range(2):
            h = 2 * p + a
            out = outs[a] / total[:, a * tile_rows : (a + 1) * tile_rows]
            out_ref[pl.ds(row, tile_rows), h * head : (h + 1) * head] = out.T.astype(BF16)

    pairs = HEADS // 2
    stage(0, 0, 0)

    def one_tile(t, carry):
        for p in range(pairs):
            last = p == pairs - 1
            following = jnp.minimum(t + 1, tiles - 1) if last else t
            stage(following, 0 if last else p + 1, (p + 1) % 2)
            blend(t, p, p % 2)
        return carry

    lax.fori_loop(0, tiles, one_tile, 0)


def fill_slots(info, lists, slot):
    tiles, entries = lists.shape
    place, other = info[1], info[2]
    for t in range(tiles):
        for j in range(entries):
            tile = lists[t, j]
            owner = lax.div(tile, jnp.int32(tiles))
            block = jnp.where(owner == place, 0, jnp.where(owner == other, 1, 2))
            slot[t * entries + j] = block * tiles + lax.rem(tile, jnp.int32(tiles))


def near_body(info, keep, got, gain, *rest, n_pieces, tile_rows):
    pieces, (q_keep, q_got, k_out, v_out, weight, normed, queries, keys, values, sems) = (
        rest[:n_pieces],
        rest[n_pieces:],
    )
    rows, width = keep.shape
    me = info[0]
    loads = piece_copies(me, pieces, weight, sems, 0)
    start_all(loads)
    block = 256
    for at, source in enumerate((keep, got)):
        for b in range(rows // block):
            normed[at * rows + b * block : at * rows + (b + 1) * block] = norm_rows(
                source[b * block : (b + 1) * block, :], gain[...]
            )
    wait_all(loads)
    writes = []
    tiles = rows // tile_rows
    for at in range(2):
        span = pl.ds(at * rows, rows)
        part = normed[span]
        queries[span] = dot(part, weight[:, :width]).astype(BF16)
        project_pairs(
            part, weight, slice(width, 2 * width), slice(2 * width, 3 * width),
            keys, values, at * rows, tile_rows,
        )
        slots = pl.ds(at * tiles, tiles)
        for i, (source, target, where) in enumerate(
            ((queries, None, span), (keys, k_out, span), (values, v_out, slots))
        ):
            place = (q_keep, q_got)[at] if target is None else target.at[where]
            copy = pltpu.make_async_copy(
                source.at[where], place, sems.at[n_pieces + 3 * at + i]
            )
            copy.start()
            writes.append(copy)
    wait_all(writes)


def third_block(info, far, gain, pieces, k_near, v_near, weight, keys, values, sems, tile_rows):
    rows, width = far.shape
    n = len(pieces)
    tiles = rows // tile_rows
    loads = piece_copies(info[0], pieces, weight, sems, 0, pl.ds(width, 2 * width))
    near = [
        pltpu.make_async_copy(k_near, keys.at[pl.ds(0, 2 * rows)], sems.at[n]),
        pltpu.make_async_copy(v_near, values.at[pl.ds(0, 2 * tiles)], sems.at[n + 1]),
    ]
    start_all(loads)
    start_all(near)
    normed = norm_rows(far[...], gain[...])
    wait_all(loads)
    project_pairs(
        normed, weight, slice(0, width), slice(width, 2 * width), keys, values, 2 * rows, tile_rows
    )
    wait_all(near)


def got_body(info, lists, counts, far, queries, k_near, v_near, gain, *rest, n_pieces, tile_rows):
    pieces, (attended, weight, keys, values, scores, tops, slot, sems) = (
        rest[:n_pieces],
        rest[n_pieces:],
    )
    fill_slots(info, lists, slot)
    third_block(
        info, far, gain, pieces, k_near, v_near, weight, keys, values, sems, tile_rows
    )
    attend_tiles(
        lists, counts, slot, queries, keys, values, attended, scores, tops, tile_rows
    )


def keep_body(
    info, lists, counts, states, far, queries, k_near, v_near, gain, second_gain, *rest,
    n_pieces, tile_rows,
):
    proj, outs, ups = (rest[i * n_pieces : (i + 1) * n_pieces] for i in range(3))
    (
        middle, hidden, weight, out_weight, up_weight, keys, values, attended, scores, tops,
        slot, sems,
    ) = rest[3 * n_pieces :]
    me = info[0]
    first = n_pieces + 2
    late = piece_copies(me, outs, out_weight, sems, first) + piece_copies(
        me, ups, up_weight, sems, first + n_pieces
    )
    fill_slots(info, lists, slot)
    third_block(info, far, gain, proj, k_near, v_near, weight, keys, values, sems, tile_rows)
    start_all(late)
    attend_tiles(
        lists, counts, slot, queries, keys, values, attended, scores, tops, tile_rows
    )
    wait_all(late)
    widen_rows(states, attended, out_weight, up_weight, second_gain, middle, hidden, ())


def widen_rows(states, attended, out_weight, up_weight, gain, middle, hidden, before_up):
    block = 256
    rows = attended.shape[0]
    for b in range(rows // block):
        at = slice(b * block, (b + 1) * block)
        mid = (states[at, :].astype(F32) + dot(attended[at, :], out_weight[...])).astype(BF16)
        middle[at, :] = mid
        normed = norm_rows(mid, gain[...])
        if b == 0:
            wait_all(before_up)
        hidden[at, :] = gelu(dot(normed, up_weight[...])).astype(BF16)


def back_body(info, states, attended, second_gain, *rest, n_pieces):
    outs, ups = (rest[i * n_pieces : (i + 1) * n_pieces] for i in range(2))
    middle, hidden, out_weight, up_weight, sems = rest[2 * n_pieces :]
    early = piece_copies(info[0], outs, out_weight, sems, 0)
    late = piece_copies(info[0], ups, up_weight, sems, n_pieces)
    start_all(early)
    start_all(late)
    wait_all(early)
    widen_rows(states, attended, out_weight, up_weight, second_gain, middle, hidden, late)


def down_body(info, middle_k, hidden_k, middle_g, hidden_g, *rest, n_pieces):
    pieces, (out, weight, acc, sems) = rest[:n_pieces], rest[n_pieces:]
    me, side = info[0], info[3]
    block = pieces[0].shape[0]
    loads = [
        pltpu.make_async_copy(piece, weight.at[k], sems.at[k]) for k, piece in enumerate(pieces)
    ]
    start_all(loads)
    for k, load in enumerate(loads):
        load.wait()
        cols = pl.ds(pl.multiple_of((me ^ k) * block, block), block)
        for i, (middle, hidden) in enumerate(((middle_k, hidden_k), (middle_g, hidden_g))):
            product = dot(hidden[:, cols], weight[k])
            if k == 0:
                acc[i] = middle[...].astype(F32) + product
            elif k < n_pieces - 1:
                acc[i] += product
            else:
                out[jnp.where(i == 0, side, 1 - side)] = (acc[i] + product).astype(BF16)


def call(body, outs, out_spaces, scratch, operands, spaces, flops, **static):
    return pl.pallas_call(
        functools.partial(body, **static),
        out_shape=[jax.ShapeDtypeStruct(shape, BF16) for shape in outs],
        in_specs=[pl.BlockSpec(memory_space=space) for space in spaces],
        out_specs=[pl.BlockSpec(memory_space=space) for space in out_spaces],
        scratch_shapes=scratch,
        cost_estimate=pl.CostEstimate(
            flops=flops, bytes_accessed=4 << 20, transcendentals=0
        ),
        compiler_params=pltpu.CompilerParams(vmem_limit_bytes=VMEM_LIMIT),
    )(*operands)


VMEM_LIMIT = 24 << 20


def send(axis, perm, array):
    return lax.ppermute(array, axis, perm)


def layer(
    node_states, projection, output_weight, up_weight, down_weight,
    attention_gain, feedforward_gain, tile_lists, tile_counts,
):
    members, rows, width = node_states.shape
    tiles, entries = tile_lists.shape
    tile_rows = rows // tiles
    hidden = up_weight.shape[1]
    ring, n = lax.axis_size("mesh"), lax.axis_size("member")
    if members != 2 or ring % 2 or ring < 4 or n & (n - 1) or RIM_T > tiles:
        raise ValueError("unsupported mesh")
    place, me = lax.axis_index("mesh"), lax.axis_index("member")
    side = place & 1
    info = jnp.stack([me, place, place ^ 1, side]).astype(jnp.int32)
    bits = [1 << b for b in reversed(range(n.bit_length() - 1))]
    swap = [(i, i ^ 1) for i in range(ring)]
    outward = [(i, (i + (2 if i % 2 else -2)) % ring) for i in range(ring)]
    inward = [(i, (i + (-2 if i % 2 else 2)) % ring) for i in range(ring)]

    def gather(shard):
        pieces = {0: shard}
        for bit in bits:
            perm = [(i, i ^ bit) for i in range(n)]
            for k, piece in list(pieces.items()):
                pieces[k ^ bit] = send("member", perm, piece)
        return [pieces[k] for k in range(n)]

    give = lax.dynamic_index_in_dim(node_states, 1 - side, 0, keepdims=False)
    keep = lax.dynamic_index_in_dim(node_states, side, 0, keepdims=False)
    their_lists = send("mesh", swap, tile_lists)
    their_counts = send("mesh", swap, tile_counts)
    got = send("mesh", swap, give)
    proj = gather(projection)
    far_near = send("mesh", outward, keep)
    far_late = send("mesh", inward, got)
    outs = gather(output_weight)
    ups = gather(up_weight)
    downs = gather(down_weight)

    gain = attention_gain.reshape(1, width)
    second = feedforward_gain.reshape(1, width)
    whole = lambda shard, cols: pltpu.VMEM((n * shard.shape[0], cols), BF16)
    window = [
        pltpu.VMEM((3 * rows, width), BF16),
        pltpu.VMEM((3 * tiles, width, tile_rows), BF16),
    ]
    flash = [
        pltpu.VMEM((2, entries * tile_rows, 2 * tile_rows), F32),
        pltpu.VMEM((2, 8, 2 * tile_rows), F32),
        pltpu.SMEM((tiles * entries,), jnp.int32),
    ]
    sems = pltpu.SemaphoreType.DMA
    static = dict(n_pieces=n, tile_rows=tile_rows)
    q_keep, q_got, k_near, v_near = call(
        near_body,
        [(rows, width), (rows, width), (2 * rows, width), (2 * tiles, width, tile_rows)],
        [ANY, ANY, ANY, ANY],
        [
            whole(projection, 3 * width),
            pltpu.VMEM((2 * rows, width), BF16),
            pltpu.VMEM((2 * rows, width), BF16),
            pltpu.VMEM((2 * rows, width), BF16),
            pltpu.VMEM((2 * tiles, width, tile_rows), BF16),
            sems((n + 6,)),
        ],
        [info, keep, got, gain, *proj],
        [SMEM, VMEM, VMEM, VMEM] + [ANY] * n,
        4 << 30, **static,
    )
    (attended_got,) = call(
        got_body,
        [(rows, width)],
        [VMEM],
        [whole(projection, 2 * width), *window, *flash, sems((n + 2,))],
        [
            info, their_lists, their_counts, far_near, q_got, k_near, v_near, gain, *proj
        ],
        [SMEM, SMEM, SMEM, VMEM, VMEM, ANY, ANY, VMEM] + [ANY] * n,
        4 << 30, **static,
    )
    attended_back = send("mesh", swap, attended_got)
    middle_k, hidden_k = call(
        keep_body,
        [(rows, width), (rows, hidden)],
        [VMEM, VMEM],
        [
            whole(projection, 2 * width),
            whole(output_weight, width),
            whole(up_weight, hidden),
            *window,
            pltpu.VMEM((rows, width), BF16),
            *flash,
            sems((3 * n + 2,)),
        ],
        [
            info, tile_lists, tile_counts, keep, far_late, q_keep, k_near, v_near,
            gain, second, *proj, *outs, *ups,
        ],
        [SMEM, SMEM, SMEM, VMEM, VMEM, VMEM, ANY, ANY, VMEM, VMEM] + [ANY] * (3 * n),
        6 << 30, **static,
    )
    middle_g, hidden_g = call(
        back_body,
        [(rows, width), (rows, hidden)],
        [VMEM, VMEM],
        [whole(output_weight, width), whole(up_weight, hidden), sems((2 * n,))],
        [info, give, attended_back, second, *outs, *ups],
        [SMEM, VMEM, VMEM, VMEM] + [ANY] * (2 * n),
        2 << 30, n_pieces=n,
    )
    (result,) = call(
        down_body,
        [node_states.shape],
        [VMEM],
        [
            pltpu.VMEM((n, *down_weight.shape), BF16),
            pltpu.VMEM((2, rows, width), F32),
            sems((n,)),
        ],
        [info, middle_k, hidden_k, middle_g, hidden_g, *downs],
        [SMEM, VMEM, VMEM, VMEM, VMEM] + [ANY] * n,
        2 << 30, n_pieces=n,
    )
    return result


def solution(mesh):
    in_specs = (
        P("member", "mesh", None),
        P("member", None),
        P("member", None),
        P("member", None),
        P("member", None),
        P(),
        P(),
        P("mesh", None),
        P("mesh"),
    )
    return jax.shard_map(
        layer, mesh=mesh, in_specs=in_specs,
        out_specs=P("member", "mesh", None), check_vma=False,
    )
```

profile of v0, /device:TPU:28, one launch (start us, length us, event | category | flops | bytes accessed | tf_op | source)
XLA Modules:
  0.0 84.6 jit_solution(12195794373960695972)
XLA Ops:
  0.0 1.6 %collective-permute-start.3 = (bf16[128,1536]{1,0:T(8,128)(2,1)}, bf16[128,1536]{1,0:T(8,128)(2,1)}, u32[]{:S(2)}, u32[]{:S(2)}) collective-permute-start(bf16[128,1536]{1,0:T(8,128)(2,1)} %rest_0_.7), channel_id=1, source_target_pairs={{0,2},{1,3},{2,0},{3,1},{4,6},{5,7},{6,4},{7,5},{8,10},{9,11},{10,... | collective-permute-start | bytes 1179656 | tf_op jit(solution)/shard_map/ppermute | solution.py:318
  1.6 1.3 %dynamic-slice_bitcast_fusion = (bf16[512,512]{1,0:T(8,128)(2,1)S(1)}, bf16[512,512]{1,0:T(8,128)(2,1)S(1)}) fusion(bf16[2,512,512]{2,1,0:T(8,128)(2,1)} %param.9, s32[]{:T(128)S(6)} %select_n.8, s32[]{:T(128)S(6)} %select_n.7), kind=kLoop, calls=%fused_computation | loop fusion | bytes 2097160 | tf_op jit(solution)/shard_map/jit(dynamic_index_in_dim)/squeeze | solution.py:348
  2.9 0.6 collective-permute-start
  3.5 0.5 collective-permute-start.9
  4.0 8.4 %collective-permute-done.3.rest_2_ = bf16[128,1536]{1,0:T(8,128)(2,1)} collective-permute-done((bf16[128,1536]{1,0:T(8,128)(2,1)}, bf16[128,1536]{1,0:T(8,128)(2,1)}, u32[]{:S(2)}, u32[]{:S(2)}) %collective-permute-start.3) | collective-permute-done | bytes 393248 | tf_op jit(solution)/shard_map/ppermute | solution.py:318
  12.4 0.5 collective-permute-start.12
  12.9 3.5 %collective-permute-done.12.counts = s32[4]{0:T(128)S(1)} collective-permute-done((s32[4]{0:T(128)S(1)}, s32[4]{0:T(128)S(1)}, u32[]{:S(2)}, u32[]{:S(2)}) %collective-permute-start.12) | collective-permute-done | bytes 48 | tf_op jit(solution)/shard_map/ppermute | solution.py:318
  16.5 0.5 copy-done.13
  17.0 0.5 collective-permute-start.11
  17.5 3.1 %collective-permute-done.11.lists = s32[4,8]{1,0:T(4,128)S(1)} collective-permute-done((s32[4,8]{1,0:T(4,128)S(1)}, s32[4,8]{1,0:T(4,128)S(1)}, u32[]{:S(2)}, u32[]{:S(2)}) %collective-permute-start.11) | collective-permute-done | bytes 160 | tf_op jit(solution)/shard_map/ppermute | solution.py:318
  20.5 1.3 %collective-permute-done.5.rest_5_.rest_1_ = bf16[128,512]{1,0:T(8,128)(2,1)S(1)} collective-permute-done((bf16[128,512]{1,0:T(8,128)(2,1)S(1)}, bf16[128,512]{1,0:T(8,128)(2,1)S(1)}, u32[]{:S(2)}, u32[]{:S(2)}) %collective-permute-start.5) | collective-permute-done | bytes 131104 | tf_op jit(solution)/shard_map/ppermute | solution.py:318
  21.9 0.7 copy-done.5
  22.5 1.0 %collective-permute-start.6 = (bf16[128,512]{1,0:T(8,128)(2,1)S(1)}, bf16[128,512]{1,0:T(8,128)(2,1)S(1)}, u32[]{:S(2)}, u32[]{:S(2)}) collective-permute-start(bf16[128,512]{1,0:T(8,128)(2,1)S(1)} %copy-done.3), channel_id=1, source_target_pairs={{0,2},{1,3},{2,0},{3,1},{4,6},{5,7},{6,4},{7,5},{8,10},{9,11},{10,... | collective-permute-start | bytes 393224 | tf_op jit(solution)/shard_map/ppermute | solution.py:318
  23.6 4.5 %collective-permute-done.6.rest_6_.rest_2_ = bf16[128,512]{1,0:T(8,128)(2,1)S(1)} collective-permute-done((bf16[128,512]{1,0:T(8,128)(2,1)S(1)}, bf16[128,512]{1,0:T(8,128)(2,1)S(1)}, u32[]{:S(2)}, u32[]{:S(2)}) %collective-permute-start.6) | collective-permute-done | bytes 131104 | tf_op jit(solution)/shard_map/ppermute | solution.py:318
  28.1 0.6 copy-done.7
  28.7 0.2 collective-permute-start.13
  29.0 0.1 pad_add_fusion.info
  29.0 0.0 collective-permute-start.8
  29.1 1.1 %collective-permute-start.16 = (bf16[512,512]{1,0:T(8,128)(2,1)S(1)}, bf16[512,512]{1,0:T(8,128)(2,1)S(1)}, u32[]{:S(2)}, u32[]{:S(2)}) collective-permute-start(bf16[512,512]{1,0:T(8,128)(2,1)S(1)} %copy-done), channel_id=1, source_target_pairs={{0,2},{1,3},{2,0},{3,1},{4,6},{5,7},{6,4},{7,5},{8,10},{9,11},{10,... | collective-permute-start | bytes 1572872 | tf_op jit(solution)/shard_map/ppermute | solution.py:318
  30.2 1.8 %collective-permute-start.1 = (bf16[512,512]{1,0:T(8,128)(2,1)S(1)}, bf16[512,512]{1,0:T(8,128)(2,1)S(1)}, u32[]{:S(2)}, u32[]{:S(2)}) collective-permute-start(bf16[512,512]{1,0:T(8,128)(2,1)S(1)} %collective-permute-done.got), channel_id=1, source_target_pairs={{0,8},{4,28},{8,16},{12,4},{16,24},{20,12},{24,0},{28,20},{1,9},{5... | collective-permute-start | bytes 1572872 | tf_op jit(solution)/shard_map/ppermute | solution.py:318
  32.0 4.8 %shard_map.91 = (bf16[512,512]{1,0:T(8,128)(2,1)S(1)}, bf16[512,512]{1,0:T(8,128)(2,1)S(1)}, bf16[1024,512]{1,0:T(8,128)(2,1)S(1)}, bf16[8,512,128]{2,1,0:T(8,128)(2,1)S(1)}) custom-call(s32[4]{0:T(128)S(1)} %pad_add_fusion.info, bf16[512,512]{1,0:T(8,128)(2,1)S(1)} %get-tuple-element.22.keep.states, bf16[512,512]{1,0:T(8,128)(2,1)S(1)} %collective-permute-done.got, ...), custom_call_target="tpu_custom_call" | custom-call | flops 4294967296 | bytes 4194304 | tf_op jit(solution)/shard_map/pallas_call | solution.py:301
  36.8 16.4 %collective-permute-done.13.far = bf16[512,512]{1,0:T(8,128)(2,1)} collective-permute-done((bf16[512,512]{1,0:T(8,128)(2,1)S(1)}, bf16[512,512]{1,0:T(8,128)(2,1)}, u32[]{:S(2)}, u32[]{:S(2)}) %collective-permute-start.13) | collective-permute-done | bytes 524320 | tf_op jit(solution)/shard_map/ppermute | solution.py:318
  53.2 0.0 copy-start.4
  53.2 0.0 copy-start.6
  53.2 0.0 copy-start.11
  53.2 7.7 %shard_map.93 = bf16[512,512]{1,0:T(8,128)(2,1)S(1)} custom-call(s32[4]{0:T(128)S(1)} %pad_add_fusion.info, s32[4,8]{1,0:T(4,128)S(1)} %collective-permute-done.11.lists, s32[4]{0:T(128)S(1)} %copy-done.14, bf16[512,512]{1,0:T(8,128)(2,1)} %collective-permute-done.13.far, bf16[512,512]{1,0:T(8,128)(2,1)S(1)} %get-tuple-element.18.queries, ...), custom_call_target="tpu_custom_call" | custom-call | flops 4294967296 | bytes 4194304 | tf_op jit(solution)/shard_map/pallas_call | solution.py:301
  61.0 0.5 collective-permute-start.15
  61.5 0.1 collective-permute-start.17
  61.7 10.8 %shard_map.92 = (bf16[512,512]{1,0:T(8,128)(2,1)S(1)}, bf16[512,2048]{1,0:T(8,128)(2,1)S(1)}) custom-call(s32[4]{0:T(128)S(1)} %pad_add_fusion.info, s32[4,8]{1,0:T(4,128)S(1)} %copy-done.9, s32[4]{0:T(128)S(1)} %copy-done.12, bf16[512,512]{1,0:T(8,128)(2,1)S(1)} %get-tuple-element.22.keep.states, bf16[512,512]{1,0:T(8,128)(2,1)S(1)} %collective-permute-done.1.far, ...), custom_call_target="tpu_custom_call" | custom-call | flops 6442450944 | bytes 4194304 | tf_op jit(solution)/shard_map/pallas_call | solution.py:301
  72.5 3.4 %collective-permute-done.14.attended = bf16[512,512]{1,0:T(8,128)(2,1)S(1)} collective-permute-done((bf16[512,512]{1,0:T(8,128)(2,1)S(1)}, bf16[512,512]{1,0:T(8,128)(2,1)S(1)}, u32[]{:S(2)}, u32[]{:S(2)}) %collective-permute-start.14) | collective-permute-done | bytes 524320 | tf_op jit(solution)/shard_map/ppermute | solution.py:318
  75.9 4.4 %shard_map.94 = (bf16[512,512]{1,0:T(8,128)(2,1)S(1)}, bf16[512,2048]{1,0:T(8,128)(2,1)S(1)}) custom-call(s32[4]{0:T(128)S(1)} %pad_add_fusion.info, bf16[512,512]{1,0:T(8,128)(2,1)S(1)} %get-tuple-element.21.states, bf16[512,512]{1,0:T(8,128)(2,1)S(1)} %collective-permute-done.14.attended, f32[1,512]{1,0:T(1,128)S(1)} %bitcast.14, ...), custom_call_target="tpu_custom_call" | custom-call | flops 2147483648 | bytes 4194304 | tf_op jit(solution)/shard_map/pallas_call | solution.py:301
  80.3 4.2 %shard_map.95 = bf16[2,512,512]{2,1,0:T(8,128)(2,1)} custom-call(s32[4]{0:T(128)S(1)} %pad_add_fusion.info, bf16[512,512]{1,0:T(8,128)(2,1)S(1)} %get-tuple-element.16.middle_k, bf16[512,2048]{1,0:T(8,128)(2,1)S(1)} %get-tuple-element.17.hidden_k, bf16[512,512]{1,0:T(8,128)(2,1)S(1)} %get-tuple-element.19.middle_g, ...), custom_call_target="tpu_custom_call" | custom-call | flops 2147483648 | bytes 4194304 | tf_op jit(solution)/shard_map/pallas_call | solution.py:301
  (41 shorter events, 0.1 us)
Async XLA Ops:
  0.0 4.0 %copy-start.2 = (bf16[128,1536]{1,0:T(8,128)(2,1)S(1)}, bf16[128,1536]{1,0:T(8,128)(2,1)}, u32[]{:S(2)}) copy-start(bf16[128,1536]{1,0:T(8,128)(2,1)} %rest_0_.7) | copy-start | bytes 1179652
  0.0 3.5 %copy-start.1 = (bf16[128,2048]{1,0:T(8,128)(2,1)S(1)}, bf16[128,2048]{1,0:T(8,128)(2,1)}, u32[]{:S(2)}) copy-start(bf16[128,2048]{1,0:T(8,128)(2,1)} %rest_4_.3) | copy-start | bytes 1572868
  0.0 12.4 %copy-start.12 = (s32[4]{0:T(128)S(1)}, s32[4]{0:T(128)}, u32[]{:S(2)}) copy-start(s32[4]{0:T(128)} %counts.1) | copy-start | bytes 52
  0.0 16.9 %copy-start.9 = (s32[4,8]{1,0:T(4,128)S(1)}, s32[4,8]{1,0:T(4,128)}, u32[]{:S(2)}) copy-start(s32[4,8]{1,0:T(4,128)} %lists.1) | copy-start | bytes 388
  0.0 29.1 %copy-start = (bf16[512,512]{1,0:T(8,128)(2,1)S(1)}, bf16[512,512]{1,0:T(8,128)(2,1)}, u32[]{:S(2)}) copy-start(bf16[512,512]{1,0:T(8,128)(2,1)} %rest_0_.9) | copy-start | bytes 1572868
  0.0 32.0 %copy-start.10 = (f32[512]{0:T(512)S(1)}, f32[512]{0:T(512)}, u32[]{:S(2)}) copy-start(f32[512]{0:T(512)} %param.14) | copy-start | bytes 6148
  0.0 12.4 %collective-permute-start.3 = (bf16[128,1536]{1,0:T(8,128)(2,1)}, bf16[128,1536]{1,0:T(8,128)(2,1)}, u32[]{:S(2)}, u32[]{:S(2)}) collective-permute-start(bf16[128,1536]{1,0:T(8,128)(2,1)} %rest_0_.7), channel_id=1, source_target_pairs={{0,2},{1,3},{2,0},{3,1},{4,6},{5,7},{6,4},{7,5},{8,10},{9,11},{10,... | collective-permute-start | bytes 1179656 | tf_op jit(solution)/shard_map/ppermute | solution.py:318
  1.6 18.9 %copy-start.3 = (bf16[128,512]{1,0:T(8,128)(2,1)S(1)}, bf16[128,512]{1,0:T(8,128)(2,1)}, u32[]{:S(2)}) copy-start(bf16[128,512]{1,0:T(8,128)(2,1)} %rest_0_.8) | copy-start | bytes 393220
  2.9 26.2 %collective-permute-start = (bf16[512,512]{1,0:T(8,128)(2,1)S(1)}, bf16[512,512]{1,0:T(8,128)(2,1)S(1)}, u32[]{:S(2)}, u32[]{:S(2)}) collective-permute-start(bf16[512,512]{1,0:T(8,128)(2,1)S(1)} %get-tuple-element.21.states), channel_id=1, source_target_pairs={{0,4},{4,0},{8,12},{12,8},{16,20},{20,16},{24,28},{28,24},{1,5},{5... | collective-permute-start | bytes 1572872 | tf_op jit(solution)/shard_map/ppermute | solution.py:318
  3.5 26.7 %collective-permute-start.9 = (bf16[128,2048]{1,0:T(8,128)(2,1)S(1)}, bf16[128,2048]{1,0:T(8,128)(2,1)S(1)}, u32[]{:S(2)}, u32[]{:S(2)}) collective-permute-start(bf16[128,2048]{1,0:T(8,128)(2,1)S(1)} %copy-done.1), channel_id=1, source_target_pairs={{0,2},{1,3},{2,0},{3,1},{4,6},{5,7},{6,4},{7,5},{8,10},{9,11},{10,... | collective-permute-start | bytes 1572872 | tf_op jit(solution)/shard_map/ppermute | solution.py:318
  4.0 25.0 %collective-permute-start.2 = (bf16[128,1536]{1,0:T(8,128)(2,1)S(1)}, bf16[128,1536]{1,0:T(8,128)(2,1)}, u32[]{:S(2)}, u32[]{:S(2)}) collective-permute-start(bf16[128,1536]{1,0:T(8,128)(2,1)S(1)} %copy-done.2), channel_id=1, source_target_pairs={{0,1},{1,0},{2,3},{3,2},{4,5},{5,4},{6,7},{7,6},{8,9},{9,8},{10,11... | collective-permute-start | bytes 1179656 | tf_op jit(solution)/shard_map/ppermute | solution.py:318
  12.4 19.6 %collective-permute-start.4 = (bf16[128,1536]{1,0:T(8,128)(2,1)}, bf16[128,1536]{1,0:T(8,128)(2,1)}, u32[]{:S(2)}, u32[]{:S(2)}) collective-permute-start(bf16[128,1536]{1,0:T(8,128)(2,1)} %collective-permute-done.3.rest_2_), channel_id=1, source_target_pairs={{0,1},{1,0},{2,3},{3,2},{4,5},{5,4},{6,7},{7,6},{8,9},{9,8},{10,11... | collective-permute-start | bytes 1179656 | tf_op jit(solution)/shard_map/ppermute | solution.py:318
  12.4 4.0 %collective-permute-start.12 = (s32[4]{0:T(128)S(1)}, s32[4]{0:T(128)S(1)}, u32[]{:S(2)}, u32[]{:S(2)}) collective-permute-start(s32[4]{0:T(128)S(1)} %copy-done.12), channel_id=1, source_target_pairs={{0,4},{4,0},{8,12},{12,8},{16,20},{20,16},{24,28},{28,24},{1,5},{5... | collective-permute-start | bytes 56 | tf_op jit(solution)/shard_map/ppermute | solution.py:318
  17.0 3.6 %collective-permute-start.11 = (s32[4,8]{1,0:T(4,128)S(1)}, s32[4,8]{1,0:T(4,128)S(1)}, u32[]{:S(2)}, u32[]{:S(2)}) collective-permute-start(s32[4,8]{1,0:T(4,128)S(1)} %copy-done.9), channel_id=1, source_target_pairs={{0,4},{4,0},{8,12},{12,8},{16,20},{20,16},{24,28},{28,24},{1,5},{5... | collective-permute-start | bytes 392 | tf_op jit(solution)/shard_map/ppermute | solution.py:318
  20.5 1.3 %collective-permute-start.5 = (bf16[128,512]{1,0:T(8,128)(2,1)S(1)}, bf16[128,512]{1,0:T(8,128)(2,1)S(1)}, u32[]{:S(2)}, u32[]{:S(2)}) collective-permute-start(bf16[128,512]{1,0:T(8,128)(2,1)S(1)} %copy-done.3), channel_id=1, source_target_pairs={{0,1},{1,0},{2,3},{3,2},{4,5},{5,4},{6,7},{7,6},{8,9},{9,8},{10,11... | collective-permute-start | bytes 393224 | tf_op jit(solution)/shard_map/ppermute | solution.py:318
  21.9 0.7 copy-start.5
  22.5 5.5 %collective-permute-start.6 = (bf16[128,512]{1,0:T(8,128)(2,1)S(1)}, bf16[128,512]{1,0:T(8,128)(2,1)S(1)}, u32[]{:S(2)}, u32[]{:S(2)}) collective-permute-start(bf16[128,512]{1,0:T(8,128)(2,1)S(1)} %copy-done.3), channel_id=1, source_target_pairs={{0,2},{1,3},{2,0},{3,1},{4,6},{5,7},{6,4},{7,5},{8,10},{9,11},{10,... | collective-permute-start | bytes 393224 | tf_op jit(solution)/shard_map/ppermute | solution.py:318
  28.1 0.6 copy-start.7
  28.7 24.5 %collective-permute-start.13 = (bf16[512,512]{1,0:T(8,128)(2,1)S(1)}, bf16[512,512]{1,0:T(8,128)(2,1)}, u32[]{:S(2)}, u32[]{:S(2)}) collective-permute-start(bf16[512,512]{1,0:T(8,128)(2,1)S(1)} %get-tuple-element.22.keep.states), channel_id=1, source_target_pairs={{0,24},{4,12},{8,0},{12,20},{16,8},{20,28},{24,16},{28,4},{1,25},{... | collective-permute-start | bytes 1572872 | tf_op jit(solution)/shard_map/ppermute | solution.py:318
  29.0 32.6 %collective-permute-start.8 = (bf16[128,2048]{1,0:T(8,128)(2,1)S(1)}, bf16[128,2048]{1,0:T(8,128)(2,1)S(1)}, u32[]{:S(2)}, u32[]{:S(2)}) collective-permute-start(bf16[128,2048]{1,0:T(8,128)(2,1)S(1)} %copy-done.1), channel_id=1, source_target_pairs={{0,1},{1,0},{2,3},{3,2},{4,5},{5,4},{6,7},{7,6},{8,9},{9,8},{10,11... | collective-permute-start | bytes 1572872 | tf_op jit(solution)/shard_map/ppermute | solution.py:318
  29.1 32.4 %collective-permute-start.16 = (bf16[512,512]{1,0:T(8,128)(2,1)S(1)}, bf16[512,512]{1,0:T(8,128)(2,1)S(1)}, u32[]{:S(2)}, u32[]{:S(2)}) collective-permute-start(bf16[512,512]{1,0:T(8,128)(2,1)S(1)} %copy-done), channel_id=1, source_target_pairs={{0,2},{1,3},{2,0},{3,1},{4,6},{5,7},{6,4},{7,5},{8,10},{9,11},{10,... | collective-permute-start | bytes 1572872 | tf_op jit(solution)/shard_map/ppermute | solution.py:318
  30.2 31.4 %collective-permute-start.1 = (bf16[512,512]{1,0:T(8,128)(2,1)S(1)}, bf16[512,512]{1,0:T(8,128)(2,1)S(1)}, u32[]{:S(2)}, u32[]{:S(2)}) collective-permute-start(bf16[512,512]{1,0:T(8,128)(2,1)S(1)} %collective-permute-done.got), channel_id=1, source_target_pairs={{0,8},{4,28},{8,16},{12,4},{16,24},{20,12},{24,0},{28,20},{1,9},{5... | collective-permute-start | bytes 1572872 | tf_op jit(solution)/shard_map/ppermute | solution.py:318
  32.0 29.6 %collective-permute-start.10 = (bf16[128,2048]{1,0:T(8,128)(2,1)S(1)}, bf16[128,2048]{1,0:T(8,128)(2,1)S(1)}, u32[]{:S(2)}, u32[]{:S(2)}) collective-permute-start(bf16[128,2048]{1,0:T(8,128)(2,1)S(1)} %collective-permute-done.9.rest_10_.rest_6_), channel_id=1, source_target_pairs={{0,1},{1,0},{2,3},{3,2},{4,5},{5,4},{6,7},{7,6},{8,9},{9,8},{10,11... | collective-permute-start | bytes 1572872 | tf_op jit(solution)/shard_map/ppermute | solution.py:318
  32.0 21.2 %copy-start.8 = (bf16[128,512]{1,0:T(8,128)(2,1)S(1)}, bf16[128,512]{1,0:T(8,128)(2,1)}, u32[]{:S(2)}) copy-start(bf16[128,512]{1,0:T(8,128)(2,1)} %copy-done.7) | copy-start | bytes 393220
  32.0 21.2 %copy-start.14 = (s32[4]{0:T(128)S(1)}, s32[4]{0:T(128)}, u32[]{:S(2)}) copy-start(s32[4]{0:T(128)} %copy-done.13) | copy-start | bytes 52
  53.2 7.8 %collective-permute-start.7 = (bf16[128,512]{1,0:T(8,128)(2,1)S(1)}, bf16[128,512]{1,0:T(8,128)(2,1)S(1)}, u32[]{:S(2)}, u32[]{:S(2)}) collective-permute-start(bf16[128,512]{1,0:T(8,128)(2,1)S(1)} %copy-done.8), channel_id=1, source_target_pairs={{0,1},{1,0},{2,3},{3,2},{4,5},{5,4},{6,7},{7,6},{8,9},{9,8},{10,11... | collective-permute-start | bytes 393224 | tf_op jit(solution)/shard_map/ppermute | solution.py:318
  53.2 8.4 %copy-start.4 = (bf16[128,512]{1,0:T(8,128)(2,1)S(1)}, bf16[128,512]{1,0:T(8,128)(2,1)}, u32[]{:S(2)}) copy-start(bf16[128,512]{1,0:T(8,128)(2,1)} %rest_0_.8) | copy-start | bytes 393220
  53.2 8.4 %copy-start.6 = (bf16[128,512]{1,0:T(8,128)(2,1)S(1)}, bf16[128,512]{1,0:T(8,128)(2,1)}, u32[]{:S(2)}) copy-start(bf16[128,512]{1,0:T(8,128)(2,1)} %copy-done.5) | copy-start | bytes 393220
  53.2 8.4 %copy-start.11 = (f32[512]{0:T(512)S(1)}, f32[512]{0:T(512)}, u32[]{:S(2)}) copy-start(f32[512]{0:T(512)} %param.15) | copy-start | bytes 6148
  61.0 19.2 %collective-permute-start.15 = (bf16[512,512]{1,0:T(8,128)(2,1)S(1)}, bf16[512,512]{1,0:T(8,128)(2,1)S(1)}, u32[]{:S(2)}, u32[]{:S(2)}) collective-permute-start(bf16[512,512]{1,0:T(8,128)(2,1)S(1)} %copy-done), channel_id=1, source_target_pairs={{0,1},{1,0},{2,3},{3,2},{4,5},{5,4},{6,7},{7,6},{8,9},{9,8},{10,11... | collective-permute-start | bytes 1572872 | tf_op jit(solution)/shard_map/ppermute | solution.py:318
  61.5 18.7 %collective-permute-start.17 = (bf16[512,512]{1,0:T(8,128)(2,1)S(1)}, bf16[512,512]{1,0:T(8,128)(2,1)S(1)}, u32[]{:S(2)}, u32[]{:S(2)}) collective-permute-start(bf16[512,512]{1,0:T(8,128)(2,1)S(1)} %collective-permute-done.16.rest_2_), channel_id=1, source_target_pairs={{0,1},{1,0},{2,3},{3,2},{4,5},{5,4},{6,7},{7,6},{8,9},{9,8},{10,11... | collective-permute-start | bytes 1572872 | tf_op jit(solution)/shard_map/ppermute | solution.py:318
  61.6 14.3 %collective-permute-start.14 = (bf16[512,512]{1,0:T(8,128)(2,1)S(1)}, bf16[512,512]{1,0:T(8,128)(2,1)S(1)}, u32[]{:S(2)}, u32[]{:S(2)}) collective-permute-start(bf16[512,512]{1,0:T(8,128)(2,1)S(1)} %shard_map.93), channel_id=1, source_target_pairs={{0,4},{4,0},{8,12},{12,8},{16,20},{20,16},{24,28},{28,24},{1,5},{5... | collective-permute-start | bytes 1572872 | tf_op jit(solution)/shard_map/ppermute | solution.py:318
  (1 other events, 0.5 us)
where the time goes:
time: 84.9 us; the launch traced here: 84.6 us
  waiting for transfers between devices  40.6 us (48%)
  Pallas kernels  31.9 us (38%)
  starting transfers between devices  8.45 us (10%)
  local copies, waits for them, and re-layouts  3.15 us (4%)
    ppermute x18, waiting for transfers between devices, send(): return lax.ppermute(array, axis, perm)  40.6 us
    pallas_call x5, Pallas kernels, call(): pl.pallas_call(functools.partial(body, **static), out_shape=[jax.ShapeDty...  31.9 us
    ppermute x18, starting transfers between devices, send(): return lax.ppermute(array, axis, perm)  8.45 us
    unnamed x30, local copies, waits for them, and re-layouts  1.85 us
  transfers between devices with their start and end apart: 18, of which 7 were waited for; matrix products, arithmetic and copies ran while one was open for 2% of the time, Pallas kernels for 33%

commit v1 on v0

v1 whole, which is shorter than its diff:
```python
import functools
import math

import jax
import jax.numpy as jnp
from jax import lax
from jax.experimental import pallas as pl
from jax.experimental.pallas import tpu as pltpu
from jax.sharding import PartitionSpec as P

HEADS = 4
RIM_T = 4
EXTRA = 16
SURE = 4
BF16 = jnp.bfloat16
F32 = jnp.float32
VMEM = pltpu.VMEM
ANY = pl.ANY
HBM = pltpu.HBM


def norm_rows(rows, gain):
    values = rows.astype(F32)
    center = values - jnp.mean(values, axis=-1, keepdims=True)
    spread = jnp.mean(center * center, axis=-1, keepdims=True)
    return (center * lax.rsqrt(spread + 1e-05) * gain).astype(BF16)


def dot(a, b):
    return lax.dot_general(a, b, (((1,), (0,)), ((), ())), preferred_element_type=F32)


def dot_t(a, b):
    return lax.dot_general(a, b, (((1,), (1,)), ((), ())), preferred_element_type=F32)


def gelu(x):
    linear = math.sqrt(2 / math.pi)
    half = 0.5 * x
    return half + half * jnp.tanh(x * (linear + (0.044715 * linear) * (x * x)))


def places(count, block):
    me = lax.axis_index("member")
    return [pl.multiple_of((me ^ k) * block, block) for k in range(count)]


def stacked(pieces, cols=slice(None)):
    return jnp.concatenate([piece[:, cols] for piece in pieces], axis=0)


def matched(rows, pieces):
    block = pieces[0].shape[0]
    return jnp.concatenate(
        [rows[:, pl.ds(at, block)] for at in places(len(pieces), block)], axis=1
    )


def norm_matched(source, gain, target, pieces):
    block = pieces[0].shape[0]
    me = lax.axis_index("member")
    step = 128
    for r in range(0, target.shape[0], step):
        normed = norm_rows(source[r : r + step, :], gain[...])
        for k in range(len(pieces)):
            target[r : r + step, pl.ds(pl.multiple_of((me ^ k) * block, block), block)] = normed[
                :, k * block : (k + 1) * block
            ]


def project(normed, pieces, queries, keys, values, key_row, first_tile, tile_rows):
    count, width = normed.shape
    rows = normed[...]
    if queries is not None:
        queries[...] = dot(rows, stacked(pieces, slice(0, width))).astype(BF16)
    keys[pl.ds(key_row, count), :] = dot(
        rows, stacked(pieces, slice(width, 2 * width))
    ).astype(BF16)
    block = dot(rows, stacked(pieces, slice(2 * width, 3 * width))).astype(BF16)
    for t in range(count // tile_rows):
        values[first_tile + t] = block[t * tile_rows : (t + 1) * tile_rows].T


def attend_tiles(plan, q_ref, k_ref, v_ref, out_ref, scores, tops, tile_rows, entries):
    rows, width = q_ref.shape
    tiles = rows // tile_rows
    head = width // HEADS
    scale = math.log2(math.e) / math.sqrt(head)
    zero = jnp.zeros((tile_rows, head), BF16)

    def stage(t, p, at):
        row = pl.multiple_of(t * tile_rows, tile_rows)
        first = q_ref[pl.ds(row, tile_rows), 2 * p * head : (2 * p + 1) * head]
        second = q_ref[pl.ds(row, tile_rows), (2 * p + 1) * head : (2 * p + 2) * head]
        both = jnp.concatenate(
            [jnp.concatenate([first, zero], 1), jnp.concatenate([zero, second], 1)], 0
        )
        cols = slice(2 * p * head, (2 * p + 2) * head)
        keys = jnp.concatenate(
            [
                k_ref[pl.ds(pl.multiple_of(plan[t, j] * tile_rows, tile_rows), tile_rows), cols]
                for j in range(entries)
            ],
            0,
        )
        product = dot_t(keys, both)
        scores[at] = product
        top = None
        for j in range(entries):
            part = product[j * tile_rows : (j + 1) * tile_rows]
            part = jnp.max(part.reshape(tile_rows // 8, 8, 2 * tile_rows), axis=0)
            if j >= SURE:
                part = jnp.where(j < plan[8, t], part, -jnp.inf)
            top = part if top is None else jnp.maximum(top, part)
        top = jnp.max(top, axis=0, keepdims=True) * scale
        tops[at] = jnp.broadcast_to(top, tops.shape[1:])

    def blend(t, p, at):
        row = pl.multiple_of(t * tile_rows, tile_rows)
        top = tops[at, 0:1]
        total, outs = None, [None, None]
        for pair in range(0, entries, 2):
            weights = []
            for j in (pair, pair + 1):
                highest = jnp.where(j < plan[8, t], top, jnp.inf) if j >= SURE else top
                weight = jnp.exp2(scores[at, j * tile_rows : (j + 1) * tile_rows] * scale - highest)
                part = jnp.sum(weight.reshape(tile_rows // 8, 8, 2 * tile_rows), axis=0)
                total = part if total is None else total + part
                weights.append(weight.astype(BF16))
            weights = jnp.concatenate(weights, 0)
            for a in range(2):
                h = 2 * p + a
                values = jnp.concatenate(
                    [
                        v_ref[plan[t, j], h * head : (h + 1) * head, :]
                        for j in (pair, pair + 1)
                    ],
                    1,
                )
                out = dot(values, weights[:, a * tile_rows : (a + 1) * tile_rows])
                outs[a] = out if outs[a] is None else outs[a] + out
        total = jnp.sum(total, axis=0, keepdims=True)
        for a in range(2):
            h = 2 * p + a
            out = outs[a] / total[:, a * tile_rows : (a + 1) * tile_rows]
            out_ref[pl.ds(row, tile_rows), h * head : (h + 1) * head] = out.T.astype(BF16)

    pairs = HEADS // 2
    stage(0, 0, 0)

    def one_tile(t, carry):
        for p in range(pairs):
            last = p == pairs - 1
            following = jnp.minimum(t + 1, tiles - 1) if last else t
            stage(following, 0 if last else p + 1, (p + 1) % 2)
            blend(t, p, p % 2)
        return carry

    lax.fori_loop(0, tiles, one_tile, 0)


def slot_rows(lists, counts, place, ring, own_block):
    tiles, _ = lists.shape
    ids = lists[...]
    other = place ^ 1
    third = lax.rem(place + jnp.where(place & 1 == 1, 1, ring - 1), jnp.int32(ring))

    def inside(device):
        inner = ids - device * tiles
        return (inner >= 0) & (inner < tiles), inner

    mine, inner = inside(place)
    theirs, inner_theirs = inside(other)
    slots = jnp.where(
        mine,
        inner + own_block * tiles,
        jnp.where(
            theirs, inner_theirs + (1 - own_block) * tiles, ids - third * tiles + 2 * tiles
        ),
    )
    return jnp.clip(slots, 0, 3 * tiles - 1).astype(F32), counts[...].astype(F32)


def write_table(target, row, slots, counts):
    target[pl.ds(row, EXTRA), :] = jnp.zeros((EXTRA, target.shape[1]), BF16)
    table = jnp.concatenate(
        [
            jnp.pad(slots, ((0, 8 - slots.shape[0]), (0, 128 - slots.shape[1]))),
            jnp.pad(counts, ((0, 7), (0, 128 - counts.shape[1]))),
        ],
        axis=0,
    )
    target[pl.ds(row, EXTRA), 0:128] = table.astype(BF16)


def pack_body(
    states, lists_in, counts_in, gains_in, more_gains_in, give, keep, table, gains, more_gains,
    lists, counts, sems, *, ring,
):
    place = lax.axis_index("mesh")
    side = place & 1
    rows = keep.shape[0]
    copies = [
        pltpu.make_async_copy(lists_in, lists, sems.at[0]),
        pltpu.make_async_copy(counts_in, counts, sems.at[1]),
        pltpu.make_async_copy(states.at[1 - side], give.at[pl.ds(0, rows)], sems.at[2]),
        pltpu.make_async_copy(states.at[side], keep, sems.at[3]),
        pltpu.make_async_copy(gains_in, gains, sems.at[4]),
        pltpu.make_async_copy(more_gains_in, more_gains, sems.at[5]),
    ]
    for copy in copies:
        copy.start()
    for copy in copies[:2]:
        copy.wait()
    write_table(table, 0, *slot_rows(lists, counts, place, ring, 0))
    write_table(give, rows, *slot_rows(lists, counts, place, ring, 1))
    for copy in copies[2:]:
        copy.wait()


def stage_body(source, target, sem):
    copy = pltpu.make_async_copy(source, target, sem)
    copy.start()
    copy.wait()


def near_body(source, gain, *rest, n_pieces, tile_rows):
    pieces, (queries, keys, values, normed) = rest[:n_pieces], rest[n_pieces:]
    norm_matched(source, gain, normed, pieces)
    project(normed, pieces, queries, keys, values, 0, 0, tile_rows)


def reach_body(
    table, far, queries, k_keep, v_keep, k_got, v_got, gain, *rest,
    n_pieces, tile_rows, entries,
):
    pieces, (attended, keys, values, normed, scores, tops, whole, plan, sems) = (
        rest[:n_pieces],
        rest[n_pieces:],
    )
    rows = queries.shape[0]
    tiles = rows // tile_rows
    last = table.shape[0] - EXTRA
    whole[...] = table[last:, 0:128].astype(F32).astype(jnp.int32)
    copies = [
        pltpu.make_async_copy(whole, plan, sems.at[0]),
        pltpu.make_async_copy(k_keep, keys.at[pl.ds(0, rows)], sems.at[1]),
        pltpu.make_async_copy(v_keep, values.at[pl.ds(0, tiles)], sems.at[2]),
        pltpu.make_async_copy(k_got, keys.at[pl.ds(rows, rows)], sems.at[3]),
        pltpu.make_async_copy(v_got, values.at[pl.ds(tiles, tiles)], sems.at[4]),
    ]
    for copy in copies:
        copy.start()
    norm_matched(far, gain, normed, pieces)
    project(normed, pieces, None, keys, values, 2 * rows, 2 * tiles, tile_rows)
    for copy in copies:
        copy.wait()
    attend_tiles(
        plan, queries, keys, values, attended, scores, tops, tile_rows, entries
    )


def widen_body(states, attended, gain, *rest, n_pieces):
    outs, ups = (rest[i * n_pieces : (i + 1) * n_pieces] for i in range(2))
    middle, hidden, mid_scratch, normed = rest[2 * n_pieces :]
    rows = attended.shape[0]
    for r in range(0, rows, 128):
        at = pl.ds(r, 128)
        mid = states[at, :].astype(F32) + dot(matched(attended.at[at], outs), stacked(outs))
        middle[at, :] = mid.astype(BF16)
        mid_scratch[at, :] = mid.astype(BF16)
    norm_matched(mid_scratch, gain, normed, ups)
    for c in range(0, hidden.shape[1], 256):
        cols = slice(c, c + 256)
        hidden[:, cols] = gelu(dot(normed[...], stacked(ups, cols))).astype(BF16)


def down_body(middle_k, hidden_k, middle_g, hidden_g, *rest, n_pieces):
    pieces, (out, staged, sems) = rest[:n_pieces], rest[n_pieces:]
    side = lax.axis_index("mesh") & 1
    starts = places(n_pieces, pieces[0].shape[0])
    rows = middle_k.shape[0]
    step = 256
    copies = []
    for member, middle, hidden in ((side, middle_k, hidden_k), (1 - side, middle_g, hidden_g)):
        for r in range(0, rows, step):
            at = pl.ds(r, step)
            total = middle[at, :].astype(F32)
            for start, piece in zip(starts, pieces):
                total = total + dot(hidden[at, pl.ds(start, piece.shape[0])], piece[...])
            where = len(copies)
            staged[where] = total.astype(BF16)
            copies.append(
                pltpu.make_async_copy(staged.at[where], out.at[member, at], sems.at[where])
            )
            copies[-1].start()
    for copy in copies:
        copy.wait()


def call(body, outs, scratch, operands, spaces, flops, space=VMEM, moved=4 << 20, **static):
    return pl.pallas_call(
        functools.partial(body, **static),
        out_shape=[
            jax.ShapeDtypeStruct(
                [d for d in shape if isinstance(d, int)],
                BF16 if isinstance(shape[-1], int) else shape[-1],
            )
            for shape in outs
        ],
        in_specs=[pl.BlockSpec(memory_space=space) for space in spaces],
        out_specs=[pl.BlockSpec(memory_space=space) for _ in outs],
        scratch_shapes=scratch,
        cost_estimate=pl.CostEstimate(
            flops=flops, bytes_accessed=moved, transcendentals=0
        ),
        compiler_params=pltpu.CompilerParams(vmem_limit_bytes=VMEM_LIMIT),
    )(*operands)


VMEM_LIMIT = 24 << 20


def in_hbm(array):
    return pltpu.with_memory_space_constraint(array, HBM)


def send(axis, perm, array):
    return lax.ppermute(array, axis, perm)


def layer(
    node_states, projection, output_weight, up_weight, down_weight,
    attention_gain, feedforward_gain, tile_lists, tile_counts,
):
    members, rows, width = node_states.shape
    tiles, entries = tile_lists.shape
    tile_rows = rows // tiles
    hidden = up_weight.shape[1]
    ring, n = lax.axis_size("mesh"), lax.axis_size("member")
    if members != 2 or ring % 2 or ring < 4 or n & (n - 1) or RIM_T > tiles or tiles > 8:
        raise ValueError("unsupported mesh")
    bits = [1 << b for b in reversed(range(n.bit_length() - 1))]
    swap = [(i, i ^ 1) for i in range(ring)]
    outward = [(i, (i + (2 if i % 2 else -2)) % ring) for i in range(ring)]
    inward = [(i, (i + (-2 if i % 2 else 2)) % ring) for i in range(ring)]

    def gather(shard):
        pieces = {0: shard}
        for bit in bits:
            perm = [(i, i ^ bit) for i in range(n)]
            for k, piece in list(pieces.items()):
                pieces[k ^ bit] = send("member", perm, piece)
        return [pieces[k] for k in range(n)]

    give, keep, table, gain, second = call(
        pack_body,
        [(rows + EXTRA, width), (rows, width), (EXTRA, width), (1, width, F32), (1, width, F32)],
        [
            pltpu.VMEM((tiles, entries), jnp.int32),
            pltpu.VMEM((1, tiles), jnp.int32),
            pltpu.SemaphoreType.DMA((6,)),
        ],
        [
            in_hbm(x)
            for x in (
                node_states, tile_lists, tile_counts.reshape(1, tiles),
                attention_gain.reshape(1, width), feedforward_gain.reshape(1, width),
            )
        ],
        [HBM] * 5,
        1 << 20, moved=0, ring=ring,
    )
    got = send("mesh", swap, give)
    proj = gather(projection)
    far_near = send("mesh", outward, keep)
    far_late = send("mesh", inward, got)
    outs = gather(output_weight)
    ups = gather(up_weight)
    downs = gather(down_weight)

    block = pltpu.VMEM((rows, width), BF16)
    window = [
        pltpu.VMEM((3 * rows, width), BF16),
        pltpu.VMEM((3 * tiles, width, tile_rows), BF16),
        block,
        pltpu.VMEM((2, entries * tile_rows, 2 * tile_rows), F32),
        pltpu.VMEM((2, 8, 2 * tile_rows), F32),
        pltpu.VMEM((EXTRA, 128), jnp.int32),
        pltpu.SMEM((EXTRA, 128), jnp.int32),
        pltpu.SemaphoreType.DMA((5,)),
    ]

    (own,) = call(
        stage_body,
        [projection.shape],
        [pltpu.SemaphoreType.DMA],
        [in_hbm(projection)],
        [HBM],
        1 << 20, moved=0,
    )
    proj = [own, *proj[1:]]

    def near(source):
        return call(
            near_body,
            [(rows, width), (rows, width), (tiles, width, tile_rows)],
            [block],
            [source, gain, *proj],
            [VMEM] * (2 + n),
            2 << 30, n_pieces=n, tile_rows=tile_rows,
        )

    def reach(table, far, queries):
        (attended,) = call(
            reach_body,
            [(rows, width)],
            window,
            [table, far, queries, k_keep, v_keep, k_got, v_got, gain, *proj],
            [VMEM, VMEM, VMEM, ANY, ANY, ANY, ANY, VMEM] + [VMEM] * n,
            4 << 30, n_pieces=n, tile_rows=tile_rows, entries=entries,
        )
        return attended

    def widen(states, attended):
        return call(
            widen_body,
            [(rows, width), (rows, hidden)],
            [block, block],
            [states, attended, second, *outs, *ups],
            [VMEM] * (3 + 2 * n),
            3 << 30, n_pieces=n,
        )

    q_keep, k_keep, v_keep = near(keep)
    q_got, k_got, v_got = near(got)
    attended_got = reach(got, far_near, q_got)
    attended_back = send("mesh", swap, attended_got)
    attended_keep = reach(table, far_late, q_keep)
    middle_k, hidden_k = widen(keep, attended_keep)
    middle_g, hidden_g = widen(give, attended_back)
    step = math.gcd(rows, 256)
    (result,) = call(
        down_body,
        [node_states.shape],
        [
            pltpu.VMEM((2 * rows // step, step, width), BF16),
            pltpu.SemaphoreType.DMA((2 * rows // step,)),
        ],
        [middle_k, hidden_k, middle_g, hidden_g, *downs],
        [VMEM] * (4 + n),
        4 << 30, space=ANY, n_pieces=n,
    )
    return result


def solution(mesh):
    in_specs = (
        P("member", "mesh", None),
        P("member", None),
        P("member", None),
        P("member", None),
        P("member", None),
        P(),
        P(),
        P("mesh", None),
        P("mesh"),
    )
    return jax.shard_map(
        layer, mesh=mesh, in_specs=in_specs,
        out_specs=P("member", "mesh", None), check_vma=False,
    )
```

time: 84.9 us -> 64.6 us (0.76)
  waiting for transfers between devices: 40.6 us -> 31.4 us
  Pallas kernels: 31.9 us -> 25.2 us
  local copies, waits for them, and re-layouts: 3.15 us -> 0.02 us
  starting transfers between devices: 8.45 us -> 7.55 us
    ppermute x18 -> x16, waiting for transfers between devices: 40.6 us -> 31.4 us  [send(): return lax.ppermute(array, axis, perm)]
    pallas_call x5 -> x9, Pallas kernels: 31.9 us -> 25.2 us  [call(): pl.pallas_call(functools.partial(body, **static), out_shape=[jax.ShapeDty...]
    unnamed x30 -> x6, local copies, waits for them, and re-layouts: 1.85 us -> 0.02 us
    squeeze x1 -> x0, local copies, waits for them, and re-layouts: 1.3 us -> none  [layer(): give = lax.dynamic_index_in_dim(node_states, 1 - side, 0, keepdims=False)]
    ppermute x18 -> x16, starting transfers between devices: 8.45 us -> 7.55 us  [send(): return lax.ppermute(array, axis, perm)]
  transfers between devices with their start and end apart: 18 -> 16, of which waited for: 7 -> 5; matrix products, arithmetic and copies ran while one was open for 2% -> 0% of each run, Pallas kernels for 33% -> 34%
where the time goes in v1:
time: 64.6 us; the launch traced here: 64.5 us
  waiting for transfers between devices  31.4 us (49%)
  Pallas kernels  25.2 us (39%)
  starting transfers between devices  7.55 us (12%)
    ppermute x16, waiting for transfers between devices, send(): return lax.ppermute(array, axis, perm)  31.4 us
    pallas_call x9, Pallas kernels, call(): pl.pallas_call(functools.partial(body, **static), out_shape=[jax.ShapeDty...  25.2 us
    ppermute x16, starting transfers between devices, send(): return lax.ppermute(array, axis, perm)  7.55 us
  transfers between devices with their start and end apart: 16, of which 5 were waited for; matrix products, arithmetic and copies ran while one was open for 0% of the time, Pallas kernels for 34%

profile of v1, /device:TPU:28, one launch (start us, length us, event | category | flops | bytes accessed | tf_op | source)
XLA Modules:
  0.0 64.5 jit_solution(9435192324638232451)
XLA Ops:
  0.0 1.5 %collective-permute-start.3 = (bf16[128,1536]{1,0:T(8,128)(2,1)}, bf16[128,1536]{1,0:T(8,128)(2,1)S(1)}, u32[]{:S(2)}, u32[]{:S(2)}) collective-permute-start(bf16[128,1536]{1,0:T(8,128)(2,1)} %source.1), channel_id=1, source_target_pairs={{0,2},{1,3},{2,0},{3,1},{4,6},{5,7},{6,4},{7,5},{8,10},{9,11},{10,... | collective-permute-start | bytes 1179656 | tf_op jit(solution)/shard_map/ppermute | solution.py:329
  1.5 1.3 %shard_map.91 = (bf16[528,512]{1,0:T(8,128)(2,1)S(1)}, bf16[512,512]{1,0:T(8,128)(2,1)S(1)}, bf16[16,512]{1,0:T(8,128)(2,1)S(1)}, f32[1,512]{1,0:T(1,128)S(1)}, f32[1,512]{1,0:T(1,128)S(1)}) custom-call(bf16[2,512,512]{2,1,0:T(8,128)(2,1)} %states.1, s32[4,8]{1,0:T(4,128)} %lists_in.1, s32[1,4]{1,0:T(1,128)} %bitcast.5, f32[1,512]{1,0:T(1,128)} %bitcast.3, ...), custom_call_target="tpu_custom_call" | custom-call | flops 1048576 | tf_op jit(solution)/shard_map/pallas_call | solution.py:302
  2.8 0.6 collective-permute-start
  3.4 7.7 %collective-permute-done.3.rest_2_ = bf16[128,1536]{1,0:T(8,128)(2,1)S(1)} collective-permute-done((bf16[128,1536]{1,0:T(8,128)(2,1)}, bf16[128,1536]{1,0:T(8,128)(2,1)S(1)}, u32[]{:S(2)}, u32[]{:S(2)}) %collective-permute-start.3) | collective-permute-done | bytes 393248 | tf_op jit(solution)/shard_map/ppermute | solution.py:329
  11.1 1.5 %collective-permute-start.9 = (bf16[128,2048]{1,0:T(8,128)(2,1)}, bf16[128,2048]{1,0:T(8,128)(2,1)S(1)}, u32[]{:S(2)}, u32[]{:S(2)}) collective-permute-start(bf16[128,2048]{1,0:T(8,128)(2,1)} %rest_4_.3), channel_id=1, source_target_pairs={{0,2},{1,3},{2,0},{3,1},{4,6},{5,7},{6,4},{7,5},{8,10},{9,11},{10,... | collective-permute-start | bytes 1572872 | tf_op jit(solution)/shard_map/ppermute | solution.py:329
  12.6 0.2 collective-permute-start.11
  12.8 1.0 %shard_map.92.rest_0_ = bf16[128,1536]{1,0:T(8,128)(2,1)S(1)} custom-call(bf16[128,1536]{1,0:T(8,128)(2,1)} %source.1), custom_call_target="tpu_custom_call" | custom-call | flops 1048576 | tf_op jit(solution)/shard_map/pallas_call | solution.py:302
  13.8 0.0 collective-permute-done.2.rest_1_
  13.8 0.1 collective-permute-start.5
  13.9 2.7 %collective-permute-done.source.table = bf16[528,512]{1,0:T(8,128)(2,1)S(1)} collective-permute-done((bf16[528,512]{1,0:T(8,128)(2,1)S(1)}, bf16[528,512]{1,0:T(8,128)(2,1)S(1)}, u32[]{:S(2)}, u32[]{:S(2)}) %collective-permute-start) | collective-permute-done | bytes 540704 | tf_op jit(solution)/shard_map/ppermute | solution.py:329
  16.6 0.5 collective-permute-start.6
  17.1 0.0 collective-permute-done.4.rest_3_
  17.1 0.5 collective-permute-start.1
  17.6 1.4 %shard_map.93 = (bf16[512,512]{1,0:T(8,128)(2,1)S(1)}, bf16[512,512]{1,0:T(8,128)(2,1)S(1)}, bf16[4,512,128]{2,1,0:T(8,128)(2,1)S(1)}) custom-call(bf16[512,512]{1,0:T(8,128)(2,1)S(1)} %get-tuple-element.20.source.states, f32[1,512]{1,0:T(1,128)S(1)} %get-tuple-element.23.gain, bf16[128,1536]{1,0:T(8,128)(2,1)S(1)} %shard_map.92.rest_0_, ...), custom_call_target="tpu_custom_call" | custom-call | flops 2147483648 | bytes 4194304 | tf_op jit(solution)/shard_map/pallas_call | solution.py:302
  19.0 0.0 copy-start
  19.0 0.0 copy-start.1
  19.0 1.4 %shard_map.94 = (bf16[512,512]{1,0:T(8,128)(2,1)S(1)}, bf16[512,512]{1,0:T(8,128)(2,1)S(1)}, bf16[4,512,128]{2,1,0:T(8,128)(2,1)S(1)}) custom-call(bf16[528,512]{1,0:T(8,128)(2,1)S(1)} %collective-permute-done.source.table, f32[1,512]{1,0:T(1,128)S(1)} %get-tuple-element.23.gain, bf16[128,1536]{1,0:T(8,128)(2,1)S(1)} %shard_map.92.rest_0_, ...), custom_call_target="tpu_custom_call" | custom-call | flops 2147483648 | bytes 4194304 | tf_op jit(solution)/shard_map/pallas_call | solution.py:302
  20.5 0.0 collective-permute-done.5.rest_1_
  20.5 0.1 collective-permute-start.8
  20.6 5.5 %collective-permute-done.9.rest_6_ = bf16[128,2048]{1,0:T(8,128)(2,1)S(1)} collective-permute-done((bf16[128,2048]{1,0:T(8,128)(2,1)}, bf16[128,2048]{1,0:T(8,128)(2,1)S(1)}, u32[]{:S(2)}, u32[]{:S(2)}) %collective-permute-start.9) | collective-permute-done | bytes 524320 | tf_op jit(solution)/shard_map/ppermute | solution.py:329
  26.1 1.5 %collective-permute-start.14 = (bf16[512,512]{1,0:T(8,128)(2,1)S(1)}, bf16[512,512]{1,0:T(8,128)(2,1)S(1)}, u32[]{:S(2)}, u32[]{:S(2)}) collective-permute-start(bf16[512,512]{1,0:T(8,128)(2,1)S(1)} %copy-done.1), channel_id=1, source_target_pairs={{0,2},{1,3},{2,0},{3,1},{4,6},{5,7},{6,4},{7,5},{8,10},{9,11},{10,... | collective-permute-start | bytes 1572872 | tf_op jit(solution)/shard_map/ppermute | solution.py:329
  27.6 10.6 %collective-permute-done.11.far = bf16[512,512]{1,0:T(8,128)(2,1)S(1)} collective-permute-done((bf16[512,512]{1,0:T(8,128)(2,1)S(1)}, bf16[512,512]{1,0:T(8,128)(2,1)S(1)}, u32[]{:S(2)}, u32[]{:S(2)}) %collective-permute-start.11) | collective-permute-done | bytes 524320 | tf_op jit(solution)/shard_map/ppermute | solution.py:329
  38.2 5.8 %shard_map.97 = bf16[512,512]{1,0:T(8,128)(2,1)S(1)} custom-call(bf16[528,512]{1,0:T(8,128)(2,1)S(1)} %collective-permute-done.source.table, bf16[512,512]{1,0:T(8,128)(2,1)S(1)} %collective-permute-done.11.far, bf16[512,512]{1,0:T(8,128)(2,1)S(1)} %get-tuple-element.32.queries, bf16[512,512]{1,0:T(8,128)(2,1)S(1)} %get-tuple-element.25.k_keep, ...), custom_call_target="tpu_custom_call" | custom-call | flops 4294967296 | bytes 4194304 | tf_op jit(solution)/shard_map/pallas_call | solution.py:302
  44.0 0.6 collective-permute-start.7
  44.6 0.0 collective-permute-done.1.far
  44.6 5.8 %shard_map.95.attended = bf16[512,512]{1,0:T(8,128)(2,1)S(1)} custom-call(bf16[16,512]{1,0:T(8,128)(2,1)S(1)} %get-tuple-element.21.table, bf16[528,512]{1,0:T(8,128)(2,1)S(1)} %collective-permute-done.1.far, bf16[512,512]{1,0:T(8,128)(2,1)S(1)} %get-tuple-element.24.queries, bf16[512,512]{1,0:T(8,128)(2,1)S(1)} %get-tuple-element.25.k_keep, ...), custom_call_target="tpu_custom_call" | custom-call | flops 4294967296 | bytes 4194304 | tf_op jit(solution)/shard_map/pallas_call | solution.py:302
  50.5 0.2 collective-permute-start.13
  50.6 0.4 collective-permute-start.15
  51.0 2.7 %shard_map.96 = (bf16[512,512]{1,0:T(8,128)(2,1)S(1)}, bf16[512,2048]{1,0:T(8,128)(2,1)S(1)}) custom-call(bf16[512,512]{1,0:T(8,128)(2,1)S(1)} %get-tuple-element.20.source.states, bf16[512,512]{1,0:T(8,128)(2,1)S(1)} %shard_map.95.attended, f32[1,512]{1,0:T(1,128)S(1)} %get-tuple-element.29.gain, bf16[128,512]{1,0:T(8,128)(2,1)S(1)} %copy-done.2, ...), custom_call_target="tpu_custom_call" | custom-call | flops 3221225472 | bytes 4194304 | tf_op jit(solution)/shard_map/pallas_call | solution.py:302
  53.7 4.8 %collective-permute-done.12.attended = bf16[512,512]{1,0:T(8,128)(2,1)S(1)} collective-permute-done((bf16[512,512]{1,0:T(8,128)(2,1)S(1)}, bf16[512,512]{1,0:T(8,128)(2,1)S(1)}, u32[]{:S(2)}, u32[]{:S(2)}) %collective-permute-start.12) | collective-permute-done | bytes 524320 | tf_op jit(solution)/shard_map/ppermute | solution.py:329
  58.5 2.6 %shard_map.98 = (bf16[512,512]{1,0:T(8,128)(2,1)S(1)}, bf16[512,2048]{1,0:T(8,128)(2,1)S(1)}) custom-call(bf16[528,512]{1,0:T(8,128)(2,1)S(1)} %get-tuple-element.22.states, bf16[512,512]{1,0:T(8,128)(2,1)S(1)} %collective-permute-done.12.attended, f32[1,512]{1,0:T(1,128)S(1)} %get-tuple-element.29.gain, bf16[128,512]{1,0:T(8,128)(2,1)S(1)} %copy-done.2, ...), custom_call_target="tpu_custom_call" | custom-call | flops 3221225472 | bytes 4194304 | tf_op jit(solution)/shard_map/pallas_call | solution.py:302
  61.2 3.1 %shard_map.99 = bf16[2,512,512]{2,1,0:T(8,128)(2,1)} custom-call(bf16[512,512]{1,0:T(8,128)(2,1)S(1)} %get-tuple-element.30.middle_k, bf16[512,2048]{1,0:T(8,128)(2,1)S(1)} %get-tuple-element.31.hidden_k, bf16[512,512]{1,0:T(8,128)(2,1)S(1)} %get-tuple-element.33.middle_g, bf16[512,2048]{1,0:T(8,128)(2,1)S(1)} %get-tuple-element.34.hidden_g, ...), custom_call_target="tpu_custom_call" | custom-call | flops 4294967296 | bytes 4194304 | tf_op jit(solution)/shard_map/pallas_call | solution.py:302
  (15 shorter events, 0.0 us)
Async XLA Ops:
  0.0 11.1 %collective-permute-start.3 = (bf16[128,1536]{1,0:T(8,128)(2,1)}, bf16[128,1536]{1,0:T(8,128)(2,1)S(1)}, u32[]{:S(2)}, u32[]{:S(2)}) collective-permute-start(bf16[128,1536]{1,0:T(8,128)(2,1)} %source.1), channel_id=1, source_target_pairs={{0,2},{1,3},{2,0},{3,1},{4,6},{5,7},{6,4},{7,5},{8,10},{9,11},{10,... | collective-permute-start | bytes 1179656 | tf_op jit(solution)/shard_map/ppermute | solution.py:329
  2.8 13.8 %collective-permute-start = (bf16[528,512]{1,0:T(8,128)(2,1)S(1)}, bf16[528,512]{1,0:T(8,128)(2,1)S(1)}, u32[]{:S(2)}, u32[]{:S(2)}) collective-permute-start(bf16[528,512]{1,0:T(8,128)(2,1)S(1)} %get-tuple-element.22.states), channel_id=1, source_target_pairs={{0,4},{4,0},{8,12},{12,8},{16,20},{20,16},{24,28},{28,24},{1,5},{5... | collective-permute-start | bytes 1622024 | tf_op jit(solution)/shard_map/ppermute | solution.py:329
  3.4 10.4 %collective-permute-start.2 = (bf16[128,1536]{1,0:T(8,128)(2,1)}, bf16[128,1536]{1,0:T(8,128)(2,1)S(1)}, u32[]{:S(2)}, u32[]{:S(2)}) collective-permute-start(bf16[128,1536]{1,0:T(8,128)(2,1)} %source.1), channel_id=1, source_target_pairs={{0,1},{1,0},{2,3},{3,2},{4,5},{5,4},{6,7},{7,6},{8,9},{9,8},{10,11... | collective-permute-start | bytes 1179656 | tf_op jit(solution)/shard_map/ppermute | solution.py:329
  11.1 6.1 %collective-permute-start.4 = (bf16[128,1536]{1,0:T(8,128)(2,1)S(1)}, bf16[128,1536]{1,0:T(8,128)(2,1)S(1)}, u32[]{:S(2)}, u32[]{:S(2)}) collective-permute-start(bf16[128,1536]{1,0:T(8,128)(2,1)S(1)} %collective-permute-done.3.rest_2_), channel_id=1, source_target_pairs={{0,1},{1,0},{2,3},{3,2},{4,5},{5,4},{6,7},{7,6},{8,9},{9,8},{10,11... | collective-permute-start | bytes 1179656 | tf_op jit(solution)/shard_map/ppermute | solution.py:329
  11.1 15.0 %collective-permute-start.9 = (bf16[128,2048]{1,0:T(8,128)(2,1)}, bf16[128,2048]{1,0:T(8,128)(2,1)S(1)}, u32[]{:S(2)}, u32[]{:S(2)}) collective-permute-start(bf16[128,2048]{1,0:T(8,128)(2,1)} %rest_4_.3), channel_id=1, source_target_pairs={{0,2},{1,3},{2,0},{3,1},{4,6},{5,7},{6,4},{7,5},{8,10},{9,11},{10,... | collective-permute-start | bytes 1572872 | tf_op jit(solution)/shard_map/ppermute | solution.py:329
  12.6 25.6 %collective-permute-start.11 = (bf16[512,512]{1,0:T(8,128)(2,1)S(1)}, bf16[512,512]{1,0:T(8,128)(2,1)S(1)}, u32[]{:S(2)}, u32[]{:S(2)}) collective-permute-start(bf16[512,512]{1,0:T(8,128)(2,1)S(1)} %get-tuple-element.20.source.states), channel_id=1, source_target_pairs={{0,24},{4,12},{8,0},{12,20},{16,8},{20,28},{24,16},{28,4},{1,25},{... | collective-permute-start | bytes 1572872 | tf_op jit(solution)/shard_map/ppermute | solution.py:329
  13.8 6.7 %collective-permute-start.5 = (bf16[128,512]{1,0:T(8,128)(2,1)}, bf16[128,512]{1,0:T(8,128)(2,1)S(1)}, u32[]{:S(2)}, u32[]{:S(2)}) collective-permute-start(bf16[128,512]{1,0:T(8,128)(2,1)} %rest_0_.4), channel_id=1, source_target_pairs={{0,1},{1,0},{2,3},{3,2},{4,5},{5,4},{6,7},{7,6},{8,9},{9,8},{10,11... | collective-permute-start | bytes 393224 | tf_op jit(solution)/shard_map/ppermute | solution.py:329
  16.6 27.4 %collective-permute-start.6 = (bf16[128,512]{1,0:T(8,128)(2,1)}, bf16[128,512]{1,0:T(8,128)(2,1)S(1)}, u32[]{:S(2)}, u32[]{:S(2)}) collective-permute-start(bf16[128,512]{1,0:T(8,128)(2,1)} %rest_0_.4), channel_id=1, source_target_pairs={{0,2},{1,3},{2,0},{3,1},{4,6},{5,7},{6,4},{7,5},{8,10},{9,11},{10,... | collective-permute-start | bytes 393224 | tf_op jit(solution)/shard_map/ppermute | solution.py:329
  17.1 27.5 %collective-permute-start.1 = (bf16[528,512]{1,0:T(8,128)(2,1)S(1)}, bf16[528,512]{1,0:T(8,128)(2,1)S(1)}, u32[]{:S(2)}, u32[]{:S(2)}) collective-permute-start(bf16[528,512]{1,0:T(8,128)(2,1)S(1)} %collective-permute-done.source.table), channel_id=1, source_target_pairs={{0,8},{4,28},{8,16},{12,4},{16,24},{20,12},{24,0},{28,20},{1,9},{5... | collective-permute-start | bytes 1622024 | tf_op jit(solution)/shard_map/ppermute | solution.py:329
  19.0 1.5 %copy-start = (bf16[128,2048]{1,0:T(8,128)(2,1)S(1)}, bf16[128,2048]{1,0:T(8,128)(2,1)}, u32[]{:S(2)}) copy-start(bf16[128,2048]{1,0:T(8,128)(2,1)} %rest_4_.3) | copy-start | bytes 1572868
  19.0 7.1 %copy-start.1 = (bf16[512,512]{1,0:T(8,128)(2,1)S(1)}, bf16[512,512]{1,0:T(8,128)(2,1)}, u32[]{:S(2)}) copy-start(bf16[512,512]{1,0:T(8,128)(2,1)} %rest_0_.5) | copy-start | bytes 1572868
  20.5 30.5 %collective-permute-start.8 = (bf16[128,2048]{1,0:T(8,128)(2,1)S(1)}, bf16[128,2048]{1,0:T(8,128)(2,1)S(1)}, u32[]{:S(2)}, u32[]{:S(2)}) collective-permute-start(bf16[128,2048]{1,0:T(8,128)(2,1)S(1)} %copy-done), channel_id=1, source_target_pairs={{0,1},{1,0},{2,3},{3,2},{4,5},{5,4},{6,7},{7,6},{8,9},{9,8},{10,11... | collective-permute-start | bytes 1572872 | tf_op jit(solution)/shard_map/ppermute | solution.py:329
  26.1 24.6 %collective-permute-start.14 = (bf16[512,512]{1,0:T(8,128)(2,1)S(1)}, bf16[512,512]{1,0:T(8,128)(2,1)S(1)}, u32[]{:S(2)}, u32[]{:S(2)}) collective-permute-start(bf16[512,512]{1,0:T(8,128)(2,1)S(1)} %copy-done.1), channel_id=1, source_target_pairs={{0,2},{1,3},{2,0},{3,1},{4,6},{5,7},{6,4},{7,5},{8,10},{9,11},{10,... | collective-permute-start | bytes 1572872 | tf_op jit(solution)/shard_map/ppermute | solution.py:329
  38.2 12.8 %collective-permute-start.10 = (bf16[128,2048]{1,0:T(8,128)(2,1)S(1)}, bf16[128,2048]{1,0:T(8,128)(2,1)S(1)}, u32[]{:S(2)}, u32[]{:S(2)}) collective-permute-start(bf16[128,2048]{1,0:T(8,128)(2,1)S(1)} %collective-permute-done.9.rest_6_), channel_id=1, source_target_pairs={{0,1},{1,0},{2,3},{3,2},{4,5},{5,4},{6,7},{7,6},{8,9},{9,8},{10,11... | collective-permute-start | bytes 1572872 | tf_op jit(solution)/shard_map/ppermute | solution.py:329
  44.0 6.4 %collective-permute-start.7 = (bf16[128,512]{1,0:T(8,128)(2,1)S(1)}, bf16[128,512]{1,0:T(8,128)(2,1)S(1)}, u32[]{:S(2)}, u32[]{:S(2)}) collective-permute-start(bf16[128,512]{1,0:T(8,128)(2,1)S(1)} %collective-permute-done.6.rest_2_), channel_id=1, source_target_pairs={{0,1},{1,0},{2,3},{3,2},{4,5},{5,4},{6,7},{7,6},{8,9},{9,8},{10,11... | collective-permute-start | bytes 393224 | tf_op jit(solution)/shard_map/ppermute | solution.py:329
  44.6 13.9 %collective-permute-start.12 = (bf16[512,512]{1,0:T(8,128)(2,1)S(1)}, bf16[512,512]{1,0:T(8,128)(2,1)S(1)}, u32[]{:S(2)}, u32[]{:S(2)}) collective-permute-start(bf16[512,512]{1,0:T(8,128)(2,1)S(1)} %shard_map.97), channel_id=1, source_target_pairs={{0,4},{4,0},{8,12},{12,8},{16,20},{20,16},{24,28},{28,24},{1,5},{5... | collective-permute-start | bytes 1572872 | tf_op jit(solution)/shard_map/ppermute | solution.py:329
  44.6 6.4 %copy-start.2 = (bf16[128,512]{1,0:T(8,128)(2,1)S(1)}, bf16[128,512]{1,0:T(8,128)(2,1)}, u32[]{:S(2)}) copy-start(bf16[128,512]{1,0:T(8,128)(2,1)} %rest_0_.4) | copy-start | bytes 393220
  50.5 10.7 %collective-permute-start.13 = (bf16[512,512]{1,0:T(8,128)(2,1)S(1)}, bf16[512,512]{1,0:T(8,128)(2,1)S(1)}, u32[]{:S(2)}, u32[]{:S(2)}) collective-permute-start(bf16[512,512]{1,0:T(8,128)(2,1)S(1)} %copy-done.1), channel_id=1, source_target_pairs={{0,1},{1,0},{2,3},{3,2},{4,5},{5,4},{6,7},{7,6},{8,9},{9,8},{10,11... | collective-permute-start | bytes 1572872 | tf_op jit(solution)/shard_map/ppermute | solution.py:329
  50.6 10.6 %collective-permute-start.15 = (bf16[512,512]{1,0:T(8,128)(2,1)S(1)}, bf16[512,512]{1,0:T(8,128)(2,1)S(1)}, u32[]{:S(2)}, u32[]{:S(2)}) collective-permute-start(bf16[512,512]{1,0:T(8,128)(2,1)S(1)} %collective-permute-done.14.rest_2_), channel_id=1, source_target_pairs={{0,1},{1,0},{2,3},{3,2},{4,5},{5,4},{6,7},{7,6},{8,9},{9,8},{10,11... | collective-permute-start | bytes 1572872 | tf_op jit(solution)/shard_map/ppermute | solution.py:329

commit v2 on v1

--- a/solution.py
+++ b/solution.py
@@ -81,7 +81,7 @@
         values[first_tile + t] = block[t * tile_rows : (t + 1) * tile_rows].T
 
 
-def attend_tiles(plan, q_ref, k_ref, v_ref, out_ref, scores, tops, tile_rows, entries):
+def attend_tiles(plan, q_ref, k_ref, v_ref, out_ref, scores, tops, sums, totals, tile_rows, entries):
     rows, width = q_ref.shape
     tiles = rows // tile_rows
     head = width // HEADS
@@ -112,12 +112,10 @@
             if j >= SURE:
                 part = jnp.where(j < plan[8, t], part, -jnp.inf)
             top = part if top is None else jnp.maximum(top, part)
-        top = jnp.max(top, axis=0, keepdims=True) * scale
-        tops[at] = jnp.broadcast_to(top, tops.shape[1:])
+        tops[at] = top
 
     def blend(t, p, at):
-        row = pl.multiple_of(t * tile_rows, tile_rows)
-        top = tops[at, 0:1]
+        top = jnp.max(tops[at], axis=0, keepdims=True) * scale
         total, outs = None, [None, None]
         for pair in range(0, entries, 2):
             weights = []
@@ -131,21 +129,25 @@
             for a in range(2):
                 h = 2 * p + a
                 values = jnp.concatenate(
-                    [
-                        v_ref[plan[t, j], h * head : (h + 1) * head, :]
-                        for j in (pair, pair + 1)
-                    ],
-                    1,
+                    [v_ref[plan[t, j], h * head : (h + 1) * head, :] for j in (pair, pair + 1)], 1
                 )
                 out = dot(values, weights[:, a * tile_rows : (a + 1) * tile_rows])
                 outs[a] = out if outs[a] is None else outs[a] + out
-        total = jnp.sum(total, axis=0, keepdims=True)
+        totals[at] = total
+        for a in range(2):
+            sums[at, a * head : (a + 1) * head] = outs[a]
+
+    def finish(t, p, at):
+        row = pl.multiple_of(t * tile_rows, tile_rows)
+        total = jnp.sum(totals[at], axis=0, keepdims=True)
         for a in range(2):
             h = 2 * p + a
-            out = outs[a] / total[:, a * tile_rows : (a + 1) * tile_rows]
+            out = sums[at, a * head : (a + 1) * head] / total[:, a * tile_rows : (a + 1) * tile_rows]
             out_ref[pl.ds(row, tile_rows), h * head : (h + 1) * head] = out.T.astype(BF16)
 
     pairs = HEADS // 2
+    totals[...] = jnp.ones(totals.shape, F32)
+    sums[...] = jnp.zeros(sums.shape, F32)
     stage(0, 0, 0)
 
     def one_tile(t, carry):
@@ -154,9 +156,12 @@
             following = jnp.minimum(t + 1, tiles - 1) if last else t
             stage(following, 0 if last else p + 1, (p + 1) % 2)
             blend(t, p, p % 2)
+            before = jnp.maximum(t - 1, 0) if p == 0 else t
+            finish(before, (p - 1) % pairs, (p + 1) % 2)
         return carry
 
-    lax.fori_loop(0, tiles, one_tile, 0)
+    lax.fori_loop(0, tiles, one_tile, 0, unroll=2 if tiles % 2 == 0 else 1)
+    finish(tiles - 1, pairs - 1, (pairs - 1) % 2)
 
 
 def slot_rows(lists, counts, place, ring, own_block):
@@ -234,7 +239,7 @@
     table, far, queries, k_keep, v_keep, k_got, v_got, gain, *rest,
     n_pieces, tile_rows, entries,
 ):
-    pieces, (attended, keys, values, normed, scores, tops, whole, plan, sems) = (
+    pieces, (attended, keys, values, normed, scores, tops, sums, totals, whole, plan, sems) = (
         rest[:n_pieces],
         rest[n_pieces:],
     )
@@ -256,44 +261,68 @@
     for copy in copies:
         copy.wait()
     attend_tiles(
-        plan, queries, keys, values, attended, scores, tops, tile_rows, entries
-    )
-
-
-def widen_body(states, attended, gain, *rest, n_pieces):
-    outs, ups = (rest[i * n_pieces : (i + 1) * n_pieces] for i in range(2))
-    middle, hidden, mid_scratch, normed = rest[2 * n_pieces :]
-    rows = attended.shape[0]
-    for r in range(0, rows, 128):
+        plan, queries, keys, values, attended, scores, tops, sums, totals, tile_rows, entries
+    )
+
+
+def middle_rows(states, attended, outs, middle):
+    for r in range(0, attended.shape[0], 128):
         at = pl.ds(r, 128)
         mid = states[at, :].astype(F32) + dot(matched(attended.at[at], outs), stacked(outs))
         middle[at, :] = mid.astype(BF16)
-        mid_scratch[at, :] = mid.astype(BF16)
-    norm_matched(mid_scratch, gain, normed, ups)
+
+
+def widen_body(states, attended, gain, *rest, n_pieces):
+    outs, ups = (rest[i * n_pieces : (i + 1) * n_pieces] for i in range(2))
+    middle, hidden, normed = rest[2 * n_pieces :]
+    middle_rows(states, attended, outs, middle)
+    norm_matched(middle, gain, normed, ups)
     for c in range(0, hidden.shape[1], 256):
         cols = slice(c, c + 256)
         hidden[:, cols] = gelu(dot(normed[...], stacked(ups, cols))).astype(BF16)
 
 
-def down_body(middle_k, hidden_k, middle_g, hidden_g, *rest, n_pieces):
-    pieces, (out, staged, sems) = rest[:n_pieces], rest[n_pieces:]
+def rest_body(states, attended, gain, middle_k, hidden_k, *rest, n_pieces, n_downs):
+    outs, ups = (rest[i * n_pieces : (i + 1) * n_pieces] for i in range(2))
+    downs = rest[2 * n_pieces : 2 * n_pieces + n_downs]
+    middle, hidden, total, normed = rest[2 * n_pieces + n_downs :]
+    starts = places(n_downs, downs[0].shape[0])
+    middle_rows(states, attended, outs, middle)
+    norm_matched(middle, gain, normed, ups)
+    chunks = hidden.shape[1] // 256
+    units = [(k, h) for k in range(n_downs) for h in range(total.shape[0])]
+    per = -(-len(units) // chunks)
+    for c in range(chunks):
+        wide = slice(c * 256, (c + 1) * 256)
+        for k, h in units[c * per : (c + 1) * per]:
+            cols = slice(h * 256, (h + 1) * 256)
+            part = dot(hidden_k[:, pl.ds(starts[k], downs[k].shape[0])], downs[k][:, cols])
+            total[h] = part + (middle_k[:, cols].astype(F32) if k == 0 else total[h])
+        hidden[:, wide] = gelu(dot(normed[...], stacked(ups, wide))).astype(BF16)
+
+
+def last_body(total, hidden_k, middle, hidden, *rest, n_pieces):
+    downs, (out, staged, sems) = rest[:n_pieces], rest[n_pieces:]
     side = lax.axis_index("mesh") & 1
-    starts = places(n_pieces, pieces[0].shape[0])
-    rows = middle_k.shape[0]
+    rows = middle.shape[0]
+    starts = places(n_pieces, downs[0].shape[0])
+    some = hidden_k[:, pl.ds(starts[-1], downs[-1].shape[0])]
+    for h in range(total.shape[0]):
+        cols = slice(h * 256, (h + 1) * 256)
+        staged[0, :, cols] = (total[h] + dot(some, downs[-1][:, cols])).astype(BF16)
+    copies = [pltpu.make_async_copy(staged.at[0], out.at[side], sems.at[0])]
+    copies[0].start()
     step = 256
-    copies = []
-    for member, middle, hidden in ((side, middle_k, hidden_k), (1 - side, middle_g, hidden_g)):
-        for r in range(0, rows, step):
-            at = pl.ds(r, step)
-            total = middle[at, :].astype(F32)
-            for start, piece in zip(starts, pieces):
-                total = total + dot(hidden[at, pl.ds(start, piece.shape[0])], piece[...])
-            where = len(copies)
-            staged[where] = total.astype(BF16)
-            copies.append(
-                pltpu.make_async_copy(staged.at[where], out.at[member, at], sems.at[where])
-            )
-            copies[-1].start()
+    for r in range(0, rows, step):
+        at = pl.ds(r, step)
+        final = middle[at, :].astype(F32)
+        for start, piece in zip(starts, downs):
+            final = final + dot(hidden[at, pl.ds(start, piece.shape[0])], piece[...])
+        staged[1, at] = final.astype(BF16)
+        copies.append(
+            pltpu.make_async_copy(staged.at[1, at], out.at[1 - side, at], sems.at[len(copies)])
+        )
+        copies[-1].start()
     for copy in copies:
         copy.wait()
 
@@ -386,6 +415,8 @@
         block,
         pltpu.VMEM((2, entries * tile_rows, 2 * tile_rows), F32),
         pltpu.VMEM((2, 8, 2 * tile_rows), F32),
+        pltpu.VMEM((2, 2 * width // HEADS, tile_rows), F32),
+        pltpu.VMEM((2, 8, 2 * tile_rows), F32),
         pltpu.VMEM((EXTRA, 128), jnp.int32),
         pltpu.SMEM((EXTRA, 128), jnp.int32),
         pltpu.SemaphoreType.DMA((5,)),
@@ -422,34 +453,34 @@
         )
         return attended
 
-    def widen(states, attended):
-        return call(
-            widen_body,
-            [(rows, width), (rows, hidden)],
-            [block, block],
-            [states, attended, second, *outs, *ups],
-            [VMEM] * (3 + 2 * n),
-            3 << 30, n_pieces=n,
-        )
-
     q_keep, k_keep, v_keep = near(keep)
     q_got, k_got, v_got = near(got)
     attended_got = reach(got, far_near, q_got)
     attended_back = send("mesh", swap, attended_got)
     attended_keep = reach(table, far_late, q_keep)
-    middle_k, hidden_k = widen(keep, attended_keep)
-    middle_g, hidden_g = widen(give, attended_back)
-    step = math.gcd(rows, 256)
+    middle_k, hidden_k = call(
+        widen_body,
+        [(rows, width), (rows, hidden)],
+        [block],
+        [keep, attended_keep, second, *outs, *ups],
+        [VMEM] * (3 + 2 * n),
+        3 << 30, n_pieces=n,
+    )
+    middle_g, hidden_g, total = call(
+        rest_body,
+        [(rows, width), (rows, hidden), (width // 256, rows, 256, F32)],
+        [block],
+        [give, attended_back, second, middle_k, hidden_k, *outs, *ups, *downs[:-1]],
+        [VMEM] * (4 + 3 * n),
+        5 << 30, n_pieces=n, n_downs=n - 1,
+    )
     (result,) = call(
-        down_body,
+        last_body,
         [node_states.shape],
-        [
-            pltpu.VMEM((2 * rows // step, step, width), BF16),
-            pltpu.SemaphoreType.DMA((2 * rows // step,)),
-        ],
-        [middle_k, hidden_k, middle_g, hidden_g, *downs],
+        [pltpu.VMEM((2, rows, width), BF16), pltpu.SemaphoreType.DMA((1 + rows // 256,))],
+        [total, hidden_k, middle_g, hidden_g, *downs],
         [VMEM] * (4 + n),
-        4 << 30, space=ANY, n_pieces=n,
+        3 << 30, space=ANY, n_pieces=n,
     )
     return result
 

time: 64.6 us -> 62.9 us (0.974)
  the two profiles are of different devices: /device:TPU:28 before, /device:TPU:30 now
where the time goes in v2:
time: 62.9 us; the launch traced here: 62.7 us
  waiting for transfers between devices  33 us (52%)
  Pallas kernels  23.7 us (38%)
  starting transfers between devices  5.61 us (9%)
    ppermute x16, waiting for transfers between devices, send(): return lax.ppermute(array, axis, perm)  33 us
    pallas_call x9, Pallas kernels, call(): pl.pallas_call(functools.partial(body, **static), out_shape=[jax.ShapeDty...  23.7 us
    ppermute x16, starting transfers between devices, send(): return lax.ppermute(array, axis, perm)  5.61 us
  transfers between devices with their start and end apart: 16, of which 5 were waited for; matrix products, arithmetic and copies ran while one was open for 0% of the time, Pallas kernels for 34%

profile of v2, /device:TPU:30, one launch (start us, length us, event | category | flops | bytes accessed | tf_op | source)
XLA Modules:
  0.0 62.7 jit_solution(619005756685127167)
XLA Ops:
  0.0 0.5 collective-permute-start.3
  0.5 1.3 %shard_map.91 = (bf16[528,512]{1,0:T(8,128)(2,1)S(1)}, bf16[512,512]{1,0:T(8,128)(2,1)S(1)}, bf16[16,512]{1,0:T(8,128)(2,1)S(1)}, f32[1,512]{1,0:T(1,128)S(1)}, f32[1,512]{1,0:T(1,128)S(1)}) custom-call(bf16[2,512,512]{2,1,0:T(8,128)(2,1)} %states.1, s32[4,8]{1,0:T(4,128)} %lists_in.1, s32[1,4]{1,0:T(1,128)} %bitcast.5, f32[1,512]{1,0:T(1,128)} %bitcast.3, ...), custom_call_target="tpu_custom_call" | custom-call | flops 1048576 | tf_op jit(solution)/shard_map/pallas_call | solution.py:331
  1.8 0.6 collective-permute-start
  2.4 8.7 %collective-permute-done.3.rest_2_ = bf16[128,1536]{1,0:T(8,128)(2,1)S(1)} collective-permute-done((bf16[128,1536]{1,0:T(8,128)(2,1)}, bf16[128,1536]{1,0:T(8,128)(2,1)S(1)}, u32[]{:S(2)}, u32[]{:S(2)}) %collective-permute-start.3) | collective-permute-done | bytes 393248 | tf_op jit(solution)/shard_map/ppermute | solution.py:358
  11.1 0.2 collective-permute-start.1
  11.3 0.5 collective-permute-start.11
  11.8 1.0 %shard_map.92.rest_0_ = bf16[128,1536]{1,0:T(8,128)(2,1)S(1)} custom-call(bf16[128,1536]{1,0:T(8,128)(2,1)} %source.1), custom_call_target="tpu_custom_call" | custom-call | flops 1048576 | tf_op jit(solution)/shard_map/pallas_call | solution.py:331
  12.8 0.0 collective-permute-done.2.rest_1_
  12.8 0.1 collective-permute-start.7
  12.9 2.7 %collective-permute-done.source.table = bf16[528,512]{1,0:T(8,128)(2,1)S(1)} collective-permute-done((bf16[528,512]{1,0:T(8,128)(2,1)S(1)}, bf16[528,512]{1,0:T(8,128)(2,1)S(1)}, u32[]{:S(2)}, u32[]{:S(2)}) %collective-permute-start) | collective-permute-done | bytes 540704 | tf_op jit(solution)/shard_map/ppermute | solution.py:358
  15.6 1.5 %collective-permute-start.8 = (bf16[128,512]{1,0:T(8,128)(2,1)}, bf16[128,512]{1,0:T(8,128)(2,1)S(1)}, u32[]{:S(2)}, u32[]{:S(2)}) collective-permute-start(bf16[128,512]{1,0:T(8,128)(2,1)} %rest_0_.4), channel_id=1, source_target_pairs={{0,2},{1,3},{2,0},{3,1},{4,6},{5,7},{6,4},{7,5},{8,10},{9,11},{10,... | collective-permute-start | bytes 393224 | tf_op jit(solution)/shard_map/ppermute | solution.py:358
  17.1 0.5 collective-permute-start.6
  17.6 1.4 %shard_map.93 = (bf16[512,512]{1,0:T(8,128)(2,1)S(1)}, bf16[512,512]{1,0:T(8,128)(2,1)S(1)}, bf16[4,512,128]{2,1,0:T(8,128)(2,1)S(1)}) custom-call(bf16[528,512]{1,0:T(8,128)(2,1)S(1)} %collective-permute-done.source.table, f32[1,512]{1,0:T(1,128)S(1)} %get-tuple-element.23.gain, bf16[128,1536]{1,0:T(8,128)(2,1)S(1)} %shard_map.92.rest_0_, ...), custom_call_target="tpu_custom_call" | custom-call | flops 2147483648 | bytes 4194304 | tf_op jit(solution)/shard_map/pallas_call | solution.py:331
  19.0 0.0 copy-start
  19.0 0.0 copy-start.1
  19.0 1.4 %shard_map.94 = (bf16[512,512]{1,0:T(8,128)(2,1)S(1)}, bf16[512,512]{1,0:T(8,128)(2,1)S(1)}, bf16[4,512,128]{2,1,0:T(8,128)(2,1)S(1)}) custom-call(bf16[512,512]{1,0:T(8,128)(2,1)S(1)} %get-tuple-element.22.source.states, f32[1,512]{1,0:T(1,128)S(1)} %get-tuple-element.23.gain, bf16[128,1536]{1,0:T(8,128)(2,1)S(1)} %shard_map.92.rest_0_, ...), custom_call_target="tpu_custom_call" | custom-call | flops 2147483648 | bytes 4194304 | tf_op jit(solution)/shard_map/pallas_call | solution.py:331
  20.5 0.1 collective-permute-start.10
  20.6 7.8 %collective-permute-done.8.rest_2_ = bf16[128,512]{1,0:T(8,128)(2,1)S(1)} collective-permute-done((bf16[128,512]{1,0:T(8,128)(2,1)}, bf16[128,512]{1,0:T(8,128)(2,1)S(1)}, u32[]{:S(2)}, u32[]{:S(2)}) %collective-permute-start.8) | collective-permute-done | bytes 131104 | tf_op jit(solution)/shard_map/ppermute | solution.py:358
  28.4 0.5 collective-permute-start.14
  29.0 8.0 %collective-permute-done.1.far = bf16[512,512]{1,0:T(8,128)(2,1)S(1)} collective-permute-done((bf16[512,512]{1,0:T(8,128)(2,1)S(1)}, bf16[512,512]{1,0:T(8,128)(2,1)S(1)}, u32[]{:S(2)}, u32[]{:S(2)}) %collective-permute-start.1) | collective-permute-done | bytes 524320 | tf_op jit(solution)/shard_map/ppermute | solution.py:358
  37.0 0.0 collective-permute-start.9
  37.0 0.5 collective-permute-start.12
  37.5 5.1 %shard_map.95 = bf16[512,512]{1,0:T(8,128)(2,1)S(1)} custom-call(bf16[528,512]{1,0:T(8,128)(2,1)S(1)} %collective-permute-done.source.table, bf16[512,512]{1,0:T(8,128)(2,1)S(1)} %collective-permute-done.1.far, bf16[512,512]{1,0:T(8,128)(2,1)S(1)} %get-tuple-element.24.queries, bf16[512,512]{1,0:T(8,128)(2,1)S(1)} %get-tuple-element.25.k_keep, ...), custom_call_target="tpu_custom_call" | custom-call | flops 4294967296 | bytes 4194304 | tf_op jit(solution)/shard_map/pallas_call | solution.py:331
  42.7 0.1 collective-permute-start.13
  42.8 0.1 collective-permute-start.5
  42.8 0.0 copy-start.2
  42.9 5.3 %shard_map.96.attended = bf16[512,512]{1,0:T(8,128)(2,1)S(1)} custom-call(bf16[16,512]{1,0:T(8,128)(2,1)S(1)} %get-tuple-element.30.table, bf16[528,512]{1,0:T(8,128)(2,1)S(1)} %collective-permute-done.6.far, bf16[512,512]{1,0:T(8,128)(2,1)S(1)} %get-tuple-element.31.queries, bf16[512,512]{1,0:T(8,128)(2,1)S(1)} %get-tuple-element.25.k_keep, ...), custom_call_target="tpu_custom_call" | custom-call | flops 4294967296 | bytes 4194304 | tf_op jit(solution)/shard_map/pallas_call | solution.py:331
  48.2 0.5 collective-permute-start.15
  48.7 2.6 %shard_map.97 = (bf16[512,512]{1,0:T(8,128)(2,1)S(1)}, bf16[512,2048]{1,0:T(8,128)(2,1)S(1)}) custom-call(bf16[512,512]{1,0:T(8,128)(2,1)S(1)} %get-tuple-element.22.source.states, bf16[512,512]{1,0:T(8,128)(2,1)S(1)} %shard_map.96.attended, f32[1,512]{1,0:T(1,128)S(1)} %get-tuple-element.29.gain, bf16[128,512]{1,0:T(8,128)(2,1)S(1)} %copy-done.2, ...), custom_call_target="tpu_custom_call" | custom-call | flops 3221225472 | bytes 4194304 | tf_op jit(solution)/shard_map/pallas_call | solution.py:331
  51.4 5.7 %collective-permute-done.5.attended = bf16[512,512]{1,0:T(8,128)(2,1)S(1)} collective-permute-done((bf16[512,512]{1,0:T(8,128)(2,1)S(1)}, bf16[512,512]{1,0:T(8,128)(2,1)S(1)}, u32[]{:S(2)}, u32[]{:S(2)}) %collective-permute-start.5) | collective-permute-done | bytes 524320 | tf_op jit(solution)/shard_map/ppermute | solution.py:358
  57.1 3.1 %shard_map.98 = (bf16[512,512]{1,0:T(8,128)(2,1)S(1)}, bf16[512,2048]{1,0:T(8,128)(2,1)S(1)}, f32[2,512,256]{2,1,0:T(8,128)S(1)}) custom-call(bf16[528,512]{1,0:T(8,128)(2,1)S(1)} %get-tuple-element.21.states, bf16[512,512]{1,0:T(8,128)(2,1)S(1)} %collective-permute-done.5.attended, f32[1,512]{1,0:T(1,128)S(1)} %get-tuple-element.29.gain, ...), custom_call_target="tpu_custom_call" | custom-call | flops 5368709120 | bytes 4194304 | tf_op jit(solution)/shard_map/pallas_call | solution.py:331
  60.2 2.3 %shard_map.99 = bf16[2,512,512]{2,1,0:T(8,128)(2,1)} custom-call(f32[2,512,256]{2,1,0:T(8,128)S(1)} %get-tuple-element.34.total, bf16[512,2048]{1,0:T(8,128)(2,1)S(1)} %get-tuple-element.33.hidden_k, bf16[512,512]{1,0:T(8,128)(2,1)S(1)} %get-tuple-element.35.middle, bf16[512,2048]{1,0:T(8,128)(2,1)S(1)} %get-tuple-element.36.hidden, ...), custom_call_target="tpu_custom_call" | custom-call | flops 3221225472 | bytes 4194304 | tf_op jit(solution)/shard_map/pallas_call | solution.py:331
  (15 shorter events, 0.0 us)
Async XLA Ops:
  0.0 11.1 %collective-permute-start.3 = (bf16[128,1536]{1,0:T(8,128)(2,1)}, bf16[128,1536]{1,0:T(8,128)(2,1)S(1)}, u32[]{:S(2)}, u32[]{:S(2)}) collective-permute-start(bf16[128,1536]{1,0:T(8,128)(2,1)} %source.1), channel_id=1, source_target_pairs={{0,2},{1,3},{2,0},{3,1},{4,6},{5,7},{6,4},{7,5},{8,10},{9,11},{10,... | collective-permute-start | bytes 1179656 | tf_op jit(solution)/shard_map/ppermute | solution.py:358
  1.8 13.8 %collective-permute-start = (bf16[528,512]{1,0:T(8,128)(2,1)S(1)}, bf16[528,512]{1,0:T(8,128)(2,1)S(1)}, u32[]{:S(2)}, u32[]{:S(2)}) collective-permute-start(bf16[528,512]{1,0:T(8,128)(2,1)S(1)} %get-tuple-element.21.states), channel_id=1, source_target_pairs={{0,4},{4,0},{8,12},{12,8},{16,20},{20,16},{24,28},{28,24},{1,5},{5... | collective-permute-start | bytes 1622024 | tf_op jit(solution)/shard_map/ppermute | solution.py:358
  2.4 10.4 %collective-permute-start.2 = (bf16[128,1536]{1,0:T(8,128)(2,1)}, bf16[128,1536]{1,0:T(8,128)(2,1)S(1)}, u32[]{:S(2)}, u32[]{:S(2)}) collective-permute-start(bf16[128,1536]{1,0:T(8,128)(2,1)} %source.1), channel_id=1, source_target_pairs={{0,1},{1,0},{2,3},{3,2},{4,5},{5,4},{6,7},{7,6},{8,9},{9,8},{10,11... | collective-permute-start | bytes 1179656 | tf_op jit(solution)/shard_map/ppermute | solution.py:358
  11.1 6.1 %collective-permute-start.4 = (bf16[128,1536]{1,0:T(8,128)(2,1)S(1)}, bf16[128,1536]{1,0:T(8,128)(2,1)S(1)}, u32[]{:S(2)}, u32[]{:S(2)}) collective-permute-start(bf16[128,1536]{1,0:T(8,128)(2,1)S(1)} %collective-permute-done.3.rest_2_), channel_id=1, source_target_pairs={{0,1},{1,0},{2,3},{3,2},{4,5},{5,4},{6,7},{7,6},{8,9},{9,8},{10,11... | collective-permute-start | bytes 1179656 | tf_op jit(solution)/shard_map/ppermute | solution.py:358
  11.1 25.9 %collective-permute-start.1 = (bf16[512,512]{1,0:T(8,128)(2,1)S(1)}, bf16[512,512]{1,0:T(8,128)(2,1)S(1)}, u32[]{:S(2)}, u32[]{:S(2)}) collective-permute-start(bf16[512,512]{1,0:T(8,128)(2,1)S(1)} %get-tuple-element.22.source.states), channel_id=1, source_target_pairs={{0,24},{4,12},{8,0},{12,20},{16,8},{20,28},{24,16},{28,4},{1,25},{... | collective-permute-start | bytes 1572872 | tf_op jit(solution)/shard_map/ppermute | solution.py:358
  11.3 25.7 %collective-permute-start.11 = (bf16[128,2048]{1,0:T(8,128)(2,1)}, bf16[128,2048]{1,0:T(8,128)(2,1)S(1)}, u32[]{:S(2)}, u32[]{:S(2)}) collective-permute-start(bf16[128,2048]{1,0:T(8,128)(2,1)} %rest_4_.3), channel_id=1, source_target_pairs={{0,2},{1,3},{2,0},{3,1},{4,6},{5,7},{6,4},{7,5},{8,10},{9,11},{10,... | collective-permute-start | bytes 1572872 | tf_op jit(solution)/shard_map/ppermute | solution.py:358
  12.8 7.6 %collective-permute-start.7 = (bf16[128,512]{1,0:T(8,128)(2,1)}, bf16[128,512]{1,0:T(8,128)(2,1)S(1)}, u32[]{:S(2)}, u32[]{:S(2)}) collective-permute-start(bf16[128,512]{1,0:T(8,128)(2,1)} %rest_0_.4), channel_id=1, source_target_pairs={{0,1},{1,0},{2,3},{3,2},{4,5},{5,4},{6,7},{7,6},{8,9},{9,8},{10,11... | collective-permute-start | bytes 393224 | tf_op jit(solution)/shard_map/ppermute | solution.py:358
  15.6 12.8 %collective-permute-start.8 = (bf16[128,512]{1,0:T(8,128)(2,1)}, bf16[128,512]{1,0:T(8,128)(2,1)S(1)}, u32[]{:S(2)}, u32[]{:S(2)}) collective-permute-start(bf16[128,512]{1,0:T(8,128)(2,1)} %rest_0_.4), channel_id=1, source_target_pairs={{0,2},{1,3},{2,0},{3,1},{4,6},{5,7},{6,4},{7,5},{8,10},{9,11},{10,... | collective-permute-start | bytes 393224 | tf_op jit(solution)/shard_map/ppermute | solution.py:358
  17.1 25.6 %collective-permute-start.6 = (bf16[528,512]{1,0:T(8,128)(2,1)S(1)}, bf16[528,512]{1,0:T(8,128)(2,1)S(1)}, u32[]{:S(2)}, u32[]{:S(2)}) collective-permute-start(bf16[528,512]{1,0:T(8,128)(2,1)S(1)} %collective-permute-done.source.table), channel_id=1, source_target_pairs={{0,8},{4,28},{8,16},{12,4},{16,24},{20,12},{24,0},{28,20},{1,9},{5... | collective-permute-start | bytes 1622024 | tf_op jit(solution)/shard_map/ppermute | solution.py:358
  19.0 1.5 %copy-start = (bf16[128,2048]{1,0:T(8,128)(2,1)S(1)}, bf16[128,2048]{1,0:T(8,128)(2,1)}, u32[]{:S(2)}) copy-start(bf16[128,2048]{1,0:T(8,128)(2,1)} %rest_4_.3) | copy-start | bytes 1572868
  19.0 9.4 %copy-start.1 = (bf16[512,512]{1,0:T(8,128)(2,1)S(1)}, bf16[512,512]{1,0:T(8,128)(2,1)}, u32[]{:S(2)}) copy-start(bf16[512,512]{1,0:T(8,128)(2,1)} %rest_0_.5) | copy-start | bytes 1572868
  20.5 28.2 %collective-permute-start.10 = (bf16[128,2048]{1,0:T(8,128)(2,1)S(1)}, bf16[128,2048]{1,0:T(8,128)(2,1)S(1)}, u32[]{:S(2)}, u32[]{:S(2)}) collective-permute-start(bf16[128,2048]{1,0:T(8,128)(2,1)S(1)} %copy-done), channel_id=1, source_target_pairs={{0,1},{1,0},{2,3},{3,2},{4,5},{5,4},{6,7},{7,6},{8,9},{9,8},{10,11... | collective-permute-start | bytes 1572872 | tf_op jit(solution)/shard_map/ppermute | solution.py:358
  28.4 19.8 %collective-permute-start.14 = (bf16[512,512]{1,0:T(8,128)(2,1)S(1)}, bf16[512,512]{1,0:T(8,128)(2,1)S(1)}, u32[]{:S(2)}, u32[]{:S(2)}) collective-permute-start(bf16[512,512]{1,0:T(8,128)(2,1)S(1)} %copy-done.1), channel_id=1, source_target_pairs={{0,2},{1,3},{2,0},{3,1},{4,6},{5,7},{6,4},{7,5},{8,10},{9,11},{10,... | collective-permute-start | bytes 1572872 | tf_op jit(solution)/shard_map/ppermute | solution.py:358
  37.0 5.7 %collective-permute-start.9 = (bf16[128,512]{1,0:T(8,128)(2,1)S(1)}, bf16[128,512]{1,0:T(8,128)(2,1)S(1)}, u32[]{:S(2)}, u32[]{:S(2)}) collective-permute-start(bf16[128,512]{1,0:T(8,128)(2,1)S(1)} %collective-permute-done.8.rest_2_), channel_id=1, source_target_pairs={{0,1},{1,0},{2,3},{3,2},{4,5},{5,4},{6,7},{7,6},{8,9},{9,8},{10,11... | collective-permute-start | bytes 393224 | tf_op jit(solution)/shard_map/ppermute | solution.py:358
  37.0 11.7 %collective-permute-start.12 = (bf16[128,2048]{1,0:T(8,128)(2,1)S(1)}, bf16[128,2048]{1,0:T(8,128)(2,1)S(1)}, u32[]{:S(2)}, u32[]{:S(2)}) collective-permute-start(bf16[128,2048]{1,0:T(8,128)(2,1)S(1)} %collective-permute-done.11.rest_6_), channel_id=1, source_target_pairs={{0,1},{1,0},{2,3},{3,2},{4,5},{5,4},{6,7},{7,6},{8,9},{9,8},{10,11... | collective-permute-start | bytes 1572872 | tf_op jit(solution)/shard_map/ppermute | solution.py:358
  42.7 8.7 %collective-permute-start.13 = (bf16[512,512]{1,0:T(8,128)(2,1)S(1)}, bf16[512,512]{1,0:T(8,128)(2,1)S(1)}, u32[]{:S(2)}, u32[]{:S(2)}) collective-permute-start(bf16[512,512]{1,0:T(8,128)(2,1)S(1)} %copy-done.1), channel_id=1, source_target_pairs={{0,1},{1,0},{2,3},{3,2},{4,5},{5,4},{6,7},{7,6},{8,9},{9,8},{10,11... | collective-permute-start | bytes 1572872 | tf_op jit(solution)/shard_map/ppermute | solution.py:358
  42.8 14.3 %collective-permute-start.5 = (bf16[512,512]{1,0:T(8,128)(2,1)S(1)}, bf16[512,512]{1,0:T(8,128)(2,1)S(1)}, u32[]{:S(2)}, u32[]{:S(2)}) collective-permute-start(bf16[512,512]{1,0:T(8,128)(2,1)S(1)} %shard_map.95), channel_id=1, source_target_pairs={{0,4},{4,0},{8,12},{12,8},{16,20},{20,16},{24,28},{28,24},{1,5},{5... | collective-permute-start | bytes 1572872 | tf_op jit(solution)/shard_map/ppermute | solution.py:358
  42.8 5.8 %copy-start.2 = (bf16[128,512]{1,0:T(8,128)(2,1)S(1)}, bf16[128,512]{1,0:T(8,128)(2,1)}, u32[]{:S(2)}) copy-start(bf16[128,512]{1,0:T(8,128)(2,1)} %rest_0_.4) | copy-start | bytes 393220
  48.2 12.0 %collective-permute-start.15 = (bf16[512,512]{1,0:T(8,128)(2,1)S(1)}, bf16[512,512]{1,0:T(8,128)(2,1)S(1)}, u32[]{:S(2)}, u32[]{:S(2)}) collective-permute-start(bf16[512,512]{1,0:T(8,128)(2,1)S(1)} %collective-permute-done.14.rest_10_.rest_2_), channel_id=1, source_target_pairs={{0,1},{1,0},{2,3},{3,2},{4,5},{5,4},{6,7},{7,6},{8,9},{9,8},{10,11... | collective-permute-start | bytes 1572872 | tf_op jit(solution)/shard_map/ppermute | solution.py:358

commit v3 on v2

--- a/solution.py
+++ b/solution.py
@@ -56,11 +56,11 @@
     )
 
 
-def norm_matched(source, gain, target, pieces):
+def norm_matched(source, gain, target, pieces, span=None):
     block = pieces[0].shape[0]
     me = lax.axis_index("member")
     step = 128
-    for r in range(0, target.shape[0], step):
+    for r in range(*(span or (0, target.shape[0])), step):
         normed = norm_rows(source[r : r + step, :], gain[...])
         for k in range(len(pieces)):
             target[r : r + step, pl.ds(pl.multiple_of((me ^ k) * block, block), block)] = normed[
@@ -68,17 +68,22 @@
             ]
 
 
-def project(normed, pieces, queries, keys, values, key_row, first_tile, tile_rows):
+def norm_project(source, gain, normed, pieces, queries, keys, values, third, tile_rows):
     count, width = normed.shape
-    rows = normed[...]
-    if queries is not None:
-        queries[...] = dot(rows, stacked(pieces, slice(0, width))).astype(BF16)
-    keys[pl.ds(key_row, count), :] = dot(
-        rows, stacked(pieces, slice(width, 2 * width))
-    ).astype(BF16)
-    block = dot(rows, stacked(pieces, slice(2 * width, 3 * width))).astype(BF16)
-    for t in range(count // tile_rows):
-        values[first_tile + t] = block[t * tile_rows : (t + 1) * tile_rows].T
+    step = count // 2
+    for r in range(0, count, step):
+        norm_matched(source, gain, normed, pieces, (r, r + step))
+        at = pl.ds(r, step)
+        rows = normed[at, :]
+        if queries is not None:
+            queries[at, :] = dot(rows, stacked(pieces, slice(0, width))).astype(BF16)
+        keys[pl.ds(third * count + r, step), :] = dot(
+            rows, stacked(pieces, slice(width, 2 * width))
+        ).astype(BF16)
+        block = dot(rows, stacked(pieces, slice(2 * width, 3 * width))).astype(BF16)
+        for t in range(step // tile_rows):
+            slot = (third * count + r) // tile_rows + t
+            values[slot] = block[t * tile_rows : (t + 1) * tile_rows].T
 
 
 def attend_tiles(plan, q_ref, k_ref, v_ref, out_ref, scores, tops, sums, totals, tile_rows, entries):
@@ -231,8 +236,7 @@
 
 def near_body(source, gain, *rest, n_pieces, tile_rows):
     pieces, (queries, keys, values, normed) = rest[:n_pieces], rest[n_pieces:]
-    norm_matched(source, gain, normed, pieces)
-    project(normed, pieces, queries, keys, values, 0, 0, tile_rows)
+    norm_project(source, gain, normed, pieces, queries, keys, values, 0, tile_rows)
 
 
 def reach_body(
@@ -256,8 +260,7 @@
     ]
     for copy in copies:
         copy.start()
-    norm_matched(far, gain, normed, pieces)
-    project(normed, pieces, None, keys, values, 2 * rows, 2 * tiles, tile_rows)
+    norm_project(far, gain, normed, pieces, None, keys, values, 2, tile_rows)
     for copy in copies:
         copy.wait()
     attend_tiles(
@@ -265,64 +268,103 @@
     )
 
 
-def middle_rows(states, attended, outs, middle):
-    for r in range(0, attended.shape[0], 128):
+def middle_rows(states, attended, outs, middle, span=None):
+    for r in range(*(span or (0, attended.shape[0])), 128):
         at = pl.ds(r, 128)
         mid = states[at, :].astype(F32) + dot(matched(attended.at[at], outs), stacked(outs))
         middle[at, :] = mid.astype(BF16)
 
 
-def widen_body(states, attended, gain, *rest, n_pieces):
+def widen_chunks(normed, middle, ups, downs, hidden, total, early, aside=()):
+    block = downs[0].shape[0]
+    step = 256
+    starts = places(hidden.shape[1] // block, block)
+    aside = list(aside)
+    behind = None
+
+    def follow():
+        if behind is not None:
+            k, i, values = behind
+            for h in range(total.shape[0]):
+                cols = slice(h * 256, (h + 1) * 256)
+                part = dot(values, downs[k][i : i + step, cols])
+                base = middle[:, cols].astype(F32) if k == i == 0 else total[h]
+                total[h] = base + part
+
+    for k, start in enumerate(starts):
+        for i in range(0, block, step):
+            cols = pl.ds(pl.multiple_of(start + i, step), step)
+            wide = dot(normed[...], stacked(ups, cols))
+            follow()
+            behind = None
+            if aside and k >= early:
+                aside.pop(0)()
+            values = gelu(wide).astype(BF16)
+            hidden[:, cols] = values
+            if k < early:
+                behind = (k, i, values)
+    follow()
+    for unit in aside:
+        unit()
+
+
+def widen_body(states, attended, gain, *rest, n_pieces, early):
     outs, ups = (rest[i * n_pieces : (i + 1) * n_pieces] for i in range(2))
-    middle, hidden, normed = rest[2 * n_pieces :]
+    downs = rest[2 * n_pieces : 2 * n_pieces + early]
+    hidden, total, middle, normed = rest[2 * n_pieces + early :]
     middle_rows(states, attended, outs, middle)
     norm_matched(middle, gain, normed, ups)
-    for c in range(0, hidden.shape[1], 256):
-        cols = slice(c, c + 256)
-        hidden[:, cols] = gelu(dot(normed[...], stacked(ups, cols))).astype(BF16)
-
-
-def rest_body(states, attended, gain, middle_k, hidden_k, *rest, n_pieces, n_downs):
+    widen_chunks(normed, middle, ups, downs, hidden, total, early)
+
+
+def rest_body(states, attended, gain, hidden_k, total_in, *rest, n_pieces, early):
     outs, ups = (rest[i * n_pieces : (i + 1) * n_pieces] for i in range(2))
-    downs = rest[2 * n_pieces : 2 * n_pieces + n_downs]
-    middle, hidden, total, normed = rest[2 * n_pieces + n_downs :]
-    starts = places(n_downs, downs[0].shape[0])
-    middle_rows(states, attended, outs, middle)
-    norm_matched(middle, gain, normed, ups)
-    chunks = hidden.shape[1] // 256
-    units = [(k, h) for k in range(n_downs) for h in range(total.shape[0])]
-    per = -(-len(units) // chunks)
-    for c in range(chunks):
-        wide = slice(c * 256, (c + 1) * 256)
-        for k, h in units[c * per : (c + 1) * per]:
-            cols = slice(h * 256, (h + 1) * 256)
-            part = dot(hidden_k[:, pl.ds(starts[k], downs[k].shape[0])], downs[k][:, cols])
-            total[h] = part + (middle_k[:, cols].astype(F32) if k == 0 else total[h])
-        hidden[:, wide] = gelu(dot(normed[...], stacked(ups, wide))).astype(BF16)
-
-
-def last_body(total, hidden_k, middle, hidden, *rest, n_pieces):
-    downs, (out, staged, sems) = rest[:n_pieces], rest[n_pieces:]
+    downs = rest[2 * n_pieces : 3 * n_pieces - 1]
+    hidden, total_k, total_g, middle, normed = rest[3 * n_pieces - 1 :]
+    block = downs[0].shape[0]
+    starts = places(n_pieces, block)
+
+    def unit(k, h):
+        def run():
+            part = dot(hidden_k[:, pl.ds(starts[k], block)], downs[k][:, h * 256 : (h + 1) * 256])
+            total_k[h] = part + (total_in[h] if k == early else total_k[h])
+
+        return run
+
+    units = [unit(k, h) for k in range(early, n_pieces - 1) for h in range(total_k.shape[0])]
+    for r in range(0, middle.shape[0], 128):
+        middle_rows(states, attended, outs, middle, (r, r + 128))
+        if r % 256 == 0 and units:
+            units.pop(0)()
+        norm_matched(middle, gain, normed, ups, (r, r + 128))
+    widen_chunks(normed, middle, ups, downs, hidden, total_g, early, units)
+
+
+def last_body(total_k, total_g, hidden_k, hidden_g, *rest, n_pieces, early):
+    late = n_pieces - early
+    downs, (out, staged, sems) = rest[:late], rest[late:]
     side = lax.axis_index("mesh") & 1
-    rows = middle.shape[0]
-    starts = places(n_pieces, downs[0].shape[0])
-    some = hidden_k[:, pl.ds(starts[-1], downs[-1].shape[0])]
-    for h in range(total.shape[0]):
-        cols = slice(h * 256, (h + 1) * 256)
-        staged[0, :, cols] = (total[h] + dot(some, downs[-1][:, cols])).astype(BF16)
-    copies = [pltpu.make_async_copy(staged.at[0], out.at[side], sems.at[0])]
-    copies[0].start()
+    rows, _ = staged.shape[1:]
+    block = downs[0].shape[0]
+    starts = places(n_pieces, block)[early:]
+    copies = []
     step = 256
-    for r in range(0, rows, step):
-        at = pl.ds(r, step)
-        final = middle[at, :].astype(F32)
-        for start, piece in zip(starts, downs):
-            final = final + dot(hidden[at, pl.ds(start, piece.shape[0])], piece[...])
-        staged[1, at] = final.astype(BF16)
-        copies.append(
-            pltpu.make_async_copy(staged.at[1, at], out.at[1 - side, at], sems.at[len(copies)])
-        )
-        copies[-1].start()
+    for i, (total, hidden, member, first) in enumerate(
+        ((total_k, hidden_k, side, late - 1), (total_g, hidden_g, 1 - side, 0))
+    ):
+        for r in range(0, rows, step):
+            at = pl.ds(r, step)
+            final = None
+            for start, piece in list(zip(starts, downs))[first:]:
+                part = dot(hidden[at, pl.ds(start, block)], piece[...])
+                final = part if final is None else final + part
+            for h in range(total.shape[0]):
+                cols = slice(h * 256, (h + 1) * 256)
+                staged[i, at, cols] = (total[h, at] + final[:, cols]).astype(BF16)
+            copies.append(
+                pltpu.make_async_copy(staged.at[i, at], out.at[member, at], sems.at[len(copies)])
+            )
+            copies[-1].start()
     for copy in copies:
         copy.wait()
 
@@ -458,29 +500,31 @@
     attended_got = reach(got, far_near, q_got)
     attended_back = send("mesh", swap, attended_got)
     attended_keep = reach(table, far_late, q_keep)
-    middle_k, hidden_k = call(
+    early = n // 2
+    sums = (width // 256, rows, 256, F32)
+    hidden_k, total_k = call(
         widen_body,
-        [(rows, width), (rows, hidden)],
-        [block],
-        [keep, attended_keep, second, *outs, *ups],
-        [VMEM] * (3 + 2 * n),
-        3 << 30, n_pieces=n,
-    )
-    middle_g, hidden_g, total = call(
+        [(rows, hidden), sums],
+        [block, block],
+        [keep, attended_keep, second, *outs, *ups, *downs[:early]],
+        [VMEM] * (3 + 2 * n + early),
+        3 << 30, n_pieces=n, early=early,
+    )
+    hidden_g, total_k, total_g = call(
         rest_body,
-        [(rows, width), (rows, hidden), (width // 256, rows, 256, F32)],
-        [block],
-        [give, attended_back, second, middle_k, hidden_k, *outs, *ups, *downs[:-1]],
+        [(rows, hidden), sums, sums],
+        [block, block],
+        [give, attended_back, second, hidden_k, total_k, *outs, *ups, *downs[:-1]],
         [VMEM] * (4 + 3 * n),
-        5 << 30, n_pieces=n, n_downs=n - 1,
+        5 << 30, n_pieces=n, early=early,
     )
     (result,) = call(
         last_body,
         [node_states.shape],
-        [pltpu.VMEM((2, rows, width), BF16), pltpu.SemaphoreType.DMA((1 + rows // 256,))],
-        [total, hidden_k, middle_g, hidden_g, *downs],
-        [VMEM] * (4 + n),
-        3 << 30, space=ANY, n_pieces=n,
+        [pltpu.VMEM((2, rows, width), BF16), pltpu.SemaphoreType.DMA((2 * rows // 256,))],
+        [total_k, total_g, hidden_k, hidden_g, *downs[early:]],
+        [VMEM] * (4 + n - early),
+        2 << 30, space=ANY, n_pieces=n, early=early,
     )
     return result
 

time: 62.9 us -> 63.5 us (level)
  the two profiles are of different devices: /device:TPU:30 before, /device:TPU:28 now
where the time goes in v3:
time: 63.5 us; the launch traced here: 63.3 us
  waiting for transfers between devices  31.8 us (50%)
  Pallas kernels  23.1 us (36%)
  starting transfers between devices  8.02 us (13%)
    ppermute x16, waiting for transfers between devices, send(): return lax.ppermute(array, axis, perm)  31.8 us
    pallas_call x9, Pallas kernels, call(): pl.pallas_call(functools.partial(body, **static), out_shape=[jax.ShapeDty...  23.1 us
    ppermute x16, starting transfers between devices, send(): return lax.ppermute(array, axis, perm)  8.02 us
  transfers between devices with their start and end apart: 16, of which 4 were waited for; matrix products, arithmetic and copies ran while one was open for 0% of the time, Pallas kernels for 34%

profile of v3, /device:TPU:28, one launch (start us, length us, event | category | flops | bytes accessed | tf_op | source)
XLA Modules:
  0.0 63.3 jit_solution(8306334920888477959)
XLA Ops:
  0.0 1.5 %collective-permute-start.3 = (bf16[128,1536]{1,0:T(8,128)(2,1)}, bf16[128,1536]{1,0:T(8,128)(2,1)S(1)}, u32[]{:S(2)}, u32[]{:S(2)}) collective-permute-start(bf16[128,1536]{1,0:T(8,128)(2,1)} %source.1), channel_id=1, source_target_pairs={{0,2},{1,3},{2,0},{3,1},{4,6},{5,7},{6,4},{7,5},{8,10},{9,11},{10,... | collective-permute-start | bytes 1179656 | tf_op jit(solution)/shard_map/ppermute | solution.py:400
  1.5 1.3 %shard_map.91 = (bf16[528,512]{1,0:T(8,128)(2,1)S(1)}, bf16[512,512]{1,0:T(8,128)(2,1)S(1)}, bf16[16,512]{1,0:T(8,128)(2,1)S(1)}, f32[1,512]{1,0:T(1,128)S(1)}, f32[1,512]{1,0:T(1,128)S(1)}) custom-call(bf16[2,512,512]{2,1,0:T(8,128)(2,1)} %states.1, s32[4,8]{1,0:T(4,128)} %lists_in.1, s32[1,4]{1,0:T(1,128)} %bitcast.5, f32[1,512]{1,0:T(1,128)} %bitcast.3, ...), custom_call_target="tpu_custom_call" | custom-call | flops 1048576 | tf_op jit(solution)/shard_map/pallas_call | solution.py:373
  2.8 0.6 collective-permute-start
  3.4 7.7 %collective-permute-done.3.rest_2_ = bf16[128,1536]{1,0:T(8,128)(2,1)S(1)} collective-permute-done((bf16[128,1536]{1,0:T(8,128)(2,1)}, bf16[128,1536]{1,0:T(8,128)(2,1)S(1)}, u32[]{:S(2)}, u32[]{:S(2)}) %collective-permute-start.3) | collective-permute-done | bytes 393248 | tf_op jit(solution)/shard_map/ppermute | solution.py:400
  11.1 1.5 %collective-permute-start.8 = (bf16[128,512]{1,0:T(8,128)(2,1)}, bf16[128,512]{1,0:T(8,128)(2,1)S(1)}, u32[]{:S(2)}, u32[]{:S(2)}) collective-permute-start(bf16[128,512]{1,0:T(8,128)(2,1)} %rest_0_.3), channel_id=1, source_target_pairs={{0,2},{1,3},{2,0},{3,1},{4,6},{5,7},{6,4},{7,5},{8,10},{9,11},{10,... | collective-permute-start | bytes 393224 | tf_op jit(solution)/shard_map/ppermute | solution.py:400
  12.6 0.2 collective-permute-start.1
  12.8 4.4 %collective-permute-done.8.rest_2_ = bf16[128,512]{1,0:T(8,128)(2,1)S(1)} collective-permute-done((bf16[128,512]{1,0:T(8,128)(2,1)}, bf16[128,512]{1,0:T(8,128)(2,1)S(1)}, u32[]{:S(2)}, u32[]{:S(2)}) %collective-permute-start.8) | collective-permute-done | bytes 131104 | tf_op jit(solution)/shard_map/ppermute | solution.py:400
  17.2 1.5 %collective-permute-start.11 = (bf16[128,2048]{1,0:T(8,128)(2,1)}, bf16[128,2048]{1,0:T(8,128)(2,1)S(1)}, u32[]{:S(2)}, u32[]{:S(2)}) collective-permute-start(bf16[128,2048]{1,0:T(8,128)(2,1)} %rest_4_.3), channel_id=1, source_target_pairs={{0,2},{1,3},{2,0},{3,1},{4,6},{5,7},{6,4},{7,5},{8,10},{9,11},{10,... | collective-permute-start | bytes 1572872 | tf_op jit(solution)/shard_map/ppermute | solution.py:400
  18.7 1.0 %shard_map.92.rest_0_ = bf16[128,1536]{1,0:T(8,128)(2,1)S(1)} custom-call(bf16[128,1536]{1,0:T(8,128)(2,1)} %source.1), custom_call_target="tpu_custom_call" | custom-call | flops 1048576 | tf_op jit(solution)/shard_map/pallas_call | solution.py:373
  19.7 0.1 collective-permute-start.7
  19.8 0.5 collective-permute-start.9
  20.3 0.5 collective-permute-start.6
  20.7 1.4 %shard_map.93 = (bf16[512,512]{1,0:T(8,128)(2,1)S(1)}, bf16[512,512]{1,0:T(8,128)(2,1)S(1)}, bf16[4,512,128]{2,1,0:T(8,128)(2,1)S(1)}) custom-call(bf16[528,512]{1,0:T(8,128)(2,1)S(1)} %collective-permute-done.source.table, f32[1,512]{1,0:T(1,128)S(1)} %get-tuple-element.23.gain, bf16[128,1536]{1,0:T(8,128)(2,1)S(1)} %shard_map.92.rest_0_, ...), custom_call_target="tpu_custom_call" | custom-call | flops 2147483648 | bytes 4194304 | tf_op jit(solution)/shard_map/pallas_call | solution.py:373
  22.2 0.0 copy-start
  22.2 0.0 copy-start.1
  22.2 1.4 %shard_map.94 = (bf16[512,512]{1,0:T(8,128)(2,1)S(1)}, bf16[512,512]{1,0:T(8,128)(2,1)S(1)}, bf16[4,512,128]{2,1,0:T(8,128)(2,1)S(1)}) custom-call(bf16[512,512]{1,0:T(8,128)(2,1)S(1)} %get-tuple-element.22.source.states, f32[1,512]{1,0:T(1,128)S(1)} %get-tuple-element.23.gain, bf16[128,1536]{1,0:T(8,128)(2,1)S(1)} %shard_map.92.rest_0_, ...), custom_call_target="tpu_custom_call" | custom-call | flops 2147483648 | bytes 4194304 | tf_op jit(solution)/shard_map/pallas_call | solution.py:373
  23.6 0.1 collective-permute-start.10
  23.7 0.5 collective-permute-start.13
  24.2 14.0 %collective-permute-done.1.far = bf16[512,512]{1,0:T(8,128)(2,1)S(1)} collective-permute-done((bf16[512,512]{1,0:T(8,128)(2,1)S(1)}, bf16[512,512]{1,0:T(8,128)(2,1)S(1)}, u32[]{:S(2)}, u32[]{:S(2)}) %collective-permute-start.1) | collective-permute-done | bytes 524320 | tf_op jit(solution)/shard_map/ppermute | solution.py:400
  38.2 0.5 collective-permute-start.14
  38.7 4.9 %shard_map.95 = bf16[512,512]{1,0:T(8,128)(2,1)S(1)} custom-call(bf16[528,512]{1,0:T(8,128)(2,1)S(1)} %collective-permute-done.source.table, bf16[512,512]{1,0:T(8,128)(2,1)S(1)} %collective-permute-done.1.far, bf16[512,512]{1,0:T(8,128)(2,1)S(1)} %get-tuple-element.24.queries, bf16[512,512]{1,0:T(8,128)(2,1)S(1)} %get-tuple-element.25.k_keep, ...), custom_call_target="tpu_custom_call" | custom-call | flops 4294967296 | bytes 4194304 | tf_op jit(solution)/shard_map/pallas_call | solution.py:373
  43.7 0.0 collective-permute-done.6.far
  43.7 0.1 collective-permute-start.5
  43.8 0.0 copy-start.2
  43.8 5.1 %shard_map.96.attended = bf16[512,512]{1,0:T(8,128)(2,1)S(1)} custom-call(bf16[16,512]{1,0:T(8,128)(2,1)S(1)} %get-tuple-element.30.table, bf16[528,512]{1,0:T(8,128)(2,1)S(1)} %collective-permute-done.6.far, bf16[512,512]{1,0:T(8,128)(2,1)S(1)} %get-tuple-element.31.queries, bf16[512,512]{1,0:T(8,128)(2,1)S(1)} %get-tuple-element.25.k_keep, ...), custom_call_target="tpu_custom_call" | custom-call | flops 4294967296 | bytes 4194304 | tf_op jit(solution)/shard_map/pallas_call | solution.py:373
  48.9 0.0 collective-permute-done.14.rest_10_.rest_0_
  48.9 0.6 collective-permute-start.15
  49.5 0.0 collective-permute-done.10.rest_5_
  49.5 3.0 %shard_map.97 = (bf16[512,2048]{1,0:T(8,128)(2,1)S(1)}, f32[2,512,256]{2,1,0:T(8,128)S(1)}) custom-call(bf16[512,512]{1,0:T(8,128)(2,1)S(1)} %get-tuple-element.22.source.states, bf16[512,512]{1,0:T(8,128)(2,1)S(1)} %shard_map.96.attended, f32[1,512]{1,0:T(1,128)S(1)} %get-tuple-element.29.gain, bf16[128,512]{1,0:T(8,128)(2,1)S(1)} %copy-done.2, ...), custom_call_target="tpu_custom_call" | custom-call | flops 3221225472 | bytes 4194304 | tf_op jit(solution)/shard_map/pallas_call | solution.py:373
  52.4 5.6 %collective-permute-done.5.attended = bf16[512,512]{1,0:T(8,128)(2,1)S(1)} collective-permute-done((bf16[512,512]{1,0:T(8,128)(2,1)S(1)}, bf16[512,512]{1,0:T(8,128)(2,1)S(1)}, u32[]{:S(2)}, u32[]{:S(2)}) %collective-permute-start.5) | collective-permute-done | bytes 524320 | tf_op jit(solution)/shard_map/ppermute | solution.py:400
  58.1 3.3 %shard_map.98 = (bf16[512,2048]{1,0:T(8,128)(2,1)S(1)}, f32[2,512,256]{2,1,0:T(8,128)S(1)}, f32[2,512,256]{2,1,0:T(8,128)S(1)}) custom-call(bf16[528,512]{1,0:T(8,128)(2,1)S(1)} %get-tuple-element.21.states, bf16[512,512]{1,0:T(8,128)(2,1)S(1)} %collective-permute-done.5.attended, f32[1,512]{1,0:T(1,128)S(1)} %get-tuple-element.29.gain, ...), custom_call_target="tpu_custom_call" | custom-call | flops 5368709120 | bytes 4194304 | tf_op jit(solution)/shard_map/pallas_call | solution.py:373
  61.4 1.7 %shard_map.99 = bf16[2,512,512]{2,1,0:T(8,128)(2,1)} custom-call(f32[2,512,256]{2,1,0:T(8,128)S(1)} %get-tuple-element.34.total_k, f32[2,512,256]{2,1,0:T(8,128)S(1)} %get-tuple-element.35.total_g, bf16[512,2048]{1,0:T(8,128)(2,1)S(1)} %get-tuple-element.32.hidden_k, bf16[512,2048]{1,0:T(8,128)(2,1)S(1)} %get-tuple-element.36.hidden_g, ...), custom_call_target="tpu_custom_call" | custom-call | flops 2147483648 | bytes 4194304 | tf_op jit(solution)/shard_map/pallas_call | solution.py:373
  (15 shorter events, 0.0 us)
Async XLA Ops:
  0.0 11.1 %collective-permute-start.3 = (bf16[128,1536]{1,0:T(8,128)(2,1)}, bf16[128,1536]{1,0:T(8,128)(2,1)S(1)}, u32[]{:S(2)}, u32[]{:S(2)}) collective-permute-start(bf16[128,1536]{1,0:T(8,128)(2,1)} %source.1), channel_id=1, source_target_pairs={{0,2},{1,3},{2,0},{3,1},{4,6},{5,7},{6,4},{7,5},{8,10},{9,11},{10,... | collective-permute-start | bytes 1179656 | tf_op jit(solution)/shard_map/ppermute | solution.py:400
  2.8 17.0 %collective-permute-start = (bf16[528,512]{1,0:T(8,128)(2,1)S(1)}, bf16[528,512]{1,0:T(8,128)(2,1)S(1)}, u32[]{:S(2)}, u32[]{:S(2)}) collective-permute-start(bf16[528,512]{1,0:T(8,128)(2,1)S(1)} %get-tuple-element.21.states), channel_id=1, source_target_pairs={{0,4},{4,0},{8,12},{12,8},{16,20},{20,16},{24,28},{28,24},{1,5},{5... | collective-permute-start | bytes 1622024 | tf_op jit(solution)/shard_map/ppermute | solution.py:400
  3.4 16.3 %collective-permute-start.2 = (bf16[128,1536]{1,0:T(8,128)(2,1)}, bf16[128,1536]{1,0:T(8,128)(2,1)S(1)}, u32[]{:S(2)}, u32[]{:S(2)}) collective-permute-start(bf16[128,1536]{1,0:T(8,128)(2,1)} %source.1), channel_id=1, source_target_pairs={{0,1},{1,0},{2,3},{3,2},{4,5},{5,4},{6,7},{7,6},{8,9},{9,8},{10,11... | collective-permute-start | bytes 1179656 | tf_op jit(solution)/shard_map/ppermute | solution.py:400
  11.1 9.2 %collective-permute-start.4 = (bf16[128,1536]{1,0:T(8,128)(2,1)S(1)}, bf16[128,1536]{1,0:T(8,128)(2,1)S(1)}, u32[]{:S(2)}, u32[]{:S(2)}) collective-permute-start(bf16[128,1536]{1,0:T(8,128)(2,1)S(1)} %collective-permute-done.3.rest_2_), channel_id=1, source_target_pairs={{0,1},{1,0},{2,3},{3,2},{4,5},{5,4},{6,7},{7,6},{8,9},{9,8},{10,11... | collective-permute-start | bytes 1179656 | tf_op jit(solution)/shard_map/ppermute | solution.py:400
  11.1 6.1 %collective-permute-start.8 = (bf16[128,512]{1,0:T(8,128)(2,1)}, bf16[128,512]{1,0:T(8,128)(2,1)S(1)}, u32[]{:S(2)}, u32[]{:S(2)}) collective-permute-start(bf16[128,512]{1,0:T(8,128)(2,1)} %rest_0_.3), channel_id=1, source_target_pairs={{0,2},{1,3},{2,0},{3,1},{4,6},{5,7},{6,4},{7,5},{8,10},{9,11},{10,... | collective-permute-start | bytes 393224 | tf_op jit(solution)/shard_map/ppermute | solution.py:400
  12.6 25.6 %collective-permute-start.1 = (bf16[512,512]{1,0:T(8,128)(2,1)S(1)}, bf16[512,512]{1,0:T(8,128)(2,1)S(1)}, u32[]{:S(2)}, u32[]{:S(2)}) collective-permute-start(bf16[512,512]{1,0:T(8,128)(2,1)S(1)} %get-tuple-element.22.source.states), channel_id=1, source_target_pairs={{0,24},{4,12},{8,0},{12,20},{16,8},{20,28},{24,16},{28,4},{1,25},{... | collective-permute-start | bytes 1572872 | tf_op jit(solution)/shard_map/ppermute | solution.py:400
  17.2 21.6 %collective-permute-start.11 = (bf16[128,2048]{1,0:T(8,128)(2,1)}, bf16[128,2048]{1,0:T(8,128)(2,1)S(1)}, u32[]{:S(2)}, u32[]{:S(2)}) collective-permute-start(bf16[128,2048]{1,0:T(8,128)(2,1)} %rest_4_.3), channel_id=1, source_target_pairs={{0,2},{1,3},{2,0},{3,1},{4,6},{5,7},{6,4},{7,5},{8,10},{9,11},{10,... | collective-permute-start | bytes 1572872 | tf_op jit(solution)/shard_map/ppermute | solution.py:400
  19.7 3.9 %collective-permute-start.7 = (bf16[128,512]{1,0:T(8,128)(2,1)}, bf16[128,512]{1,0:T(8,128)(2,1)S(1)}, u32[]{:S(2)}, u32[]{:S(2)}) collective-permute-start(bf16[128,512]{1,0:T(8,128)(2,1)} %rest_0_.3), channel_id=1, source_target_pairs={{0,1},{1,0},{2,3},{3,2},{4,5},{5,4},{6,7},{7,6},{8,9},{9,8},{10,11... | collective-permute-start | bytes 393224 | tf_op jit(solution)/shard_map/ppermute | solution.py:400
  19.8 3.9 %collective-permute-start.9 = (bf16[128,512]{1,0:T(8,128)(2,1)S(1)}, bf16[128,512]{1,0:T(8,128)(2,1)S(1)}, u32[]{:S(2)}, u32[]{:S(2)}) collective-permute-start(bf16[128,512]{1,0:T(8,128)(2,1)S(1)} %collective-permute-done.8.rest_2_), channel_id=1, source_target_pairs={{0,1},{1,0},{2,3},{3,2},{4,5},{5,4},{6,7},{7,6},{8,9},{9,8},{10,11... | collective-permute-start | bytes 393224 | tf_op jit(solution)/shard_map/ppermute | solution.py:400
  20.3 23.4 %collective-permute-start.6 = (bf16[528,512]{1,0:T(8,128)(2,1)S(1)}, bf16[528,512]{1,0:T(8,128)(2,1)S(1)}, u32[]{:S(2)}, u32[]{:S(2)}) collective-permute-start(bf16[528,512]{1,0:T(8,128)(2,1)S(1)} %collective-permute-done.source.table), channel_id=1, source_target_pairs={{0,8},{4,28},{8,16},{12,4},{16,24},{20,12},{24,0},{28,20},{1,9},{5... | collective-permute-start | bytes 1622024 | tf_op jit(solution)/shard_map/ppermute | solution.py:400
  22.2 1.5 %copy-start = (bf16[128,2048]{1,0:T(8,128)(2,1)S(1)}, bf16[128,2048]{1,0:T(8,128)(2,1)}, u32[]{:S(2)}) copy-start(bf16[128,2048]{1,0:T(8,128)(2,1)} %rest_4_.3) | copy-start | bytes 1572868
  22.2 1.5 %copy-start.1 = (bf16[512,512]{1,0:T(8,128)(2,1)S(1)}, bf16[512,512]{1,0:T(8,128)(2,1)}, u32[]{:S(2)}) copy-start(bf16[512,512]{1,0:T(8,128)(2,1)} %rest_8_.3) | copy-start | bytes 1572868
  23.6 25.8 %collective-permute-start.10 = (bf16[128,2048]{1,0:T(8,128)(2,1)S(1)}, bf16[128,2048]{1,0:T(8,128)(2,1)S(1)}, u32[]{:S(2)}, u32[]{:S(2)}) collective-permute-start(bf16[128,2048]{1,0:T(8,128)(2,1)S(1)} %copy-done), channel_id=1, source_target_pairs={{0,1},{1,0},{2,3},{3,2},{4,5},{5,4},{6,7},{7,6},{8,9},{9,8},{10,11... | collective-permute-start | bytes 1572872 | tf_op jit(solution)/shard_map/ppermute | solution.py:400
  23.7 25.7 %collective-permute-start.13 = (bf16[512,512]{1,0:T(8,128)(2,1)S(1)}, bf16[512,512]{1,0:T(8,128)(2,1)S(1)}, u32[]{:S(2)}, u32[]{:S(2)}) collective-permute-start(bf16[512,512]{1,0:T(8,128)(2,1)S(1)} %copy-done.1), channel_id=1, source_target_pairs={{0,1},{1,0},{2,3},{3,2},{4,5},{5,4},{6,7},{7,6},{8,9},{9,8},{10,11... | collective-permute-start | bytes 1572872 | tf_op jit(solution)/shard_map/ppermute | solution.py:400
  38.2 10.7 %collective-permute-start.14 = (bf16[512,512]{1,0:T(8,128)(2,1)S(1)}, bf16[512,512]{1,0:T(8,128)(2,1)S(1)}, u32[]{:S(2)}, u32[]{:S(2)}) collective-permute-start(bf16[512,512]{1,0:T(8,128)(2,1)S(1)} %copy-done.1), channel_id=1, source_target_pairs={{0,2},{1,3},{2,0},{3,1},{4,6},{5,7},{6,4},{7,5},{8,10},{9,11},{10,... | collective-permute-start | bytes 1572872 | tf_op jit(solution)/shard_map/ppermute | solution.py:400
  38.7 10.7 %collective-permute-start.12 = (bf16[128,2048]{1,0:T(8,128)(2,1)S(1)}, bf16[128,2048]{1,0:T(8,128)(2,1)S(1)}, u32[]{:S(2)}, u32[]{:S(2)}) collective-permute-start(bf16[128,2048]{1,0:T(8,128)(2,1)S(1)} %collective-permute-done.11.rest_6_), channel_id=1, source_target_pairs={{0,1},{1,0},{2,3},{3,2},{4,5},{5,4},{6,7},{7,6},{8,9},{9,8},{10,11... | collective-permute-start | bytes 1572872 | tf_op jit(solution)/shard_map/ppermute | solution.py:400
  43.7 14.4 %collective-permute-start.5 = (bf16[512,512]{1,0:T(8,128)(2,1)S(1)}, bf16[512,512]{1,0:T(8,128)(2,1)S(1)}, u32[]{:S(2)}, u32[]{:S(2)}) collective-permute-start(bf16[512,512]{1,0:T(8,128)(2,1)S(1)} %shard_map.95), channel_id=1, source_target_pairs={{0,4},{4,0},{8,12},{12,8},{16,20},{20,16},{24,28},{28,24},{1,5},{5... | collective-permute-start | bytes 1572872 | tf_op jit(solution)/shard_map/ppermute | solution.py:400
  43.8 5.7 %copy-start.2 = (bf16[128,512]{1,0:T(8,128)(2,1)S(1)}, bf16[128,512]{1,0:T(8,128)(2,1)}, u32[]{:S(2)}) copy-start(bf16[128,512]{1,0:T(8,128)(2,1)} %rest_0_.3) | copy-start | bytes 393220
  48.9 12.5 %collective-permute-start.15 = (bf16[512,512]{1,0:T(8,128)(2,1)S(1)}, bf16[512,512]{1,0:T(8,128)(2,1)S(1)}, u32[]{:S(2)}, u32[]{:S(2)}) collective-permute-start(bf16[512,512]{1,0:T(8,128)(2,1)S(1)} %collective-permute-done.14.rest_10_.rest_0_), channel_id=1, source_target_pairs={{0,1},{1,0},{2,3},{3,2},{4,5},{5,4},{6,7},{7,6},{8,9},{9,8},{10,11... | collective-permute-start | bytes 1572872 | tf_op jit(solution)/shard_map/ppermute | solution.py:400

commit v4 on v3

--- a/solution.py
+++ b/solution.py
@@ -120,13 +120,14 @@
         tops[at] = top
 
     def blend(t, p, at):
-        top = jnp.max(tops[at], axis=0, keepdims=True) * scale
+        top = jnp.max(tops[at], axis=0, keepdims=True)
         total, outs = None, [None, None]
         for pair in range(0, entries, 2):
             weights = []
             for j in (pair, pair + 1):
                 highest = jnp.where(j < plan[8, t], top, jnp.inf) if j >= SURE else top
-                weight = jnp.exp2(scores[at, j * tile_rows : (j + 1) * tile_rows] * scale - highest)
+                below = scores[at, j * tile_rows : (j + 1) * tile_rows] - highest
+                weight = jnp.exp2(below * scale)
                 part = jnp.sum(weight.reshape(tile_rows // 8, 8, 2 * tile_rows), axis=0)
                 total = part if total is None else total + part
                 weights.append(weight.astype(BF16))
@@ -144,10 +145,10 @@
 
     def finish(t, p, at):
         row = pl.multiple_of(t * tile_rows, tile_rows)
-        total = jnp.sum(totals[at], axis=0, keepdims=True)
+        share = 1.0 / jnp.sum(totals[at], axis=0, keepdims=True)
         for a in range(2):
             h = 2 * p + a
-            out = sums[at, a * head : (a + 1) * head] / total[:, a * tile_rows : (a + 1) * tile_rows]
+            out = sums[at, a * head : (a + 1) * head] * share[:, a * tile_rows : (a + 1) * tile_rows]
             out_ref[pl.ds(row, tile_rows), h * head : (h + 1) * head] = out.T.astype(BF16)
 
     pairs = HEADS // 2
@@ -191,8 +192,7 @@
     return jnp.clip(slots, 0, 3 * tiles - 1).astype(F32), counts[...].astype(F32)
 
 
-def write_table(target, row, slots, counts):
-    target[pl.ds(row, EXTRA), :] = jnp.zeros((EXTRA, target.shape[1]), BF16)
+def write_table(target, slots, counts):
     table = jnp.concatenate(
         [
             jnp.pad(slots, ((0, 8 - slots.shape[0]), (0, 128 - slots.shape[1]))),
@@ -200,20 +200,19 @@
         ],
         axis=0,
     )
-    target[pl.ds(row, EXTRA), 0:128] = table.astype(BF16)
+    target[...] = table.astype(BF16)
 
 
 def pack_body(
-    states, lists_in, counts_in, gains_in, more_gains_in, give, keep, table, gains, more_gains,
+    states, lists_in, counts_in, gains_in, more_gains_in, give, keep, table, sent, gains, more_gains,
     lists, counts, sems, *, ring,
 ):
     place = lax.axis_index("mesh")
     side = place & 1
-    rows = keep.shape[0]
     copies = [
         pltpu.make_async_copy(lists_in, lists, sems.at[0]),
         pltpu.make_async_copy(counts_in, counts, sems.at[1]),
-        pltpu.make_async_copy(states.at[1 - side], give.at[pl.ds(0, rows)], sems.at[2]),
+        pltpu.make_async_copy(states.at[1 - side], give, sems.at[2]),
         pltpu.make_async_copy(states.at[side], keep, sems.at[3]),
         pltpu.make_async_copy(gains_in, gains, sems.at[4]),
         pltpu.make_async_copy(more_gains_in, more_gains, sems.at[5]),
@@ -222,8 +221,8 @@
         copy.start()
     for copy in copies[:2]:
         copy.wait()
-    write_table(table, 0, *slot_rows(lists, counts, place, ring, 0))
-    write_table(give, rows, *slot_rows(lists, counts, place, ring, 1))
+    write_table(table, *slot_rows(lists, counts, place, ring, 0))
+    write_table(sent, *slot_rows(lists, counts, place, ring, 1))
     for copy in copies[2:]:
         copy.wait()
 
@@ -249,8 +248,7 @@
     )
     rows = queries.shape[0]
     tiles = rows // tile_rows
-    last = table.shape[0] - EXTRA
-    whole[...] = table[last:, 0:128].astype(F32).astype(jnp.int32)
+    whole[...] = table[...].astype(F32).astype(jnp.int32)
     copies = [
         pltpu.make_async_copy(whole, plan, sems.at[0]),
         pltpu.make_async_copy(k_keep, keys.at[pl.ds(0, rows)], sems.at[1]),
@@ -424,9 +422,12 @@
                 pieces[k ^ bit] = send("member", perm, piece)
         return [pieces[k] for k in range(n)]
 
-    give, keep, table, gain, second = call(
+    give, keep, table, sent, gain, second = call(
         pack_body,
-        [(rows + EXTRA, width), (rows, width), (EXTRA, width), (1, width, F32), (1, width, F32)],
+        [
+            (rows, width), (rows, width), (EXTRA, 128), (EXTRA, 128),
+            (1, width, F32), (1, width, F32),
+        ],
         [
             pltpu.VMEM((tiles, entries), jnp.int32),
             pltpu.VMEM((1, tiles), jnp.int32),
@@ -443,6 +444,7 @@
         1 << 20, moved=0, ring=ring,
     )
     got = send("mesh", swap, give)
+    plan = send("mesh", swap, sent)
     proj = gather(projection)
     far_near = send("mesh", outward, keep)
     far_late = send("mesh", inward, got)
@@ -497,7 +499,7 @@
 
     q_keep, k_keep, v_keep = near(keep)
     q_got, k_got, v_got = near(got)
-    attended_got = reach(got, far_near, q_got)
+    attended_got = reach(plan, far_near, q_got)
     attended_back = send("mesh", swap, attended_got)
     attended_keep = reach(table, far_late, q_keep)
     early = n // 2

time: 63.5 us -> 60.2 us (0.948)
  the two profiles are of different devices: /device:TPU:28 before, /device:TPU:0 now
where the time goes in v4:
time: 60.2 us; the launch traced here: 60.1 us
  Pallas kernels  22.7 us (38%)
  waiting for transfers between devices  19.4 us (32%)
  starting transfers between devices  17.5 us (29%)
    pallas_call x9, Pallas kernels, call(): pl.pallas_call(functools.partial(body, **static), out_shape=[jax.ShapeDty...  22.7 us
    ppermute x17, waiting for transfers between devices, send(): return lax.ppermute(array, axis, perm)  19.4 us
    ppermute x17, starting transfers between devices, send(): return lax.ppermute(array, axis, perm)  17.5 us
  transfers between devices with their start and end apart: 17, of which 7 were waited for; matrix products, arithmetic and copies ran while one was open for 0% of the time, Pallas kernels for 35%

profile of v4, /device:TPU:0, one launch (start us, length us, event | category | flops | bytes accessed | tf_op | source)
XLA Modules:
  0.0 60.1 jit_solution(9225681937458015765)
XLA Ops:
  0.0 3.0 %collective-permute-start.4 = (bf16[128,1536]{1,0:T(8,128)(2,1)}, bf16[128,1536]{1,0:T(8,128)(2,1)S(1)}, u32[]{:S(2)}, u32[]{:S(2)}) collective-permute-start(bf16[128,1536]{1,0:T(8,128)(2,1)} %source.1), channel_id=1, source_target_pairs={{0,2},{1,3},{2,0},{3,1},{4,6},{5,7},{6,4},{7,5},{8,10},{9,11},{10,... | collective-permute-start | bytes 1179656 | tf_op jit(solution)/shard_map/ppermute | solution.py:398
  3.0 1.3 %shard_map.91 = (bf16[512,512]{1,0:T(8,128)(2,1)S(1)}, bf16[512,512]{1,0:T(8,128)(2,1)S(1)}, bf16[16,128]{1,0:T(8,128)(2,1)S(1)}, bf16[16,128]{1,0:T(8,128)(2,1)...) custom-call(bf16[2,512,512]{2,1,0:T(8,128)(2,1)} %states.1, s32[4,8]{1,0:T(4,128)} %lists_in.1, s32[1,4]{1,0:T(1,128)} %bitcast.5, ...), custom_call_target="tpu_custom_call" | custom-call | flops 1048576 | tf_op jit(solution)/shard_map/pallas_call | solution.py:371
  4.3 1.6 %collective-permute-start.2 = (bf16[512,512]{1,0:T(8,128)(2,1)S(1)}, bf16[512,512]{1,0:T(8,128)(2,1)S(1)}, u32[]{:S(2)}, u32[]{:S(2)}) collective-permute-start(bf16[512,512]{1,0:T(8,128)(2,1)S(1)} %get-tuple-element.22.states), channel_id=1, source_target_pairs={{0,4},{4,0},{8,12},{12,8},{16,20},{20,16},{24,28},{28,24},{1,5},{5... | collective-permute-start | bytes 1572872 | tf_op jit(solution)/shard_map/ppermute | solution.py:398
  5.8 6.4 %collective-permute-done.4.rest_2_ = bf16[128,1536]{1,0:T(8,128)(2,1)S(1)} collective-permute-done((bf16[128,1536]{1,0:T(8,128)(2,1)}, bf16[128,1536]{1,0:T(8,128)(2,1)S(1)}, u32[]{:S(2)}, u32[]{:S(2)}) %collective-permute-start.4) | collective-permute-done | bytes 393248 | tf_op jit(solution)/shard_map/ppermute | solution.py:398
  12.3 1.7 %collective-permute-start.9 = (bf16[128,512]{1,0:T(8,128)(2,1)}, bf16[128,512]{1,0:T(8,128)(2,1)S(1)}, u32[]{:S(2)}, u32[]{:S(2)}) collective-permute-start(bf16[128,512]{1,0:T(8,128)(2,1)} %rest_0_.3), channel_id=1, source_target_pairs={{0,2},{1,3},{2,0},{3,1},{4,6},{5,7},{6,4},{7,5},{8,10},{9,11},{10,... | collective-permute-start | bytes 393224 | tf_op jit(solution)/shard_map/ppermute | solution.py:398
  14.0 3.6 %collective-permute-start.1 = (bf16[512,512]{1,0:T(8,128)(2,1)S(1)}, bf16[512,512]{1,0:T(8,128)(2,1)S(1)}, u32[]{:S(2)}, u32[]{:S(2)}) collective-permute-start(bf16[512,512]{1,0:T(8,128)(2,1)S(1)} %get-tuple-element.24.source.states), channel_id=1, source_target_pairs={{0,24},{4,12},{8,0},{12,20},{16,8},{20,28},{24,16},{28,4},{1,25},{... | collective-permute-start | bytes 1572872 | tf_op jit(solution)/shard_map/ppermute | solution.py:398
  17.6 0.8 %collective-permute-done.9.rest_2_ = bf16[128,512]{1,0:T(8,128)(2,1)S(1)} collective-permute-done((bf16[128,512]{1,0:T(8,128)(2,1)}, bf16[128,512]{1,0:T(8,128)(2,1)S(1)}, u32[]{:S(2)}, u32[]{:S(2)}) %collective-permute-start.9) | collective-permute-done | bytes 131104 | tf_op jit(solution)/shard_map/ppermute | solution.py:398
  18.4 1.7 %collective-permute-start.12 = (bf16[128,2048]{1,0:T(8,128)(2,1)}, bf16[128,2048]{1,0:T(8,128)(2,1)S(1)}, u32[]{:S(2)}, u32[]{:S(2)}) collective-permute-start(bf16[128,2048]{1,0:T(8,128)(2,1)} %rest_4_.3), channel_id=1, source_target_pairs={{0,2},{1,3},{2,0},{3,1},{4,6},{5,7},{6,4},{7,5},{8,10},{9,11},{10,... | collective-permute-start | bytes 1572872 | tf_op jit(solution)/shard_map/ppermute | solution.py:398
  20.2 1.0 %shard_map.92.rest_0_ = bf16[128,1536]{1,0:T(8,128)(2,1)S(1)} custom-call(bf16[128,1536]{1,0:T(8,128)(2,1)} %source.1), custom_call_target="tpu_custom_call" | custom-call | flops 1048576 | tf_op jit(solution)/shard_map/pallas_call | solution.py:371
  21.2 0.1 collective-permute-start.8
  21.3 1.6 %collective-permute-start = (bf16[16,128]{1,0:T(8,128)(2,1)S(1)}, bf16[16,128]{1,0:T(8,128)(2,1)S(1)}, u32[]{:S(2)}, u32[]{:S(2)}) collective-permute-start(bf16[16,128]{1,0:T(8,128)(2,1)S(1)} %get-tuple-element.23), channel_id=1, source_target_pairs={{0,4},{4,0},{8,12},{12,8},{16,20},{20,16},{24,28},{28,24},{1,5},{5... | collective-permute-start | bytes 12296 | tf_op jit(solution)/shard_map/ppermute | solution.py:398
  22.9 0.1 collective-permute-start.10
  23.0 1.4 %shard_map.93 = (bf16[512,512]{1,0:T(8,128)(2,1)S(1)}, bf16[512,512]{1,0:T(8,128)(2,1)S(1)}, bf16[4,512,128]{2,1,0:T(8,128)(2,1)S(1)}) custom-call(bf16[512,512]{1,0:T(8,128)(2,1)S(1)} %collective-permute-done.2.source, f32[1,512]{1,0:T(1,128)S(1)} %get-tuple-element.25.gain, bf16[128,1536]{1,0:T(8,128)(2,1)S(1)} %shard_map.92.rest_0_, ...), custom_call_target="tpu_custom_call" | custom-call | flops 2147483648 | bytes 4194304 | tf_op jit(solution)/shard_map/pallas_call | solution.py:371
  24.4 0.0 copy-start
  24.4 0.0 copy-start.1
  24.4 0.5 collective-permute-done.table
  24.9 1.6 %collective-permute-start.7 = (bf16[512,512]{1,0:T(8,128)(2,1)S(1)}, bf16[512,512]{1,0:T(8,128)(2,1)S(1)}, u32[]{:S(2)}, u32[]{:S(2)}) collective-permute-start(bf16[512,512]{1,0:T(8,128)(2,1)S(1)} %collective-permute-done.2.source), channel_id=1, source_target_pairs={{0,8},{4,28},{8,16},{12,4},{16,24},{20,12},{24,0},{28,20},{1,9},{5... | collective-permute-start | bytes 1572872 | tf_op jit(solution)/shard_map/ppermute | solution.py:398
  26.5 1.4 %shard_map.94 = (bf16[512,512]{1,0:T(8,128)(2,1)S(1)}, bf16[512,512]{1,0:T(8,128)(2,1)S(1)}, bf16[4,512,128]{2,1,0:T(8,128)(2,1)S(1)}) custom-call(bf16[512,512]{1,0:T(8,128)(2,1)S(1)} %get-tuple-element.24.source.states, f32[1,512]{1,0:T(1,128)S(1)} %get-tuple-element.25.gain, bf16[128,1536]{1,0:T(8,128)(2,1)S(1)} %shard_map.92.rest_0_, ...), custom_call_target="tpu_custom_call" | custom-call | flops 2147483648 | bytes 4194304 | tf_op jit(solution)/shard_map/pallas_call | solution.py:371
  28.0 0.1 collective-permute-start.11
  28.1 0.5 collective-permute-start.14
  28.5 1.4 %collective-permute-done.1.far = bf16[512,512]{1,0:T(8,128)(2,1)S(1)} collective-permute-done((bf16[512,512]{1,0:T(8,128)(2,1)S(1)}, bf16[512,512]{1,0:T(8,128)(2,1)S(1)}, u32[]{:S(2)}, u32[]{:S(2)}) %collective-permute-start.1) | collective-permute-done | bytes 524320 | tf_op jit(solution)/shard_map/ppermute | solution.py:398
  30.0 0.5 collective-permute-start.15
  30.5 2.4 %collective-permute-done.12.rest_6_ = bf16[128,2048]{1,0:T(8,128)(2,1)S(1)} collective-permute-done((bf16[128,2048]{1,0:T(8,128)(2,1)}, bf16[128,2048]{1,0:T(8,128)(2,1)S(1)}, u32[]{:S(2)}, u32[]{:S(2)}) %collective-permute-start.12) | collective-permute-done | bytes 524320 | tf_op jit(solution)/shard_map/ppermute | solution.py:398
  33.0 4.8 %shard_map.95 = bf16[512,512]{1,0:T(8,128)(2,1)S(1)} custom-call(bf16[16,128]{1,0:T(8,128)(2,1)S(1)} %collective-permute-done.table, bf16[512,512]{1,0:T(8,128)(2,1)S(1)} %collective-permute-done.1.far, bf16[512,512]{1,0:T(8,128)(2,1)S(1)} %get-tuple-element.26.queries, bf16[512,512]{1,0:T(8,128)(2,1)S(1)} %get-tuple-element.27.k_keep, ...), custom_call_target="tpu_custom_call" | custom-call | flops 4294967296 | bytes 4194304 | tf_op jit(solution)/shard_map/pallas_call | solution.py:371
  37.8 3.6 %collective-permute-done.7.far = bf16[512,512]{1,0:T(8,128)(2,1)S(1)} collective-permute-done((bf16[512,512]{1,0:T(8,128)(2,1)S(1)}, bf16[512,512]{1,0:T(8,128)(2,1)S(1)}, u32[]{:S(2)}, u32[]{:S(2)}) %collective-permute-start.7) | collective-permute-done | bytes 524320 | tf_op jit(solution)/shard_map/ppermute | solution.py:398
  41.4 1.4 %collective-permute-start.6 = (bf16[512,512]{1,0:T(8,128)(2,1)S(1)}, bf16[512,512]{1,0:T(8,128)(2,1)S(1)}, u32[]{:S(2)}, u32[]{:S(2)}) collective-permute-start(bf16[512,512]{1,0:T(8,128)(2,1)S(1)} %shard_map.95), channel_id=1, source_target_pairs={{0,4},{4,0},{8,12},{12,8},{16,20},{20,16},{24,28},{28,24},{1,5},{5... | collective-permute-start | bytes 1572872 | tf_op jit(solution)/shard_map/ppermute | solution.py:398
  42.7 4.8 %shard_map.96.attended = bf16[512,512]{1,0:T(8,128)(2,1)S(1)} custom-call(bf16[16,128]{1,0:T(8,128)(2,1)S(1)} %get-tuple-element.32.table, bf16[512,512]{1,0:T(8,128)(2,1)S(1)} %collective-permute-done.7.far, bf16[512,512]{1,0:T(8,128)(2,1)S(1)} %get-tuple-element.33.queries, bf16[512,512]{1,0:T(8,128)(2,1)S(1)} %get-tuple-element.27.k_keep, ...), custom_call_target="tpu_custom_call" | custom-call | flops 4294967296 | bytes 4194304 | tf_op jit(solution)/shard_map/pallas_call | solution.py:371
  47.5 0.1 collective-permute-start.16
  47.7 3.0 %shard_map.97 = (bf16[512,2048]{1,0:T(8,128)(2,1)S(1)}, f32[2,512,256]{2,1,0:T(8,128)S(1)}) custom-call(bf16[512,512]{1,0:T(8,128)(2,1)S(1)} %get-tuple-element.24.source.states, bf16[512,512]{1,0:T(8,128)(2,1)S(1)} %shard_map.96.attended, f32[1,512]{1,0:T(1,128)S(1)} %get-tuple-element.31.gain, bf16[128,512]{1,0:T(8,128)(2,1)S(1)} %copy-done.2, ...), custom_call_target="tpu_custom_call" | custom-call | flops 3221225472 | bytes 4194304 | tf_op jit(solution)/shard_map/pallas_call | solution.py:371
  50.6 4.2 %collective-permute-done.6.attended = bf16[512,512]{1,0:T(8,128)(2,1)S(1)} collective-permute-done((bf16[512,512]{1,0:T(8,128)(2,1)S(1)}, bf16[512,512]{1,0:T(8,128)(2,1)S(1)}, u32[]{:S(2)}, u32[]{:S(2)}) %collective-permute-start.6) | collective-permute-done | bytes 524320 | tf_op jit(solution)/shard_map/ppermute | solution.py:398
  54.8 3.3 %shard_map.98 = (bf16[512,2048]{1,0:T(8,128)(2,1)S(1)}, f32[2,512,256]{2,1,0:T(8,128)S(1)}, f32[2,512,256]{2,1,0:T(8,128)S(1)}) custom-call(bf16[512,512]{1,0:T(8,128)(2,1)S(1)} %get-tuple-element.22.states, bf16[512,512]{1,0:T(8,128)(2,1)S(1)} %collective-permute-done.6.attended, f32[1,512]{1,0:T(1,128)S(1)} %get-tuple-element.31.gain, ...), custom_call_target="tpu_custom_call" | custom-call | flops 5368709120 | bytes 4194304 | tf_op jit(solution)/shard_map/pallas_call | solution.py:371
  58.1 1.8 %shard_map.99 = bf16[2,512,512]{2,1,0:T(8,128)(2,1)} custom-call(f32[2,512,256]{2,1,0:T(8,128)S(1)} %get-tuple-element.36.total_k, f32[2,512,256]{2,1,0:T(8,128)S(1)} %get-tuple-element.37.total_g, bf16[512,2048]{1,0:T(8,128)(2,1)S(1)} %get-tuple-element.34.hidden_k, bf16[512,2048]{1,0:T(8,128)(2,1)S(1)} %get-tuple-element.38.hidden_g, ...), custom_call_target="tpu_custom_call" | custom-call | flops 2147483648 | bytes 4194304 | tf_op jit(solution)/shard_map/pallas_call | solution.py:371
  (17 shorter events, 0.0 us)
Async XLA Ops:
  0.0 12.3 %collective-permute-start.4 = (bf16[128,1536]{1,0:T(8,128)(2,1)}, bf16[128,1536]{1,0:T(8,128)(2,1)S(1)}, u32[]{:S(2)}, u32[]{:S(2)}) collective-permute-start(bf16[128,1536]{1,0:T(8,128)(2,1)} %source.1), channel_id=1, source_target_pairs={{0,2},{1,3},{2,0},{3,1},{4,6},{5,7},{6,4},{7,5},{8,10},{9,11},{10,... | collective-permute-start | bytes 1179656 | tf_op jit(solution)/shard_map/ppermute | solution.py:398
  4.3 17.0 %collective-permute-start.2 = (bf16[512,512]{1,0:T(8,128)(2,1)S(1)}, bf16[512,512]{1,0:T(8,128)(2,1)S(1)}, u32[]{:S(2)}, u32[]{:S(2)}) collective-permute-start(bf16[512,512]{1,0:T(8,128)(2,1)S(1)} %get-tuple-element.22.states), channel_id=1, source_target_pairs={{0,4},{4,0},{8,12},{12,8},{16,20},{20,16},{24,28},{28,24},{1,5},{5... | collective-permute-start | bytes 1572872 | tf_op jit(solution)/shard_map/ppermute | solution.py:398
  5.8 15.3 %collective-permute-start.3 = (bf16[128,1536]{1,0:T(8,128)(2,1)}, bf16[128,1536]{1,0:T(8,128)(2,1)S(1)}, u32[]{:S(2)}, u32[]{:S(2)}) collective-permute-start(bf16[128,1536]{1,0:T(8,128)(2,1)} %source.1), channel_id=1, source_target_pairs={{0,1},{1,0},{2,3},{3,2},{4,5},{5,4},{6,7},{7,6},{8,9},{9,8},{10,11... | collective-permute-start | bytes 1179656 | tf_op jit(solution)/shard_map/ppermute | solution.py:398
  12.3 10.6 %collective-permute-start.5 = (bf16[128,1536]{1,0:T(8,128)(2,1)S(1)}, bf16[128,1536]{1,0:T(8,128)(2,1)S(1)}, u32[]{:S(2)}, u32[]{:S(2)}) collective-permute-start(bf16[128,1536]{1,0:T(8,128)(2,1)S(1)} %collective-permute-done.4.rest_2_), channel_id=1, source_target_pairs={{0,1},{1,0},{2,3},{3,2},{4,5},{5,4},{6,7},{7,6},{8,9},{9,8},{10,11... | collective-permute-start | bytes 1179656 | tf_op jit(solution)/shard_map/ppermute | solution.py:398
  12.3 6.1 %collective-permute-start.9 = (bf16[128,512]{1,0:T(8,128)(2,1)}, bf16[128,512]{1,0:T(8,128)(2,1)S(1)}, u32[]{:S(2)}, u32[]{:S(2)}) collective-permute-start(bf16[128,512]{1,0:T(8,128)(2,1)} %rest_0_.3), channel_id=1, source_target_pairs={{0,2},{1,3},{2,0},{3,1},{4,6},{5,7},{6,4},{7,5},{8,10},{9,11},{10,... | collective-permute-start | bytes 393224 | tf_op jit(solution)/shard_map/ppermute | solution.py:398
  14.0 15.9 %collective-permute-start.1 = (bf16[512,512]{1,0:T(8,128)(2,1)S(1)}, bf16[512,512]{1,0:T(8,128)(2,1)S(1)}, u32[]{:S(2)}, u32[]{:S(2)}) collective-permute-start(bf16[512,512]{1,0:T(8,128)(2,1)S(1)} %get-tuple-element.24.source.states), channel_id=1, source_target_pairs={{0,24},{4,12},{8,0},{12,20},{16,8},{20,28},{24,16},{28,4},{1,25},{... | collective-permute-start | bytes 1572872 | tf_op jit(solution)/shard_map/ppermute | solution.py:398
  18.4 14.6 %collective-permute-start.12 = (bf16[128,2048]{1,0:T(8,128)(2,1)}, bf16[128,2048]{1,0:T(8,128)(2,1)S(1)}, u32[]{:S(2)}, u32[]{:S(2)}) collective-permute-start(bf16[128,2048]{1,0:T(8,128)(2,1)} %rest_4_.3), channel_id=1, source_target_pairs={{0,2},{1,3},{2,0},{3,1},{4,6},{5,7},{6,4},{7,5},{8,10},{9,11},{10,... | collective-permute-start | bytes 1572872 | tf_op jit(solution)/shard_map/ppermute | solution.py:398
  21.2 6.8 %collective-permute-start.8 = (bf16[128,512]{1,0:T(8,128)(2,1)}, bf16[128,512]{1,0:T(8,128)(2,1)S(1)}, u32[]{:S(2)}, u32[]{:S(2)}) collective-permute-start(bf16[128,512]{1,0:T(8,128)(2,1)} %rest_0_.3), channel_id=1, source_target_pairs={{0,1},{1,0},{2,3},{3,2},{4,5},{5,4},{6,7},{7,6},{8,9},{9,8},{10,11... | collective-permute-start | bytes 393224 | tf_op jit(solution)/shard_map/ppermute | solution.py:398
  21.3 3.7 %collective-permute-start = (bf16[16,128]{1,0:T(8,128)(2,1)S(1)}, bf16[16,128]{1,0:T(8,128)(2,1)S(1)}, u32[]{:S(2)}, u32[]{:S(2)}) collective-permute-start(bf16[16,128]{1,0:T(8,128)(2,1)S(1)} %get-tuple-element.23), channel_id=1, source_target_pairs={{0,4},{4,0},{8,12},{12,8},{16,20},{20,16},{24,28},{28,24},{1,5},{5... | collective-permute-start | bytes 12296 | tf_op jit(solution)/shard_map/ppermute | solution.py:398
  22.9 5.2 %collective-permute-start.10 = (bf16[128,512]{1,0:T(8,128)(2,1)S(1)}, bf16[128,512]{1,0:T(8,128)(2,1)S(1)}, u32[]{:S(2)}, u32[]{:S(2)}) collective-permute-start(bf16[128,512]{1,0:T(8,128)(2,1)S(1)} %collective-permute-done.9.rest_2_), channel_id=1, source_target_pairs={{0,1},{1,0},{2,3},{3,2},{4,5},{5,4},{6,7},{7,6},{8,9},{9,8},{10,11... | collective-permute-start | bytes 393224 | tf_op jit(solution)/shard_map/ppermute | solution.py:398
  24.4 3.5 %copy-start = (bf16[128,2048]{1,0:T(8,128)(2,1)S(1)}, bf16[128,2048]{1,0:T(8,128)(2,1)}, u32[]{:S(2)}) copy-start(bf16[128,2048]{1,0:T(8,128)(2,1)} %rest_4_.3) | copy-start | bytes 1572868
  24.4 3.6 %copy-start.1 = (bf16[512,512]{1,0:T(8,128)(2,1)S(1)}, bf16[512,512]{1,0:T(8,128)(2,1)}, u32[]{:S(2)}) copy-start(bf16[512,512]{1,0:T(8,128)(2,1)} %rest_8_.3) | copy-start | bytes 1572868
  24.9 16.4 %collective-permute-start.7 = (bf16[512,512]{1,0:T(8,128)(2,1)S(1)}, bf16[512,512]{1,0:T(8,128)(2,1)S(1)}, u32[]{:S(2)}, u32[]{:S(2)}) collective-permute-start(bf16[512,512]{1,0:T(8,128)(2,1)S(1)} %collective-permute-done.2.source), channel_id=1, source_target_pairs={{0,8},{4,28},{8,16},{12,4},{16,24},{20,12},{24,0},{28,20},{1,9},{5... | collective-permute-start | bytes 1572872 | tf_op jit(solution)/shard_map/ppermute | solution.py:398
  28.0 19.7 %collective-permute-start.11 = (bf16[128,2048]{1,0:T(8,128)(2,1)S(1)}, bf16[128,2048]{1,0:T(8,128)(2,1)S(1)}, u32[]{:S(2)}, u32[]{:S(2)}) collective-permute-start(bf16[128,2048]{1,0:T(8,128)(2,1)S(1)} %copy-done), channel_id=1, source_target_pairs={{0,1},{1,0},{2,3},{3,2},{4,5},{5,4},{6,7},{7,6},{8,9},{9,8},{10,11... | collective-permute-start | bytes 1572872 | tf_op jit(solution)/shard_map/ppermute | solution.py:398
  28.1 19.6 %collective-permute-start.14 = (bf16[512,512]{1,0:T(8,128)(2,1)S(1)}, bf16[512,512]{1,0:T(8,128)(2,1)S(1)}, u32[]{:S(2)}, u32[]{:S(2)}) collective-permute-start(bf16[512,512]{1,0:T(8,128)(2,1)S(1)} %copy-done.1), channel_id=1, source_target_pairs={{0,1},{1,0},{2,3},{3,2},{4,5},{5,4},{6,7},{7,6},{8,9},{9,8},{10,11... | collective-permute-start | bytes 1572872 | tf_op jit(solution)/shard_map/ppermute | solution.py:398
  30.0 17.5 %collective-permute-start.15 = (bf16[512,512]{1,0:T(8,128)(2,1)S(1)}, bf16[512,512]{1,0:T(8,128)(2,1)S(1)}, u32[]{:S(2)}, u32[]{:S(2)}) collective-permute-start(bf16[512,512]{1,0:T(8,128)(2,1)S(1)} %copy-done.1), channel_id=1, source_target_pairs={{0,2},{1,3},{2,0},{3,1},{4,6},{5,7},{6,4},{7,5},{8,10},{9,11},{10,... | collective-permute-start | bytes 1572872 | tf_op jit(solution)/shard_map/ppermute | solution.py:398
  33.0 14.7 %collective-permute-start.13 = (bf16[128,2048]{1,0:T(8,128)(2,1)S(1)}, bf16[128,2048]{1,0:T(8,128)(2,1)S(1)}, u32[]{:S(2)}, u32[]{:S(2)}) collective-permute-start(bf16[128,2048]{1,0:T(8,128)(2,1)S(1)} %collective-permute-done.12.rest_6_), channel_id=1, source_target_pairs={{0,1},{1,0},{2,3},{3,2},{4,5},{5,4},{6,7},{7,6},{8,9},{9,8},{10,11... | collective-permute-start | bytes 1572872 | tf_op jit(solution)/shard_map/ppermute | solution.py:398
  41.4 13.5 %collective-permute-start.6 = (bf16[512,512]{1,0:T(8,128)(2,1)S(1)}, bf16[512,512]{1,0:T(8,128)(2,1)S(1)}, u32[]{:S(2)}, u32[]{:S(2)}) collective-permute-start(bf16[512,512]{1,0:T(8,128)(2,1)S(1)} %shard_map.95), channel_id=1, source_target_pairs={{0,4},{4,0},{8,12},{12,8},{16,20},{20,16},{24,28},{28,24},{1,5},{5... | collective-permute-start | bytes 1572872 | tf_op jit(solution)/shard_map/ppermute | solution.py:398
  42.7 4.9 %copy-start.2 = (bf16[128,512]{1,0:T(8,128)(2,1)S(1)}, bf16[128,512]{1,0:T(8,128)(2,1)}, u32[]{:S(2)}) copy-start(bf16[128,512]{1,0:T(8,128)(2,1)} %rest_0_.3) | copy-start | bytes 393220
  47.5 10.6 %collective-permute-start.16 = (bf16[512,512]{1,0:T(8,128)(2,1)S(1)}, bf16[512,512]{1,0:T(8,128)(2,1)S(1)}, u32[]{:S(2)}, u32[]{:S(2)}) collective-permute-start(bf16[512,512]{1,0:T(8,128)(2,1)S(1)} %collective-permute-done.15.rest_10_.rest_0_), channel_id=1, source_target_pairs={{0,1},{1,0},{2,3},{3,2},{4,5},{5,4},{6,7},{7,6},{8,9},{9,8},{10,11... | collective-permute-start | bytes 1572872 | tf_op jit(solution)/shard_map/ppermute | solution.py:398

commit v5 on v4

--- a/solution.py
+++ b/solution.py
@@ -233,9 +233,15 @@
     copy.wait()
 
 
-def near_body(source, gain, *rest, n_pieces, tile_rows):
-    pieces, (queries, keys, values, normed) = rest[:n_pieces], rest[n_pieces:]
+def near_body(source, gain, *rest, n_pieces, tile_rows, asks):
+    pieces, (first, keys, values, *scratch) = rest[:n_pieces], rest[n_pieces:]
+    queries, normed = (first, scratch[0]) if asks else (None, first)
     norm_project(source, gain, normed, pieces, queries, keys, values, 0, tile_rows)
+
+
+def ask_body(normed, *rest):
+    *pieces, queries = rest
+    queries[...] = dot(normed[...], stacked(pieces, slice(0, normed.shape[1]))).astype(BF16)
 
 
 def reach_body(
@@ -476,14 +482,14 @@
     )
     proj = [own, *proj[1:]]
 
-    def near(source):
+    def near(source, asks):
         return call(
             near_body,
             [(rows, width), (rows, width), (tiles, width, tile_rows)],
-            [block],
+            [block] if asks else [],
             [source, gain, *proj],
             [VMEM] * (2 + n),
-            2 << 30, n_pieces=n, tile_rows=tile_rows,
+            2 << 30, n_pieces=n, tile_rows=tile_rows, asks=asks,
         )
 
     def reach(table, far, queries):
@@ -497,10 +503,11 @@
         )
         return attended
 
-    q_keep, k_keep, v_keep = near(keep)
-    q_got, k_got, v_got = near(got)
+    normed_keep, k_keep, v_keep = near(keep, False)
+    q_got, k_got, v_got = near(got, True)
     attended_got = reach(plan, far_near, q_got)
     attended_back = send("mesh", swap, attended_got)
+    (q_keep,) = call(ask_body, [(rows, width)], [], [normed_keep, *proj], [VMEM] * (1 + n), 1 << 29)
     attended_keep = reach(table, far_late, q_keep)
     early = n // 2
     sums = (width // 256, rows, 256, F32)

time: 60.2 us -> 60.2 us (level)
    pallas_call x9 -> x10, Pallas kernels: 22.7 us -> 23 us  [call(): pl.pallas_call(functools.partial(body, **static), out_shape=[jax.ShapeDty...]
where the time goes in v5:
time: 60.2 us; the launch traced here: 60.1 us
  Pallas kernels  23 us (38%)
  waiting for transfers between devices  19.2 us (32%)
  starting transfers between devices  17.5 us (29%)
    pallas_call x10, Pallas kernels, call(): pl.pallas_call(functools.partial(body, **static), out_shape=[jax.ShapeDty...  23 us
    ppermute x17, waiting for transfers between devices, send(): return lax.ppermute(array, axis, perm)  19.2 us
    ppermute x17, starting transfers between devices, send(): return lax.ppermute(array, axis, perm)  17.5 us
  transfers between devices with their start and end apart: 17, of which 7 were waited for; matrix products, arithmetic and copies ran while one was open for 0% of the time, Pallas kernels for 35%

profile of v5, /device:TPU:0, one launch (start us, length us, event | category | flops | bytes accessed | tf_op | source)
XLA Modules:
  0.0 60.1 jit_solution(547120937421383144)
XLA Ops:
  0.0 3.0 %collective-permute-start.4 = (bf16[128,1536]{1,0:T(8,128)(2,1)}, bf16[128,1536]{1,0:T(8,128)(2,1)S(1)}, u32[]{:S(2)}, u32[]{:S(2)}) collective-permute-start(bf16[128,1536]{1,0:T(8,128)(2,1)} %source.1), channel_id=1, source_target_pairs={{0,2},{1,3},{2,0},{3,1},{4,6},{5,7},{6,4},{7,5},{8,10},{9,11},{10,... | collective-permute-start | bytes 1179656 | tf_op jit(solution)/shard_map/ppermute | solution.py:404
  3.0 1.3 %shard_map.91 = (bf16[512,512]{1,0:T(8,128)(2,1)S(1)}, bf16[512,512]{1,0:T(8,128)(2,1)S(1)}, bf16[16,128]{1,0:T(8,128)(2,1)S(1)}, bf16[16,128]{1,0:T(8,128)(2,1)...) custom-call(bf16[2,512,512]{2,1,0:T(8,128)(2,1)} %states.1, s32[4,8]{1,0:T(4,128)} %lists_in.1, s32[1,4]{1,0:T(1,128)} %bitcast.5, ...), custom_call_target="tpu_custom_call" | custom-call | flops 1048576 | tf_op jit(solution)/shard_map/pallas_call | solution.py:377
  4.3 1.6 %collective-permute-start.2 = (bf16[512,512]{1,0:T(8,128)(2,1)S(1)}, bf16[512,512]{1,0:T(8,128)(2,1)S(1)}, u32[]{:S(2)}, u32[]{:S(2)}) collective-permute-start(bf16[512,512]{1,0:T(8,128)(2,1)S(1)} %get-tuple-element.22.states), channel_id=1, source_target_pairs={{0,4},{4,0},{8,12},{12,8},{16,20},{20,16},{24,28},{28,24},{1,5},{5... | collective-permute-start | bytes 1572872 | tf_op jit(solution)/shard_map/ppermute | solution.py:404
  5.8 6.4 %collective-permute-done.4.rest_2_ = bf16[128,1536]{1,0:T(8,128)(2,1)S(1)} collective-permute-done((bf16[128,1536]{1,0:T(8,128)(2,1)}, bf16[128,1536]{1,0:T(8,128)(2,1)S(1)}, u32[]{:S(2)}, u32[]{:S(2)}) %collective-permute-start.4) | collective-permute-done | bytes 393248 | tf_op jit(solution)/shard_map/ppermute | solution.py:404
  12.3 1.7 %collective-permute-start.9 = (bf16[128,512]{1,0:T(8,128)(2,1)}, bf16[128,512]{1,0:T(8,128)(2,1)S(1)}, u32[]{:S(2)}, u32[]{:S(2)}) collective-permute-start(bf16[128,512]{1,0:T(8,128)(2,1)} %rest_0_.3), channel_id=1, source_target_pairs={{0,2},{1,3},{2,0},{3,1},{4,6},{5,7},{6,4},{7,5},{8,10},{9,11},{10,... | collective-permute-start | bytes 393224 | tf_op jit(solution)/shard_map/ppermute | solution.py:404
  14.0 3.6 %collective-permute-start.1 = (bf16[512,512]{1,0:T(8,128)(2,1)S(1)}, bf16[512,512]{1,0:T(8,128)(2,1)S(1)}, u32[]{:S(2)}, u32[]{:S(2)}) collective-permute-start(bf16[512,512]{1,0:T(8,128)(2,1)S(1)} %get-tuple-element.24.source.states), channel_id=1, source_target_pairs={{0,24},{4,12},{8,0},{12,20},{16,8},{20,28},{24,16},{28,4},{1,25},{... | collective-permute-start | bytes 1572872 | tf_op jit(solution)/shard_map/ppermute | solution.py:404
  17.6 0.8 %collective-permute-done.9.rest_2_ = bf16[128,512]{1,0:T(8,128)(2,1)S(1)} collective-permute-done((bf16[128,512]{1,0:T(8,128)(2,1)}, bf16[128,512]{1,0:T(8,128)(2,1)S(1)}, u32[]{:S(2)}, u32[]{:S(2)}) %collective-permute-start.9) | collective-permute-done | bytes 131104 | tf_op jit(solution)/shard_map/ppermute | solution.py:404
  18.4 1.7 %collective-permute-start.12 = (bf16[128,2048]{1,0:T(8,128)(2,1)}, bf16[128,2048]{1,0:T(8,128)(2,1)S(1)}, u32[]{:S(2)}, u32[]{:S(2)}) collective-permute-start(bf16[128,2048]{1,0:T(8,128)(2,1)} %rest_4_.3), channel_id=1, source_target_pairs={{0,2},{1,3},{2,0},{3,1},{4,6},{5,7},{6,4},{7,5},{8,10},{9,11},{10,... | collective-permute-start | bytes 1572872 | tf_op jit(solution)/shard_map/ppermute | solution.py:404
  20.2 1.0 %shard_map.92.rest_0_ = bf16[128,1536]{1,0:T(8,128)(2,1)S(1)} custom-call(bf16[128,1536]{1,0:T(8,128)(2,1)} %source.1), custom_call_target="tpu_custom_call" | custom-call | flops 1048576 | tf_op jit(solution)/shard_map/pallas_call | solution.py:377
  21.2 0.1 collective-permute-start.8
  21.3 1.6 %collective-permute-start = (bf16[16,128]{1,0:T(8,128)(2,1)S(1)}, bf16[16,128]{1,0:T(8,128)(2,1)S(1)}, u32[]{:S(2)}, u32[]{:S(2)}) collective-permute-start(bf16[16,128]{1,0:T(8,128)(2,1)S(1)} %get-tuple-element.23), channel_id=1, source_target_pairs={{0,4},{4,0},{8,12},{12,8},{16,20},{20,16},{24,28},{28,24},{1,5},{5... | collective-permute-start | bytes 12296 | tf_op jit(solution)/shard_map/ppermute | solution.py:404
  22.9 0.1 collective-permute-start.10
  23.0 1.4 %shard_map.93 = (bf16[512,512]{1,0:T(8,128)(2,1)S(1)}, bf16[512,512]{1,0:T(8,128)(2,1)S(1)}, bf16[4,512,128]{2,1,0:T(8,128)(2,1)S(1)}) custom-call(bf16[512,512]{1,0:T(8,128)(2,1)S(1)} %collective-permute-done.2.source, f32[1,512]{1,0:T(1,128)S(1)} %get-tuple-element.25.gain, bf16[128,1536]{1,0:T(8,128)(2,1)S(1)} %shard_map.92.rest_0_, ...), custom_call_target="tpu_custom_call" | custom-call | flops 2147483648 | bytes 4194304 | tf_op jit(solution)/shard_map/pallas_call | solution.py:377
  24.4 0.0 copy-start
  24.4 0.5 collective-permute-done.table
  24.9 1.6 %collective-permute-start.7 = (bf16[512,512]{1,0:T(8,128)(2,1)S(1)}, bf16[512,512]{1,0:T(8,128)(2,1)S(1)}, u32[]{:S(2)}, u32[]{:S(2)}) collective-permute-start(bf16[512,512]{1,0:T(8,128)(2,1)S(1)} %collective-permute-done.2.source), channel_id=1, source_target_pairs={{0,8},{4,28},{8,16},{12,4},{16,24},{20,12},{24,0},{28,20},{1,9},{5... | collective-permute-start | bytes 1572872 | tf_op jit(solution)/shard_map/ppermute | solution.py:404
  26.5 1.1 %shard_map.94 = (bf16[512,512]{1,0:T(8,128)(2,1)S(1)}, bf16[512,512]{1,0:T(8,128)(2,1)S(1)}, bf16[4,512,128]{2,1,0:T(8,128)(2,1)S(1)}) custom-call(bf16[512,512]{1,0:T(8,128)(2,1)S(1)} %get-tuple-element.24.source.states, f32[1,512]{1,0:T(1,128)S(1)} %get-tuple-element.25.gain, bf16[128,1536]{1,0:T(8,128)(2,1)S(1)} %shard_map.92.rest_0_, ...), custom_call_target="tpu_custom_call" | custom-call | flops 2147483648 | bytes 4194304 | tf_op jit(solution)/shard_map/pallas_call | solution.py:377
  27.7 0.1 collective-permute-start.11
  27.8 0.5 collective-permute-start.14
  28.3 1.7 %collective-permute-done.1.far = bf16[512,512]{1,0:T(8,128)(2,1)S(1)} collective-permute-done((bf16[512,512]{1,0:T(8,128)(2,1)S(1)}, bf16[512,512]{1,0:T(8,128)(2,1)S(1)}, u32[]{:S(2)}, u32[]{:S(2)}) %collective-permute-start.1) | collective-permute-done | bytes 524320 | tf_op jit(solution)/shard_map/ppermute | solution.py:404
  30.0 0.5 collective-permute-start.15
  30.5 2.5 %collective-permute-done.12.rest_6_ = bf16[128,2048]{1,0:T(8,128)(2,1)S(1)} collective-permute-done((bf16[128,2048]{1,0:T(8,128)(2,1)}, bf16[128,2048]{1,0:T(8,128)(2,1)S(1)}, u32[]{:S(2)}, u32[]{:S(2)}) %collective-permute-start.12) | collective-permute-done | bytes 524320 | tf_op jit(solution)/shard_map/ppermute | solution.py:404
  33.0 4.8 %shard_map.95 = bf16[512,512]{1,0:T(8,128)(2,1)S(1)} custom-call(bf16[16,128]{1,0:T(8,128)(2,1)S(1)} %collective-permute-done.table, bf16[512,512]{1,0:T(8,128)(2,1)S(1)} %collective-permute-done.1.far, bf16[512,512]{1,0:T(8,128)(2,1)S(1)} %get-tuple-element.26.queries, bf16[512,512]{1,0:T(8,128)(2,1)S(1)} %get-tuple-element.27.k_keep, ...), custom_call_target="tpu_custom_call" | custom-call | flops 4294967296 | bytes 4194304 | tf_op jit(solution)/shard_map/pallas_call | solution.py:377
  37.8 0.4 shard_map.96.queries
  38.2 3.1 %collective-permute-done.7.far = bf16[512,512]{1,0:T(8,128)(2,1)S(1)} collective-permute-done((bf16[512,512]{1,0:T(8,128)(2,1)S(1)}, bf16[512,512]{1,0:T(8,128)(2,1)S(1)}, u32[]{:S(2)}, u32[]{:S(2)}) %collective-permute-start.7) | collective-permute-done | bytes 524320 | tf_op jit(solution)/shard_map/ppermute | solution.py:404
  41.4 1.4 %collective-permute-start.6 = (bf16[512,512]{1,0:T(8,128)(2,1)S(1)}, bf16[512,512]{1,0:T(8,128)(2,1)S(1)}, u32[]{:S(2)}, u32[]{:S(2)}) collective-permute-start(bf16[512,512]{1,0:T(8,128)(2,1)S(1)} %shard_map.95), channel_id=1, source_target_pairs={{0,4},{4,0},{8,12},{12,8},{16,20},{20,16},{24,28},{28,24},{1,5},{5... | collective-permute-start | bytes 1572872 | tf_op jit(solution)/shard_map/ppermute | solution.py:404
  42.7 4.9 %shard_map.97.attended = bf16[512,512]{1,0:T(8,128)(2,1)S(1)} custom-call(bf16[16,128]{1,0:T(8,128)(2,1)S(1)} %get-tuple-element.32.table, bf16[512,512]{1,0:T(8,128)(2,1)S(1)} %collective-permute-done.7.far, bf16[512,512]{1,0:T(8,128)(2,1)S(1)} %shard_map.96.queries, bf16[512,512]{1,0:T(8,128)(2,1)S(1)} %get-tuple-element.27.k_keep, ...), custom_call_target="tpu_custom_call" | custom-call | flops 4294967296 | bytes 4194304 | tf_op jit(solution)/shard_map/pallas_call | solution.py:377
  47.6 0.1 collective-permute-start.16
  47.8 3.0 %shard_map.98 = (bf16[512,2048]{1,0:T(8,128)(2,1)S(1)}, f32[2,512,256]{2,1,0:T(8,128)S(1)}) custom-call(bf16[512,512]{1,0:T(8,128)(2,1)S(1)} %get-tuple-element.24.source.states, bf16[512,512]{1,0:T(8,128)(2,1)S(1)} %shard_map.97.attended, f32[1,512]{1,0:T(1,128)S(1)} %get-tuple-element.31.gain, bf16[128,512]{1,0:T(8,128)(2,1)S(1)} %copy-done.2, ...), custom_call_target="tpu_custom_call" | custom-call | flops 3221225472 | bytes 4194304 | tf_op jit(solution)/shard_map/pallas_call | solution.py:377
  50.7 4.1 %collective-permute-done.6.attended = bf16[512,512]{1,0:T(8,128)(2,1)S(1)} collective-permute-done((bf16[512,512]{1,0:T(8,128)(2,1)S(1)}, bf16[512,512]{1,0:T(8,128)(2,1)S(1)}, u32[]{:S(2)}, u32[]{:S(2)}) %collective-permute-start.6) | collective-permute-done | bytes 524320 | tf_op jit(solution)/shard_map/ppermute | solution.py:404
  54.8 3.3 %shard_map.99 = (bf16[512,2048]{1,0:T(8,128)(2,1)S(1)}, f32[2,512,256]{2,1,0:T(8,128)S(1)}, f32[2,512,256]{2,1,0:T(8,128)S(1)}) custom-call(bf16[512,512]{1,0:T(8,128)(2,1)S(1)} %get-tuple-element.22.states, bf16[512,512]{1,0:T(8,128)(2,1)S(1)} %collective-permute-done.6.attended, f32[1,512]{1,0:T(1,128)S(1)} %get-tuple-element.31.gain, ...), custom_call_target="tpu_custom_call" | custom-call | flops 5368709120 | bytes 4194304 | tf_op jit(solution)/shard_map/pallas_call | solution.py:377
  58.1 1.8 %shard_map.100 = bf16[2,512,512]{2,1,0:T(8,128)(2,1)} custom-call(f32[2,512,256]{2,1,0:T(8,128)S(1)} %get-tuple-element.36.total_k, f32[2,512,256]{2,1,0:T(8,128)S(1)} %get-tuple-element.37.total_g, bf16[512,2048]{1,0:T(8,128)(2,1)S(1)} %get-tuple-element.34.hidden_k, bf16[512,2048]{1,0:T(8,128)(2,1)S(1)} %get-tuple-element.38.hidden_g, ...), custom_call_target="tpu_custom_call" | custom-call | flops 2147483648 | bytes 4194304 | tf_op jit(solution)/shard_map/pallas_call | solution.py:377
  (18 shorter events, 0.0 us)
Async XLA Ops:
  0.0 12.3 %collective-permute-start.4 = (bf16[128,1536]{1,0:T(8,128)(2,1)}, bf16[128,1536]{1,0:T(8,128)(2,1)S(1)}, u32[]{:S(2)}, u32[]{:S(2)}) collective-permute-start(bf16[128,1536]{1,0:T(8,128)(2,1)} %source.1), channel_id=1, source_target_pairs={{0,2},{1,3},{2,0},{3,1},{4,6},{5,7},{6,4},{7,5},{8,10},{9,11},{10,... | collective-permute-start | bytes 1179656 | tf_op jit(solution)/shard_map/ppermute | solution.py:404
  4.3 17.0 %collective-permute-start.2 = (bf16[512,512]{1,0:T(8,128)(2,1)S(1)}, bf16[512,512]{1,0:T(8,128)(2,1)S(1)}, u32[]{:S(2)}, u32[]{:S(2)}) collective-permute-start(bf16[512,512]{1,0:T(8,128)(2,1)S(1)} %get-tuple-element.22.states), channel_id=1, source_target_pairs={{0,4},{4,0},{8,12},{12,8},{16,20},{20,16},{24,28},{28,24},{1,5},{5... | collective-permute-start | bytes 1572872 | tf_op jit(solution)/shard_map/ppermute | solution.py:404
  5.8 15.3 %collective-permute-start.3 = (bf16[128,1536]{1,0:T(8,128)(2,1)}, bf16[128,1536]{1,0:T(8,128)(2,1)S(1)}, u32[]{:S(2)}, u32[]{:S(2)}) collective-permute-start(bf16[128,1536]{1,0:T(8,128)(2,1)} %source.1), channel_id=1, source_target_pairs={{0,1},{1,0},{2,3},{3,2},{4,5},{5,4},{6,7},{7,6},{8,9},{9,8},{10,11... | collective-permute-start | bytes 1179656 | tf_op jit(solution)/shard_map/ppermute | solution.py:404
  12.3 10.6 %collective-permute-start.5 = (bf16[128,1536]{1,0:T(8,128)(2,1)S(1)}, bf16[128,1536]{1,0:T(8,128)(2,1)S(1)}, u32[]{:S(2)}, u32[]{:S(2)}) collective-permute-start(bf16[128,1536]{1,0:T(8,128)(2,1)S(1)} %collective-permute-done.4.rest_2_), channel_id=1, source_target_pairs={{0,1},{1,0},{2,3},{3,2},{4,5},{5,4},{6,7},{7,6},{8,9},{9,8},{10,11... | collective-permute-start | bytes 1179656 | tf_op jit(solution)/shard_map/ppermute | solution.py:404
  12.3 6.1 %collective-permute-start.9 = (bf16[128,512]{1,0:T(8,128)(2,1)}, bf16[128,512]{1,0:T(8,128)(2,1)S(1)}, u32[]{:S(2)}, u32[]{:S(2)}) collective-permute-start(bf16[128,512]{1,0:T(8,128)(2,1)} %rest_0_.3), channel_id=1, source_target_pairs={{0,2},{1,3},{2,0},{3,1},{4,6},{5,7},{6,4},{7,5},{8,10},{9,11},{10,... | collective-permute-start | bytes 393224 | tf_op jit(solution)/shard_map/ppermute | solution.py:404
  14.0 16.0 %collective-permute-start.1 = (bf16[512,512]{1,0:T(8,128)(2,1)S(1)}, bf16[512,512]{1,0:T(8,128)(2,1)S(1)}, u32[]{:S(2)}, u32[]{:S(2)}) collective-permute-start(bf16[512,512]{1,0:T(8,128)(2,1)S(1)} %get-tuple-element.24.source.states), channel_id=1, source_target_pairs={{0,24},{4,12},{8,0},{12,20},{16,8},{20,28},{24,16},{28,4},{1,25},{... | collective-permute-start | bytes 1572872 | tf_op jit(solution)/shard_map/ppermute | solution.py:404
  18.4 14.6 %collective-permute-start.12 = (bf16[128,2048]{1,0:T(8,128)(2,1)}, bf16[128,2048]{1,0:T(8,128)(2,1)S(1)}, u32[]{:S(2)}, u32[]{:S(2)}) collective-permute-start(bf16[128,2048]{1,0:T(8,128)(2,1)} %rest_4_.3), channel_id=1, source_target_pairs={{0,2},{1,3},{2,0},{3,1},{4,6},{5,7},{6,4},{7,5},{8,10},{9,11},{10,... | collective-permute-start | bytes 1572872 | tf_op jit(solution)/shard_map/ppermute | solution.py:404
  21.2 6.5 %collective-permute-start.8 = (bf16[128,512]{1,0:T(8,128)(2,1)}, bf16[128,512]{1,0:T(8,128)(2,1)S(1)}, u32[]{:S(2)}, u32[]{:S(2)}) collective-permute-start(bf16[128,512]{1,0:T(8,128)(2,1)} %rest_0_.3), channel_id=1, source_target_pairs={{0,1},{1,0},{2,3},{3,2},{4,5},{5,4},{6,7},{7,6},{8,9},{9,8},{10,11... | collective-permute-start | bytes 393224 | tf_op jit(solution)/shard_map/ppermute | solution.py:404
  21.3 3.7 %collective-permute-start = (bf16[16,128]{1,0:T(8,128)(2,1)S(1)}, bf16[16,128]{1,0:T(8,128)(2,1)S(1)}, u32[]{:S(2)}, u32[]{:S(2)}) collective-permute-start(bf16[16,128]{1,0:T(8,128)(2,1)S(1)} %get-tuple-element.23), channel_id=1, source_target_pairs={{0,4},{4,0},{8,12},{12,8},{16,20},{20,16},{24,28},{28,24},{1,5},{5... | collective-permute-start | bytes 12296 | tf_op jit(solution)/shard_map/ppermute | solution.py:404
  22.9 4.9 %collective-permute-start.10 = (bf16[128,512]{1,0:T(8,128)(2,1)S(1)}, bf16[128,512]{1,0:T(8,128)(2,1)S(1)}, u32[]{:S(2)}, u32[]{:S(2)}) collective-permute-start(bf16[128,512]{1,0:T(8,128)(2,1)S(1)} %collective-permute-done.9.rest_2_), channel_id=1, source_target_pairs={{0,1},{1,0},{2,3},{3,2},{4,5},{5,4},{6,7},{7,6},{8,9},{9,8},{10,11... | collective-permute-start | bytes 393224 | tf_op jit(solution)/shard_map/ppermute | solution.py:404
  24.4 3.3 %copy-start = (bf16[128,2048]{1,0:T(8,128)(2,1)S(1)}, bf16[128,2048]{1,0:T(8,128)(2,1)}, u32[]{:S(2)}) copy-start(bf16[128,2048]{1,0:T(8,128)(2,1)} %rest_4_.3) | copy-start | bytes 1572868
  24.4 3.4 %copy-start.1 = (bf16[512,512]{1,0:T(8,128)(2,1)S(1)}, bf16[512,512]{1,0:T(8,128)(2,1)}, u32[]{:S(2)}) copy-start(bf16[512,512]{1,0:T(8,128)(2,1)} %rest_8_.3) | copy-start | bytes 1572868
  24.9 16.4 %collective-permute-start.7 = (bf16[512,512]{1,0:T(8,128)(2,1)S(1)}, bf16[512,512]{1,0:T(8,128)(2,1)S(1)}, u32[]{:S(2)}, u32[]{:S(2)}) collective-permute-start(bf16[512,512]{1,0:T(8,128)(2,1)S(1)} %collective-permute-done.2.source), channel_id=1, source_target_pairs={{0,8},{4,28},{8,16},{12,4},{16,24},{20,12},{24,0},{28,20},{1,9},{5... | collective-permute-start | bytes 1572872 | tf_op jit(solution)/shard_map/ppermute | solution.py:404
  27.7 20.0 %collective-permute-start.11 = (bf16[128,2048]{1,0:T(8,128)(2,1)S(1)}, bf16[128,2048]{1,0:T(8,128)(2,1)S(1)}, u32[]{:S(2)}, u32[]{:S(2)}) collective-permute-start(bf16[128,2048]{1,0:T(8,128)(2,1)S(1)} %copy-done), channel_id=1, source_target_pairs={{0,1},{1,0},{2,3},{3,2},{4,5},{5,4},{6,7},{7,6},{8,9},{9,8},{10,11... | collective-permute-start | bytes 1572872 | tf_op jit(solution)/shard_map/ppermute | solution.py:404
  27.8 20.0 %collective-permute-start.14 = (bf16[512,512]{1,0:T(8,128)(2,1)S(1)}, bf16[512,512]{1,0:T(8,128)(2,1)S(1)}, u32[]{:S(2)}, u32[]{:S(2)}) collective-permute-start(bf16[512,512]{1,0:T(8,128)(2,1)S(1)} %copy-done.1), channel_id=1, source_target_pairs={{0,1},{1,0},{2,3},{3,2},{4,5},{5,4},{6,7},{7,6},{8,9},{9,8},{10,11... | collective-permute-start | bytes 1572872 | tf_op jit(solution)/shard_map/ppermute | solution.py:404
  30.0 17.6 %collective-permute-start.15 = (bf16[512,512]{1,0:T(8,128)(2,1)S(1)}, bf16[512,512]{1,0:T(8,128)(2,1)S(1)}, u32[]{:S(2)}, u32[]{:S(2)}) collective-permute-start(bf16[512,512]{1,0:T(8,128)(2,1)S(1)} %copy-done.1), channel_id=1, source_target_pairs={{0,2},{1,3},{2,0},{3,1},{4,6},{5,7},{6,4},{7,5},{8,10},{9,11},{10,... | collective-permute-start | bytes 1572872 | tf_op jit(solution)/shard_map/ppermute | solution.py:404
  33.0 14.7 %collective-permute-start.13 = (bf16[128,2048]{1,0:T(8,128)(2,1)S(1)}, bf16[128,2048]{1,0:T(8,128)(2,1)S(1)}, u32[]{:S(2)}, u32[]{:S(2)}) collective-permute-start(bf16[128,2048]{1,0:T(8,128)(2,1)S(1)} %collective-permute-done.12.rest_6_), channel_id=1, source_target_pairs={{0,1},{1,0},{2,3},{3,2},{4,5},{5,4},{6,7},{7,6},{8,9},{9,8},{10,11... | collective-permute-start | bytes 1572872 | tf_op jit(solution)/shard_map/ppermute | solution.py:404
  41.4 13.5 %collective-permute-start.6 = (bf16[512,512]{1,0:T(8,128)(2,1)S(1)}, bf16[512,512]{1,0:T(8,128)(2,1)S(1)}, u32[]{:S(2)}, u32[]{:S(2)}) collective-permute-start(bf16[512,512]{1,0:T(8,128)(2,1)S(1)} %shard_map.95), channel_id=1, source_target_pairs={{0,4},{4,0},{8,12},{12,8},{16,20},{20,16},{24,28},{28,24},{1,5},{5... | collective-permute-start | bytes 1572872 | tf_op jit(solution)/shard_map/ppermute | solution.py:404
  42.7 5.0 %copy-start.2 = (bf16[128,512]{1,0:T(8,128)(2,1)S(1)}, bf16[128,512]{1,0:T(8,128)(2,1)}, u32[]{:S(2)}) copy-start(bf16[128,512]{1,0:T(8,128)(2,1)} %rest_0_.3) | copy-start | bytes 393220
  47.6 10.5 %collective-permute-start.16 = (bf16[512,512]{1,0:T(8,128)(2,1)S(1)}, bf16[512,512]{1,0:T(8,128)(2,1)S(1)}, u32[]{:S(2)}, u32[]{:S(2)}) collective-permute-start(bf16[512,512]{1,0:T(8,128)(2,1)S(1)} %collective-permute-done.15.rest_10_.rest_0_), channel_id=1, source_target_pairs={{0,1},{1,0},{2,3},{3,2},{4,5},{5,4},{6,7},{7,6},{8,9},{9,8},{10,11... | collective-permute-start | bytes 1572872 | tf_op jit(solution)/shard_map/ppermute | solution.py:404
